TPU v7x, 128 devices: a whole 4x4x4 slice. The times are simulated.
128 devices in a mesh: lon: 16 (over x, y_hi, core), lat: 8 (over y_lo, z).
Axes of the slice: x: 4, y: 4 (y_hi: 2, y_lo: 2; y = y_hi * 2 + y_lo), z: 4, core: 2. Of those that a mesh axis runs over, the one named last changes fastest.
Arguments:
- normed: bfloat16 [8, 192, 384, 192], P(None, 'lat', 'lon'), may hold values from -6 to 6
- cotangent: bfloat16 [8, 192, 384, 192], P(None, 'lat', 'lon'), may hold values from -6 to 6
- weight_qkv: bfloat16 [192, 576], replicated, may hold values from -0.4375 to 0.4375
- weight_proj: bfloat16 [192, 192], replicated, may hold values from -0.4375 to 0.4375
- bias_table: bfloat16 [128, 6, 20736], P('lat'), may hold values from -6 to 390
Outputs:
- input_grad: bfloat16 [8, 192, 384, 192], P(None, 'lat', 'lon')
- qkv_grad: float32 [192, 576], replicated
- proj_grad: float32 [192, 192], replicated
- bias_grad: float32 [128, 6, 20736], P('lat')
All inputs are finite; a program needn't handle non-finite values.
Results may differ from a plain program's by a relative error of at most 0.019.
Values may be sent and summed in bfloat16 or wider, within the bound.
A program may use at most 192 MiB of HBM per device.

v0:
```python
import jax
import jax.numpy as jnp
from jax import lax
from jax.sharding import PartitionSpec as P

HEADS = 6
WIN_Z = 2
WIN_LAT = 6
WIN_LON = 12
WTOK = 144


def passed_along(block, axis, distance):
    devices = range(lax.axis_size(axis))
    route = [(i - distance, i) for i in devices if i - distance in devices]
    return lax.ppermute(block, axis, route)


def from_behind(block, axis, distance):
    devices = range(lax.axis_size(axis))
    route = [((i - distance) % len(devices), i) for i in devices]
    return lax.ppermute(block, axis, route)


def sent_to_all(x, axis):
    count = lax.axis_size(axis)
    return lax.all_to_all(jnp.broadcast_to(x[None], (count, *x.shape)), axis, 0, 0, tiled=True)


def of_everyone(x, axis):
    everything = sent_to_all(x, axis)
    return jnp.sum(everything.astype(jnp.float32), axis=0)


def window_split(grid_field):
    levels, height, breadth = grid_field.shape[:3]
    trailing_dims = grid_field.shape[3:]
    shaped = grid_field.reshape(
        (levels // WIN_Z, WIN_Z, height // WIN_LAT, WIN_LAT, breadth // WIN_LON, WIN_LON)
        + trailing_dims
    )
    axes_order = (0, 2, 4, 1, 3, 5) + tuple(range(6, 6 + len(trailing_dims)))
    return shaped.transpose(axes_order).reshape((-1, WTOK) + trailing_dims)


def window_merge(windowed, levels, height, breadth):
    channels = windowed.shape[-1]
    shaped = windowed.reshape(
        levels // WIN_Z, height // WIN_LAT, breadth // WIN_LON, WIN_Z, WIN_LAT, WIN_LON, channels
    )
    return shaped.transpose(0, 3, 1, 4, 2, 5, 6).reshape(levels, height, breadth, channels)


def window_backward(
    block_in, block_cot, block_region, block_live, block_types, bias_rows, weight_qkv, weight_proj
):
    windows = block_in.shape[0]
    channels = block_in.shape[2]
    head_dim = channels // HEADS
    softmax_scale = head_dim ** (-0.5)
    f32 = jnp.float32
    projected = jnp.einsum("bnc,cf->bnf", block_in, weight_qkv, preferred_element_type=f32).astype(
        jnp.bfloat16
    )
    projected = projected.reshape(windows, WTOK, 3, HEADS, head_dim)
    queries = projected[:, :, 0]
    key_rows = projected[:, :, 1]
    values = projected[:, :, 2]
    bias_add = jnp.dot(
        block_types.astype(jnp.bfloat16), bias_rows, preferred_element_type=f32
    ).reshape(windows, HEADS, WTOK, WTOK)
    scores = (
        jnp.einsum("bqhd,bkhd->bhqk", queries, key_rows, preferred_element_type=f32) * softmax_scale
        + bias_add
    )
    allowed = (block_region[:, :, None] == block_region[:, None, :]) & (
        block_live[:, :, None] == block_live[:, None, :]
    )
    allowed = allowed[:, None]
    peak_score = jnp.max(jnp.where(allowed, scores, -1e30), axis=-1, keepdims=True)
    exp_terms = jnp.where(allowed, jnp.exp(scores - peak_score), 0.0)
    attn_probs = exp_terms / jnp.sum(exp_terms, axis=-1, keepdims=True)
    probs_b = attn_probs.astype(jnp.bfloat16)
    mixed = jnp.einsum("bhqk,bkhd->bqhd", probs_b, values, preferred_element_type=f32).astype(
        jnp.bfloat16
    )
    mixed = mixed.reshape(windows, WTOK, channels)
    grad_proj = jnp.einsum("bnc,bnf->cf", mixed, block_cot, preferred_element_type=f32)
    mixed_grad = jnp.einsum(
        "bnf,cf->bnc", block_cot, weight_proj, preferred_element_type=f32
    ).astype(jnp.bfloat16)
    mixed_grad = mixed_grad.reshape(windows, WTOK, HEADS, head_dim)
    prob_grad = jnp.einsum("bqhd,bkhd->bhqk", mixed_grad, values, preferred_element_type=f32)
    row_delta = jnp.sum(attn_probs * prob_grad, axis=-1, keepdims=True)
    score_grad = attn_probs * (prob_grad - row_delta)
    grad_bias = jnp.dot(block_types.T, score_grad.reshape(windows, -1), preferred_element_type=f32)
    score_grad_b = score_grad.astype(jnp.bfloat16)
    query_grad = (
        jnp.einsum("bhqk,bkhd->bqhd", score_grad_b, key_rows, preferred_element_type=f32)
        * softmax_scale
    ).astype(jnp.bfloat16)
    key_grad = (
        jnp.einsum("bhqk,bqhd->bkhd", score_grad_b, queries, preferred_element_type=f32)
        * softmax_scale
    ).astype(jnp.bfloat16)
    value_grad = jnp.einsum(
        "bhqk,bqhd->bkhd", probs_b, mixed_grad, preferred_element_type=f32
    ).astype(jnp.bfloat16)
    cols_grad = jnp.stack([query_grad, key_grad, value_grad], axis=2).reshape(
        windows, WTOK, 3 * channels
    )
    grad_qkv = jnp.einsum("bnc,bnf->cf", block_in, cols_grad, preferred_element_type=f32)
    grad_in = jnp.einsum("bnf,cf->bnc", cols_grad, weight_qkv, preferred_element_type=f32).astype(
        jnp.bfloat16
    )
    return (grad_in, grad_qkv, grad_proj, grad_bias)


def local(normed, cotangent, weight_qkv, weight_proj, bias_table):
    levels, height, breadth, channels = normed.shape
    level_shift = WIN_Z // 2
    lat_shift = WIN_LAT // 2
    lon_shift = WIN_LON // 2
    normed = jnp.roll(normed, -level_shift, axis=0)
    cotangent = jnp.roll(cotangent, -level_shift, axis=0)
    upward = passed_along((normed[:, :lat_shift], cotangent[:, :lat_shift]), "lat", -1)
    tall_in = jnp.concatenate([normed[:, lat_shift:], upward[0]], axis=1)
    tall_cot = jnp.concatenate([cotangent[:, lat_shift:], upward[1]], axis=1)
    across = from_behind((tall_in[:, :, :lon_shift], tall_cot[:, :, :lon_shift]), "lon", -1)
    frame_in = jnp.concatenate([tall_in[:, :, lon_shift:], across[0]], axis=2)
    frame_cot = jnp.concatenate([tall_cot[:, :, lon_shift:], across[1]], axis=2)
    is_last = lax.axis_index("lat") == lax.axis_size("lat") - 1
    row_index = jnp.arange(height, dtype=jnp.int32)
    live_rows = jnp.logical_not(is_last & (row_index >= height - lat_shift))
    live_field = jnp.broadcast_to(live_rows[None, :, None], (levels, height, breadth))
    level_index = jnp.arange(levels, dtype=jnp.int32)
    wrapped_levels = (level_index >= levels - level_shift).astype(jnp.int32)
    wrapped_field = jnp.broadcast_to(wrapped_levels[:, None, None], (levels, height, breadth))
    level_windows = levels // WIN_Z
    lat_windows = height // WIN_LAT
    lon_windows = breadth // WIN_LON
    types_local = level_windows * lat_windows
    level_part = jnp.arange(level_windows, dtype=jnp.int32)[:, None, None]
    lat_part = jnp.arange(lat_windows, dtype=jnp.int32)[None, :, None]
    kinds = jnp.broadcast_to(
        lat_part * level_windows + level_part, (level_windows, lat_windows, lon_windows)
    )
    onehot = (
        kinds.reshape(-1)[:, None] == jnp.arange(types_local, dtype=jnp.int32)[None, :]
    ).astype(jnp.float32)
    bias_rows = bias_table.reshape(types_local, -1)
    framed_in = window_split(frame_in)
    window_total = framed_in.shape[0]
    block_size = max((divisor for divisor in range(1, 17) if window_total % divisor == 0))
    blocks = window_total // block_size

    def regroup(array):
        return array.reshape((blocks, block_size) + array.shape[1:])

    def step_block(totals, pieces):
        grad_in, grad_qkv, grad_proj, grad_bias = window_backward(
            pieces[0],
            pieces[1],
            pieces[2],
            pieces[3],
            pieces[4],
            bias_rows,
            weight_qkv,
            weight_proj,
        )
        return ((totals[0] + grad_qkv, totals[1] + grad_proj, totals[2] + grad_bias), grad_in)

    start = (
        jnp.zeros((channels, 3 * channels), jnp.float32),
        jnp.zeros((channels, channels), jnp.float32),
        jnp.zeros((types_local, HEADS * WTOK * WTOK), jnp.float32),
    )
    pieces = (
        regroup(framed_in),
        regroup(window_split(frame_cot)),
        regroup(window_split(wrapped_field)),
        regroup(window_split(live_field)),
        regroup(onehot),
    )
    totals, grads = lax.scan(step_block, start, pieces)
    framed_grad = window_merge(grads.reshape(window_total, WTOK, channels), levels, height, breadth)
    sideways = from_behind(framed_grad[:, :, breadth - lon_shift :], "lon", 1)
    tall_grad = jnp.concatenate([sideways, framed_grad[:, :, : breadth - lon_shift]], axis=2)
    returned = passed_along(tall_grad[:, height - lat_shift :], "lat", 1)
    shifted_grad = jnp.concatenate([returned, tall_grad[:, : height - lat_shift]], axis=1)
    input_grad = jnp.roll(shifted_grad, level_shift, axis=0)
    lat_qkv, lat_proj = (
        of_everyone(totals[0].astype(jnp.bfloat16), "lat").astype(jnp.float32),
        of_everyone(totals[1].astype(jnp.bfloat16), "lat").astype(jnp.float32),
    )
    bias_grad, qkv_grad, proj_grad = (
        lax.psum(totals[2].astype(jnp.bfloat16), "lon").astype(jnp.float32),
        lax.psum(lat_qkv.astype(jnp.bfloat16), "lon").astype(jnp.float32),
        lax.psum(lat_proj.astype(jnp.bfloat16), "lon").astype(jnp.float32),
    )
    return (input_grad, qkv_grad, proj_grad, bias_grad.reshape(types_local, HEADS, WTOK * WTOK))


def solution(mesh):
    in_specs = (
        P(None, "lat", "lon", None),
        P(None, "lat", "lon", None),
        P(),
        P(),
        P("lat", None, None),
    )
    out_specs = (P(None, "lat", "lon", None), P(), P(), P("lat", None, None))
    return jax.shard_map(local, mesh=mesh, in_specs=in_specs, out_specs=out_specs, check_vma=False)
```

profile of v0, /device:TPU:1, one launch (start us, length us, event | category | flops | bytes accessed | tf_op | source)
XLA Modules:
  0.0 658.5 jit_solution(13714143662319422248)
XLA Ops:
  62.0 357.1 %while.17 = (s32[]{:T(128)}, f32[192,576]{1,0:T(8,128)}, f32[192,192]{1,0:T(8,128)}, f32[16,124416]{1,0:T(8,128)}, bf16[2,16,144,192]{3,1,0,2:T(8,128)(2,1)}, /*...) while((s32[]{:T(128)}, f32[192,576]{1,0:T(8,128)}, ...), condition=%wide.region_4.5_spmd.clone, body=%wide.region_0.4_spmd.clone.sunk | while | flops 2806995456 | bytes 370116224 | solution.py:185
  69.2 15.1 %dot_general.59 = bf16[6,144,144,16]{2,1,0,3:T(8,128)(2,1)} reshape(bf16[124416,16]{0,1:T(8,128)(2,1)} %bitcast.202) | data formatting | bytes 7962624 | tf_op jit(solution)/shard_map/while/body/eval_jaxpr/dot_general | solution.py:69
  84.4 12.4 %fusion.132 = f32[16,6,144,144]{3,0,2,1:T(8,128)} fusion(bf16[6,144,144,16]{2,1,0,3:T(8,128)(2,1)} %dot_general.59, bf16[2,16,16]{2,1,0:T(8,128)(2,1)S(1)} %get-tuple-element.347, s32[]{:T(128)} %get-tuple-element.323), kind=kOutput, calls=%fused_computation.8.clone.1 | convolution fusion | flops 63700992 | bytes 11948036 | tf_op jit(solution)/shard_map/while/body/eval_jaxpr/dot_general | solution.py:69
  96.7 17.4 %copy.178 = f32[16,6,144,144]{2,3,1,0:T(8,128)} copy(f32[16,6,144,144]{3,0,2,1:T(8,128)} %fusion.132) | data formatting | bytes 15925248 | tf_op jit(solution)/shard_map/while/body/eval_jaxpr/dot_general | solution.py:69
  114.2 13.1 %multiply_add_fusion.2 = f32[16,6,144,144]{2,3,1,0:T(8,128)} fusion(f32[16,6,144,144]{2,3,1,0:T(8,128)} %copy.178, bf16[16,144,3,6,32]{1,4,3,2,0:T(8,128)(2,1)} %bitcast.194), kind=kOutput, calls=%fused_computation.7.clone.1 | convolution fusion | flops 131383296 | bytes 25264128 | tf_op jit(solution)/shard_map/while/body/eval_jaxpr/bqhd,bkhd->bhqk/dot_general | solution.py:73
  128.3 16.0 %fusion.133 = (f32[16,6,144]{2,1,0:T(8,128)S(1)}, f32[16,6,144,144]{2,3,1,0:T(8,128)}) fusion(f32[16,6,144,144]{2,3,1,0:T(8,128)} %multiply_add_fusion.2, pred[16,144,144]{1,2,0:T(8,128)(4,1)S(1)} %compare_and_fusion.2), kind=kOutput, calls=%fused_computation.97.clone.1 | output fusion | flops 7962767 | bytes 16312320 | tf_op jit(solution)/shard_map/while/body/eval_jaxpr/sub | solution.py:81
  145.6 12.8 %multiply_reduce_fusion.2 = (f32[16,6,144]{2,1,0:T(8,128)S(1)}, f32[16,6,144,144]{2,3,1,0:T(8,128)}) fusion(f32[16,6,144,144]{2,3,1,0:T(8,128)} %get-tuple-element.304, f32[16,6,144]{2,1,0:T(8,128)S(1)} %get-tuple-element.305, bf16[16,144,6,32]{1,3,2,0:T(8,128)(2,1)S(1)} %bitcast.203, bf16[16,144,3,6,32]{1,4,3,2,0:T(8,128)(2,1)} %bitcast.195), kind=kOutput, calls=%fused_computation.3.clone.1 | convolution fusion | flops 133360128 | bytes 24686592 | tf_op jit(solution)/shard_map/while/body/eval_jaxpr/bqhd,bkhd->bhqk/dot_general | solution.py:93
  160.6 9.2 %subtract_multiply_fusion.2 = bf16[16,6,144,144]{2,3,1,0:T(8,128)(2,1)} fusion(f32[16,6,144,144]{2,3,1,0:T(8,128)} %get-tuple-element.306, f32[16,6,144]{2,1,0:T(8,128)S(1)} %get-tuple-element.307, f32[16,6,144,144]{2,3,1,0:T(8,128)S(1)} %bitcast.191, f32[16,6,144]{2,1,0:T(8,128)S(1)} %get-tuple-element.305), kind=kLoop, calls=%fused_computation.2.clone.1 | loop fusion | flops 7962624 | bytes 20017152 | tf_op jit(solution)/shard_map/while/body/eval_jaxpr/mul | solution.py:95
  169.8 11.2 %copy.181 = bf16[16,6,144,144]{3,2,1,0:T(8,128)(2,1)} copy(bf16[16,6,144,144]{2,3,1,0:T(8,128)(2,1)} %subtract_multiply_fusion.2) | data formatting | bytes 7962624 | tf_op jit(solution)/shard_map/while/body/eval_jaxpr/mul | solution.py:95
  181.0 18.3 %reshape.134 = bf16[16,124416]{1,0:T(8,128)(2,1)} reshape(bf16[16,6,144,144]{3,2,1,0:T(8,128)(2,1)} %copy.181) | data formatting | bytes 7962624 | tf_op jit(solution)/shard_map/while/body/eval_jaxpr/reshape | solution.py:96
  199.3 6.7 %convolution_add_fusion.2 = f32[16,124416]{1,0:T(8,128)} fusion(bf16[16,124416]{1,0:T(8,128)(2,1)} %reshape.134, f32[16,124416]{1,0:T(8,128)} %get-tuple-element.326, pred[]{:T(512)S(6)} %compare.3, bf16[2,16,16]{2,1,0:T(8,128)(2,1)S(1)} %get-tuple-element.347, s32[]{:T(128)} %get-tuple-element.323), kind=kOutput, calls=%fused_computation.1.clone.1 | convolution fusion | flops 67682304 | bytes 19910660 | tf_op jit(solution)/shard_map/while/body/eval_jaxpr/dot_general | solution.py:96
  212.4 7.4 %fusion.134 = bf16[16,144,1,6,32]{1,4,3,0,2:T(8,128)(2,1)S(1)} fusion(bf16[16,144,6,32]{1,3,2,0:T(8,128)(2,1)S(1)} %bitcast.204, f32[16,6,144,144]{2,3,1,0:T(8,128)} %get-tuple-element.304, f32[16,6,144]{2,1,0:T(8,128)S(1)} %get-tuple-element.305), kind=kOutput, calls=%fused_computation.33.clone.1 | convolution fusion | flops 131825664 | bytes 9787392 | tf_op jit(solution)/shard_map/while/body/eval_jaxpr/bhqk,bqhd->bkhd/dot_general | solution.py:106
  242.3 15.1 %dot_general.59 = bf16[6,144,144,16]{2,1,0,3:T(8,128)(2,1)} reshape(bf16[124416,16]{0,1:T(8,128)(2,1)} %bitcast.202) | data formatting | bytes 7962624 | tf_op jit(solution)/shard_map/while/body/eval_jaxpr/dot_general | solution.py:69
  257.4 12.4 %fusion.132 = f32[16,6,144,144]{3,0,2,1:T(8,128)} fusion(bf16[6,144,144,16]{2,1,0,3:T(8,128)(2,1)} %dot_general.59, bf16[2,16,16]{2,1,0:T(8,128)(2,1)S(1)} %get-tuple-element.347, s32[]{:T(128)} %get-tuple-element.323), kind=kOutput, calls=%fused_computation.8.clone.1 | convolution fusion | flops 63700992 | bytes 11948036 | tf_op jit(solution)/shard_map/while/body/eval_jaxpr/dot_general | solution.py:69
  269.8 17.2 %copy.178 = f32[16,6,144,144]{2,3,1,0:T(8,128)} copy(f32[16,6,144,144]{3,0,2,1:T(8,128)} %fusion.132) | data formatting | bytes 15925248 | tf_op jit(solution)/shard_map/while/body/eval_jaxpr/dot_general | solution.py:69
  287.0 13.1 %multiply_add_fusion.2 = f32[16,6,144,144]{2,3,1,0:T(8,128)} fusion(f32[16,6,144,144]{2,3,1,0:T(8,128)} %copy.178, bf16[16,144,3,6,32]{1,4,3,2,0:T(8,128)(2,1)} %bitcast.194), kind=kOutput, calls=%fused_computation.7.clone.1 | convolution fusion | flops 131383296 | bytes 25264128 | tf_op jit(solution)/shard_map/while/body/eval_jaxpr/bqhd,bkhd->bhqk/dot_general | solution.py:73
  301.1 16.0 %fusion.133 = (f32[16,6,144]{2,1,0:T(8,128)S(1)}, f32[16,6,144,144]{2,3,1,0:T(8,128)}) fusion(f32[16,6,144,144]{2,3,1,0:T(8,128)} %multiply_add_fusion.2, pred[16,144,144]{1,2,0:T(8,128)(4,1)S(1)} %compare_and_fusion.2), kind=kOutput, calls=%fused_computation.97.clone.1 | output fusion | flops 7962767 | bytes 16312320 | tf_op jit(solution)/shard_map/while/body/eval_jaxpr/sub | solution.py:81
  318.4 12.8 %multiply_reduce_fusion.2 = (f32[16,6,144]{2,1,0:T(8,128)S(1)}, f32[16,6,144,144]{2,3,1,0:T(8,128)}) fusion(f32[16,6,144,144]{2,3,1,0:T(8,128)} %get-tuple-element.304, f32[16,6,144]{2,1,0:T(8,128)S(1)} %get-tuple-element.305, bf16[16,144,6,32]{1,3,2,0:T(8,128)(2,1)S(1)} %bitcast.203, bf16[16,144,3,6,32]{1,4,3,2,0:T(8,128)(2,1)} %bitcast.195), kind=kOutput, calls=%fused_computation.3.clone.1 | convolution fusion | flops 133360128 | bytes 24686592 | tf_op jit(solution)/shard_map/while/body/eval_jaxpr/bqhd,bkhd->bhqk/dot_general | solution.py:93
  333.4 9.2 %subtract_multiply_fusion.2 = bf16[16,6,144,144]{2,3,1,0:T(8,128)(2,1)} fusion(f32[16,6,144,144]{2,3,1,0:T(8,128)} %get-tuple-element.306, f32[16,6,144]{2,1,0:T(8,128)S(1)} %get-tuple-element.307, f32[16,6,144,144]{2,3,1,0:T(8,128)S(1)} %bitcast.191, f32[16,6,144]{2,1,0:T(8,128)S(1)} %get-tuple-element.305), kind=kLoop, calls=%fused_computation.2.clone.1 | loop fusion | flops 7962624 | bytes 20017152 | tf_op jit(solution)/shard_map/while/body/eval_jaxpr/mul | solution.py:95
  342.6 11.2 %copy.181 = bf16[16,6,144,144]{3,2,1,0:T(8,128)(2,1)} copy(bf16[16,6,144,144]{2,3,1,0:T(8,128)(2,1)} %subtract_multiply_fusion.2) | data formatting | bytes 7962624 | tf_op jit(solution)/shard_map/while/body/eval_jaxpr/mul | solution.py:95
  353.8 18.3 %reshape.134 = bf16[16,124416]{1,0:T(8,128)(2,1)} reshape(bf16[16,6,144,144]{3,2,1,0:T(8,128)(2,1)} %copy.181) | data formatting | bytes 7962624 | tf_op jit(solution)/shard_map/while/body/eval_jaxpr/reshape | solution.py:96
  372.2 9.1 %convolution_add_fusion.2 = f32[16,124416]{1,0:T(8,128)} fusion(bf16[16,124416]{1,0:T(8,128)(2,1)} %reshape.134, f32[16,124416]{1,0:T(8,128)} %get-tuple-element.326, pred[]{:T(512)S(6)} %compare.3, bf16[2,16,16]{2,1,0:T(8,128)(2,1)S(1)} %get-tuple-element.347, s32[]{:T(128)} %get-tuple-element.323), kind=kOutput, calls=%fused_computation.1.clone.1 | convolution fusion | flops 67682304 | bytes 19910660 | tf_op jit(solution)/shard_map/while/body/eval_jaxpr/dot_general | solution.py:96
  387.5 7.4 %fusion.134 = bf16[16,144,1,6,32]{1,4,3,0,2:T(8,128)(2,1)S(1)} fusion(bf16[16,144,6,32]{1,3,2,0:T(8,128)(2,1)S(1)} %bitcast.204, f32[16,6,144,144]{2,3,1,0:T(8,128)} %get-tuple-element.304, f32[16,6,144]{2,1,0:T(8,128)S(1)} %get-tuple-element.305), kind=kOutput, calls=%fused_computation.33.clone.1 | convolution fusion | flops 131825664 | bytes 9787392 | tf_op jit(solution)/shard_map/while/body/eval_jaxpr/bhqk,bqhd->bkhd/dot_general | solution.py:106
  421.0 8.1 %all-to-all-start.1 = ((bf16[8,192,192]{2,1,0:T(8,128)(2,1)}), bf16[8,192,192]{2,1,0:T(8,128)(2,1)S(1)}, u32[]{:S(2)}, u32[]{:S(2)}) async-start(bf16[8,192,192]{2,1,0:T(8,128)(2,1)} %broadcast_in_dim.50), calls=%async_computation.1 | async-start | bytes 1572864 | tf_op jit(solution)/shard_map/all_to_all | solution.py:27
  429.2 9.1 %all-to-all-done.1 = bf16[8,192,192]{2,1,0:T(8,128)(2,1)S(1)} async-done(((bf16[8,192,192]{2,1,0:T(8,128)(2,1)}), bf16[8,192,192]{2,1,0:T(8,128)(2,1)S(1)}, u32[]{:S(2)}, u32[]{:S(2)}) %all-to-all-start.1) | async-done | bytes 589856 | tf_op jit(solution)/shard_map/all_to_all | solution.py:27
  439.7 6.6 all-to-all-start
  451.9 9.0 %reshape.119 = bf16[16,6,20736]{2,1,0:T(8,128)(2,1)} reshape(bf16[16,124416]{1,0:T(8,128)(2,1)} %convert_element_type.82) | data formatting | bytes 7962624 | tf_op jit(solution)/shard_map/reshape | solution.py:201
  461.6 9.4 %all-to-all-done = bf16[8,192,576]{2,1,0:T(8,128)(2,1)S(1)} async-done(((bf16[8,192,576]{2,1,0:T(8,128)(2,1)}), bf16[8,192,576]{2,1,0:T(8,128)(2,1)S(1)}, u32[]{:S(2)}, u32[]{:S(2)}) %all-to-all-start) | async-done | bytes 1769504 | tf_op jit(solution)/shard_map/all_to_all | solution.py:27
  488.5 13.8 %collective-permute-done.4 = bf16[8,24,6,192]{3,0,2,1:T(8,128)(2,1)S(1)} collective-permute-done((bf16[8,24,6,192]{3,0,2,1:T(8,128)(2,1)S(1)}, bf16[8,24,6,192]{3,0,2,1:T(8,128)(2,1)S(1)}, u32[]{:S(2)}, u32[]{:S(2)}) %collective-permute-start.4) | collective-permute-done | bytes 442400 | tf_op jit(solution)/shard_map/ppermute | solution.py:22
  505.0 5.8 collective-permute-done.5
  514.1 129.2 %all-reduce.3.cloned.1.call-done = (bf16[16,6,20736]{2,1,0:T(8,128)(2,1)}, bf16[192,576]{1,0:T(8,128)(2,1)}, bf16[192,192]{1,0:T(8,128)(2,1)}) async-done(((bf16[16,6,20736]{2,1,0:T(8,128)(2,1)}, bf16[192,576]{1,0:T(8,128)(2,1)}, bf16[192,192]{1,0:T(8,128)(2,1)}), (bf16[16,6,20736]{2,1,0:T(8,128)(2,1)}, bf16[192,576]{1,0:T(8,128)(2,1)}, bf16[192,192]{1,0:T(8,128)(2,1)})) %all-reduce.3.cloned.1.call-update) | async-done | bytes 4276240 | tf_op jit(solution)/shard_map/psum | solution.py:197
  643.3 6.6 copy.144
  (219 shorter events, 154.7 us)
Async XLA Ops:
  10.8 11.5 %collective-permute-start = (bf16[8,3,24,192]{3,2,1,0:T(8,128)(2,1)}, bf16[8,3,24,192]{3,2,1,0:T(8,128)(2,1)S(1)}, u32[]{:S(2)}, u32[]{:S(2)}) collective-permute-start(bf16[8,3,24,192]{3,2,1,0:T(8,128)(2,1)} %pad_maximum_fusion.11), channel_id=1, source_target_pairs={{1,0},{2,1},{3,2},{4,3},{5,4},{6,5},{7,6},{9,8},{10,9},{11,10},{12... | collective-permute-start | bytes 663560 | tf_op jit(solution)/shard_map/ppermute | solution.py:16
  13.7 14.7 %collective-permute-start.2 = (bf16[8,3,24,192]{3,2,1,0:T(8,128)(2,1)}, bf16[8,3,24,192]{3,2,1,0:T(8,128)(2,1)S(1)}, u32[]{:S(2)}, u32[]{:S(2)}) collective-permute-start(bf16[8,3,24,192]{3,2,1,0:T(8,128)(2,1)} %pad_maximum_fusion.10), channel_id=1, source_target_pairs={{1,0},{2,1},{3,2},{4,3},{5,4},{6,5},{7,6},{9,8},{10,9},{11,10},{12... | collective-permute-start | bytes 663560 | tf_op jit(solution)/shard_map/ppermute | solution.py:16
  22.6 12.4 %collective-permute-start.1 = (bf16[8,24,6,192]{3,1,2,0:T(8,128)(2,1)S(1)}, bf16[8,24,6,192]{3,1,2,0:T(8,128)(2,1)S(1)}, u32[]{:S(2)}, u32[]{:S(2)}) collective-permute-start(bf16[8,24,6,192]{3,1,2,0:T(8,128)(2,1)S(1)} %copy.130), channel_id=1, source_target_pairs={{8,0},{16,8},{24,16},{32,24},{40,32},{48,40},{56,48},{64,56},{72,6... | collective-permute-start | bytes 1327112 | tf_op jit(solution)/shard_map/ppermute | solution.py:22
  29.5 15.4 %collective-permute-start.3 = (bf16[8,24,6,192]{3,1,2,0:T(8,128)(2,1)}, bf16[8,24,6,192]{3,1,2,0:T(8,128)(2,1)}, u32[]{:S(2)}, u32[]{:S(2)}) collective-permute-start(bf16[8,24,6,192]{3,1,2,0:T(8,128)(2,1)} %copy.135), channel_id=1, source_target_pairs={{8,0},{16,8},{24,16},{32,24},{40,32},{48,40},{56,48},{64,56},{72,6... | collective-permute-start | bytes 1327112 | tf_op jit(solution)/shard_map/ppermute | solution.py:22
  62.2 65.1 %copy-start.13 = (s32[2,16,144]{2,1,0:T(8,128)}, s32[2,16,144]{2,1,0:T(8,128)S(1)}, u32[]{:S(2)}) copy-start(s32[2,16,144]{2,1,0:T(8,128)S(1)} %get-tuple-element.345) | copy-start | bytes 55300 | tf_op jit(solution)/shard_map/while
  62.2 65.1 %copy-start.18 = (pred[2,16,144]{2,1,0:T(8,128)(4,1)}, pred[2,16,144]{2,1,0:T(8,128)(4,1)S(1)}, u32[]{:S(2)}) copy-start(pred[2,16,144]{2,1,0:T(8,128)(4,1)S(1)} %get-tuple-element.346) | copy-start | bytes 13828 | tf_op jit(solution)/shard_map/while
  128.3 16.0 %copy-start.3 = (bf16[2,16,144,192]{3,2,1,0:T(8,128)(2,1)S(1)}, bf16[2,16,144,192]{3,2,1,0:T(8,128)(2,1)}, u32[]{:S(2)}) copy-start(bf16[2,16,144,192]{3,2,1,0:T(8,128)(2,1)} %get-tuple-element.349) | copy-start | bytes 5308420 | tf_op jit(solution)/shard_map/while
  145.6 12.8 %copy-start = (bf16[16,144,192]{1,2,0:T(8,128)(2,1)}, bf16[16,144,192]{1,2,0:T(8,128)(2,1)S(1)}, u32[]{:S(2)}) copy-start(bf16[16,144,192]{1,2,0:T(8,128)(2,1)S(1)} %copy.177) | copy-start | bytes 2654212 | tf_op jit(solution)/shard_map/while
  145.6 12.8 %slice-start.2 = ((s8[14155776]{0:T(1024)(128)(4,1)}), s8[4194304]{0:T(1024)(128)(4,1)S(1)}, s32[]{:S(2)}) async-start(s8[14155776]{0:T(1024)(128)(4,1)} %bitcast.190), calls=%async_computation.5 | async-start | bytes 8388608 | tf_op jit(solution)/shard_map/while
  145.6 12.8 %slice-start.3 = ((s8[14155776]{0:T(1024)(128)(4,1)}), s8[4194304]{0:T(1024)(128)(4,1)S(1)}, s32[]{:S(2)}) async-start(s8[14155776]{0:T(1024)(128)(4,1)} %bitcast.190), calls=%async_computation.6 | async-start | bytes 8388608 | tf_op jit(solution)/shard_map/while
  145.6 14.6 %slice-start.4 = ((s8[14155776]{0:T(1024)(128)(4,1)}), s8[4194304]{0:T(1024)(128)(4,1)S(1)}, s32[]{:S(2)}) async-start(s8[14155776]{0:T(1024)(128)(4,1)} %bitcast.190), calls=%async_computation.7 | async-start | bytes 8388608 | tf_op jit(solution)/shard_map/while
  145.6 15.0 %slice-start.5 = ((s8[14155776]{0:T(1024)(128)(4,1)}), s8[1572864]{0:T(1024)(128)(4,1)S(1)}, s32[]{:S(2)}) async-start(s8[14155776]{0:T(1024)(128)(4,1)} %bitcast.190), calls=%async_computation.8 | async-start | bytes 3145728 | tf_op jit(solution)/shard_map/while
  181.0 25.0 %slice-start = ((s8[7077888]{0:T(1024)(128)(4,1)}), s8[2883584]{0:T(1024)(128)(4,1)S(1)}, s32[]{:S(2)}) async-start(s8[7077888]{0:T(1024)(128)(4,1)} %bitcast.188), calls=%async_computation.3 | async-start | bytes 5767168 | tf_op jit(solution)/shard_map/while
  199.3 6.8 %slice-start.1 = ((s8[7077888]{0:T(1024)(128)(4,1)}), s8[4194304]{0:T(1024)(128)(4,1)S(1)}, s32[]{:S(2)}) async-start(s8[7077888]{0:T(1024)(128)(4,1)} %bitcast.188), calls=%async_computation.4 | async-start | bytes 8388608 | tf_op jit(solution)/shard_map/while
  235.2 64.9 %copy-start.13 = (s32[2,16,144]{2,1,0:T(8,128)}, s32[2,16,144]{2,1,0:T(8,128)S(1)}, u32[]{:S(2)}) copy-start(s32[2,16,144]{2,1,0:T(8,128)S(1)} %get-tuple-element.345) | copy-start | bytes 55300 | tf_op jit(solution)/shard_map/while
  235.2 64.9 %copy-start.18 = (pred[2,16,144]{2,1,0:T(8,128)(4,1)}, pred[2,16,144]{2,1,0:T(8,128)(4,1)S(1)}, u32[]{:S(2)}) copy-start(pred[2,16,144]{2,1,0:T(8,128)(4,1)S(1)} %get-tuple-element.346) | copy-start | bytes 13828 | tf_op jit(solution)/shard_map/while
  301.1 16.0 %copy-start.3 = (bf16[2,16,144,192]{3,2,1,0:T(8,128)(2,1)S(1)}, bf16[2,16,144,192]{3,2,1,0:T(8,128)(2,1)}, u32[]{:S(2)}) copy-start(bf16[2,16,144,192]{3,2,1,0:T(8,128)(2,1)} %get-tuple-element.349) | copy-start | bytes 5308420 | tf_op jit(solution)/shard_map/while
  318.4 12.8 %copy-start = (bf16[16,144,192]{1,2,0:T(8,128)(2,1)}, bf16[16,144,192]{1,2,0:T(8,128)(2,1)S(1)}, u32[]{:S(2)}) copy-start(bf16[16,144,192]{1,2,0:T(8,128)(2,1)S(1)} %copy.177) | copy-start | bytes 2654212 | tf_op jit(solution)/shard_map/while
  318.4 12.8 %slice-start.2 = ((s8[14155776]{0:T(1024)(128)(4,1)}), s8[4194304]{0:T(1024)(128)(4,1)S(1)}, s32[]{:S(2)}) async-start(s8[14155776]{0:T(1024)(128)(4,1)} %bitcast.190), calls=%async_computation.5 | async-start | bytes 8388608 | tf_op jit(solution)/shard_map/while
  318.4 12.8 %slice-start.3 = ((s8[14155776]{0:T(1024)(128)(4,1)}), s8[4194304]{0:T(1024)(128)(4,1)S(1)}, s32[]{:S(2)}) async-start(s8[14155776]{0:T(1024)(128)(4,1)} %bitcast.190), calls=%async_computation.6 | async-start | bytes 8388608 | tf_op jit(solution)/shard_map/while
  318.4 14.6 %slice-start.4 = ((s8[14155776]{0:T(1024)(128)(4,1)}), s8[4194304]{0:T(1024)(128)(4,1)S(1)}, s32[]{:S(2)}) async-start(s8[14155776]{0:T(1024)(128)(4,1)} %bitcast.190), calls=%async_computation.7 | async-start | bytes 8388608 | tf_op jit(solution)/shard_map/while
  318.4 15.0 %slice-start.5 = ((s8[14155776]{0:T(1024)(128)(4,1)}), s8[1572864]{0:T(1024)(128)(4,1)S(1)}, s32[]{:S(2)}) async-start(s8[14155776]{0:T(1024)(128)(4,1)} %bitcast.190), calls=%async_computation.8 | async-start | bytes 3145728 | tf_op jit(solution)/shard_map/while
  353.8 27.4 %slice-start = ((s8[7077888]{0:T(1024)(128)(4,1)}), s8[2883584]{0:T(1024)(128)(4,1)S(1)}, s32[]{:S(2)}) async-start(s8[7077888]{0:T(1024)(128)(4,1)} %bitcast.188), calls=%async_computation.3 | async-start | bytes 5767168 | tf_op jit(solution)/shard_map/while
  372.2 9.1 %slice-start.1 = ((s8[7077888]{0:T(1024)(128)(4,1)}), s8[4194304]{0:T(1024)(128)(4,1)S(1)}, s32[]{:S(2)}) async-start(s8[7077888]{0:T(1024)(128)(4,1)} %bitcast.188), calls=%async_computation.4 | async-start | bytes 8388608 | tf_op jit(solution)/shard_map/while
  419.1 10.1 %copy-start.12 = (f32[192,576]{1,0:T(8,128)S(1)}, f32[192,576]{1,0:T(8,128)}, u32[]{:S(2)}) copy-start(f32[192,576]{1,0:T(8,128)} %get-tuple-element.368) | copy-start | bytes 1327108
  421.0 17.2 %all-to-all-start.1 = ((bf16[8,192,192]{2,1,0:T(8,128)(2,1)}), bf16[8,192,192]{2,1,0:T(8,128)(2,1)S(1)}, u32[]{:S(2)}, u32[]{:S(2)}) async-start(bf16[8,192,192]{2,1,0:T(8,128)(2,1)} %broadcast_in_dim.50), calls=%async_computation.1 | async-start | bytes 1572864 | tf_op jit(solution)/shard_map/all_to_all | solution.py:27
  439.7 31.4 %all-to-all-start = ((bf16[8,192,576]{2,1,0:T(8,128)(2,1)}), bf16[8,192,576]{2,1,0:T(8,128)(2,1)S(1)}, u32[]{:S(2)}, u32[]{:S(2)}) async-start(bf16[8,192,576]{2,1,0:T(8,128)(2,1)} %broadcast_in_dim.49), calls=%async_computation | async-start | bytes 3932160 | tf_op jit(solution)/shard_map/all_to_all | solution.py:27
  446.3 197.0 %all-reduce.3.cloned.1.call-start = ((), (), s32[]{:S(2)}) async-start(), calls=%async_computation.2 | async-start | bytes 11304960 | tf_op jit(solution)/shard_map/psum | solution.py:197
  486.0 16.3 %collective-permute-start.4 = (bf16[8,24,6,192]{3,0,2,1:T(8,128)(2,1)S(1)}, bf16[8,24,6,192]{3,0,2,1:T(8,128)(2,1)S(1)}, u32[]{:S(2)}, u32[]{:S(2)}) collective-permute-start(bf16[8,24,6,192]{3,0,2,1:T(8,128)(2,1)S(1)} %slice.99), channel_id=1, source_target_pairs={{120,0},{0,8},{8,16},{16,24},{24,32},{32,40},{40,48},{48,56},{56,6... | collective-permute-start | bytes 1327112 | tf_op jit(solution)/shard_map/ppermute | solution.py:22
  502.3 8.5 %collective-permute-start.5 = (bf16[8,3,24,192]{3,0,2,1:T(8,128)(2,1)S(1)}, bf16[8,3,24,192]{3,0,2,1:T(8,128)(2,1)S(1)}, u32[]{:S(2)}, u32[]{:S(2)}) collective-permute-start(bf16[8,3,24,192]{3,0,2,1:T(8,128)(2,1)S(1)} %pad_maximum_fusion.9), channel_id=1, source_target_pairs={{0,1},{1,2},{2,3},{3,4},{4,5},{5,6},{6,7},{8,9},{9,10},{10,11},{11... | collective-permute-start | bytes 663560 | tf_op jit(solution)/shard_map/ppermute | solution.py:16
  643.3 6.6 copy-start.15
  643.3 7.4 %copy-start.20 = (bf16[192,192]{1,0:T(8,128)(2,1)S(1)}, bf16[192,192]{1,0:T(8,128)(2,1)}, u32[]{:S(2)}) copy-start(bf16[192,192]{1,0:T(8,128)(2,1)} %get-tuple-element.216) | copy-start | bytes 221188
  (32 other events, 105.6 us)
Sparse Core Ops, SparseCore 0:
  472.3 170.9 all-reduce.2
where the time goes:
time: 665 us; the launch traced here: 658 us
  local copies, waits for them, and re-layouts  214 us (32%)
  waiting for transfers between devices  172 us (26%)
  matrix products  145 us (22%)
  other arithmetic  76.8 us (12%)
  starting transfers between devices  25.7 us (4%)
  between operations  14.6 us (2%)
  loops' own time  10.1 us (2%)
    psum x1, waiting for transfers between devices, local(): lax.psum(totals[2].astype(jnp.bfloat16), 'lon').astype(jnp.float32)  129 us
    dot_general x4, local copies, waits for them, and re-layouts, window_backward(): jnp.dot(block_types.astype(jnp.bfloat16), bias_rows, preferred_element_ty...  64.9 us
    reshape x2, local copies, waits for them, and re-layouts, window_backward(): score_grad.reshape(windows, -1)  36.6 us
    sub x2, other arithmetic, window_backward(): exp_terms = jnp.where(allowed, jnp.exp(scores - peak_score), 0.0)  31.9 us
    dot_general x2, matrix products, window_backward(): jnp.einsum('bqhd,bkhd->bhqk', queries, key_rows, preferred_element_type=f32)  26.2 us
    dot_general x2, matrix products, window_backward(): jnp.einsum('bqhd,bkhd->bhqk', mixed_grad, values, preferred_element_type=...  25.6 us
    dot_general x2, matrix products, window_backward(): jnp.dot(block_types.astype(jnp.bfloat16), bias_rows, preferred_element_ty...  24.7 us
    unnamed x20, local copies, waits for them, and re-layouts  23.4 us
  transfers between devices with their start and end apart: 9, of which 7 were waited for; matrix products, arithmetic and copies ran while one was open for 8% of the time, Pallas kernels for 0%

commit v1 on v0

v1 whole, which is shorter than its diff:
```python
import functools
import jax
import jax.numpy as jnp
from jax import lax
from jax.experimental import pallas as pl
from jax.experimental.pallas import tpu as pltpu
from jax.sharding import PartitionSpec as P

HEADS = 6
WIN_Z = 2
WIN_LAT = 6
WIN_LON = 12
WTOK = 144
HD = 32
C = 192
MAIN = 128
TAIL = WTOK - MAIN
PACK = 896
SCALE = HD ** -0.5
LOG2E = 1.4426950408889634
BF = jnp.bfloat16
F32 = jnp.float32


def dot(a, b):
    return jnp.dot(a, b, preferred_element_type=F32)


def lane_head(shape):
    return lax.broadcasted_iota(jnp.int32, shape, 1) // HD


def core_kernel(x_ref, g_ref, wq_ref, wqt_ref, wpt_ref, bias_ref, penz_ref, penl_ref,
                gin_ref, gq_ref, gp_ref, gb_ref, gsum):
    t = pl.program_id(0)
    last = (lax.axis_index("lat") == lax.axis_size("lat") - 1)
    z_on = (t % 4 == 3).astype(F32)
    l_on = (jnp.logical_and(last, t // 4 == 3)).astype(F32)

    @pl.when(t == 0)
    def _():
        gq_ref[...] = jnp.zeros_like(gq_ref)
        gp_ref[...] = jnp.zeros_like(gp_ref)

    x = x_ref[0]
    cot = g_ref[0]
    proj = dot(x, wq_ref[...]).astype(BF)
    dmix = dot(cot, wpt_ref[...]).astype(BF)
    xt = x.T
    dq_l, dk_l, dv_l, mixm, mixt, cott = [], [], [], [], [], []
    for c in range(2):
        rows = slice(c * WTOK, (c + 1) * WTOK)
        q = proj[rows, 0:192]
        k = proj[rows, 256:448]
        v = proj[rows, 512:704]
        dm = dmix[rows]
        ct = cot[rows]
        qt, kt, vt, dmt = q.T, k.T, v.T, dm.T
        hm = lane_head((MAIN, C))
        ht = lane_head((TAIL, C))
        zq = jnp.zeros((HD, MAIN), BF)

        def blk(at, p):
            top = jnp.concatenate([at[64 * p:64 * p + 32, :MAIN], zq], axis=1)
            bot = jnp.concatenate([zq, at[64 * p + 32:64 * p + 64, :MAIN]], axis=1)
            two = jnp.concatenate([top, bot], axis=0)
            if p == 2:
                return two
            z64 = jnp.zeros((64, 256), BF)
            return jnp.concatenate([two, z64] if p == 0 else [z64, two], axis=0)

        def nat(a, p):
            lanes = slice(0, 128) if p < 2 else slice(128, 192)
            am = a[:MAIN, lanes]
            hh = hm[:, lanes]
            z = jnp.zeros_like(am)
            return jnp.concatenate([jnp.where(hh == 2 * p, am, z), jnp.where(hh == 2 * p + 1, am, z)], axis=0)

        def nat_tail(a):
            am = a[MAIN:]
            z = jnp.zeros_like(am)
            return jnp.concatenate([jnp.where(ht == h, am, z) for h in range(HEADS)], axis=0)

        q_tail, dm_tail = nat_tail(q), nat_tail(dm)
        dn = (((1,), (1,)), ((), ()))
        dk_a = dk_b = dv_a = dv_b = None
        mix_parts, dq_parts = [], []
        for p in range(4):
            if p < 3:
                ln = slice(256 * p, 256 * p + 256)
                sub = slice(0, 128) if p < 2 else slice(128, 192)
                s = dot(k[:, sub], blk(qt, p))
                dp = dot(v[:, sub], blk(dmt, p))
            else:
                ln = slice(768, 864)
                s = lax.dot_general(k, q_tail, dn, preferred_element_type=F32)
                dp = lax.dot_general(v, dm_tail, dn, preferred_element_type=F32)
            bias = bias_ref[0, :, ln].astype(F32) * LOG2E + z_on * penz_ref[:, ln].astype(F32) + l_on * penl_ref[:, ln].astype(F32)
            s = s * (SCALE * LOG2E) + bias
            m = jnp.max(s, axis=0, keepdims=True)
            e = jnp.exp2(s - m)
            r = 1.0 / jnp.sum(e, axis=0, keepdims=True)
            pr = e * r
            pb = pr.astype(BF)
            d = jnp.sum(pr * dp, axis=0, keepdims=True)
            gs = pr * (dp - d)
            gb = gs.astype(BF)
            if c == 0:
                gsum[:, ln] = gs
            else:
                gb_ref[0, :, ln] = (gsum[:, ln] + gs).astype(BF)
            if p < 3:
                mo = dot(vt[64 * p:64 * p + 64], pb).astype(BF)
                do = dot(kt[64 * p:64 * p + 64], gb)
                mix_parts += [mo[:32, :MAIN], mo[32:, MAIN:]]
                dq_parts += [do[:32, :MAIN], do[32:, MAIN:]]
                dkp = dot(gb, nat(q, p))
                dvp = dot(pb, nat(dm, p))
                if p < 2:
                    dk_a = dkp if dk_a is None else dk_a + dkp
                    dv_a = dvp if dv_a is None else dv_a + dvp
                else:
                    dk_b, dv_b = dkp, dvp
            else:
                mo = dot(vt, pb).astype(BF)
                do = (dot(kt, gb) * SCALE).astype(BF)
                rh = lax.broadcasted_iota(jnp.int32, (C, 96), 0) // HD
                lh = lax.broadcasted_iota(jnp.int32, (C, 96), 1) // TAIL
                mixt.append(jnp.where(rh == lh, mo, jnp.zeros_like(mo)))
                dot_t = do.T
                dq_tail = jnp.zeros((TAIL, C), BF)
                for h in range(HEADS):
                    dq_tail = jnp.where(ht == h, dot_t[TAIL * h:TAIL * h + TAIL], dq_tail)
                dk_a = dk_a + dot(gb, q_tail[:, :128])
                dk_b = dk_b + dot(gb, q_tail[:, 128:])
                dv_a = dv_a + dot(pb, dm_tail[:, :128])
                dv_b = dv_b + dot(pb, dm_tail[:, 128:])
        mixm.append(jnp.concatenate(mix_parts, axis=0))
        dqt = (jnp.concatenate(dq_parts, axis=0) * SCALE).astype(BF)
        dq_l.append(jnp.concatenate([dqt.T, dq_tail], axis=0))
        dk_l.append((jnp.concatenate([dk_a, dk_b], axis=1) * SCALE).astype(BF))
        dv_l.append(jnp.concatenate([dv_a, dv_b], axis=1).astype(BF))
        cott.append(jnp.concatenate([ct[MAIN:]] * HEADS, axis=0))
    mm = jnp.concatenate(mixm, axis=1)
    cm = jnp.concatenate([cot[0:MAIN], cot[WTOK:WTOK + MAIN]], axis=0)
    gp_ref[...] += dot(mm, cm) + dot(mixt[0], cott[0]) + dot(mixt[1], cott[1])
    dq = jnp.concatenate(dq_l, axis=0)
    dk = jnp.concatenate(dk_l, axis=0)
    dv = jnp.concatenate(dv_l, axis=0)
    gq_ref[0] += dot(xt, dq)
    gq_ref[1] += dot(xt, dk)
    gq_ref[2] += dot(xt, dv)
    gin = dot(dq, wqt_ref[0]) + dot(dk, wqt_ref[1]) + dot(dv, wqt_ref[2])
    gin_ref[0] = gin.astype(BF)


def penalties():
    k = jnp.arange(WTOK, dtype=jnp.int32)
    lane = jnp.arange(PACK, dtype=jnp.int32)
    q = jnp.where(lane < 768, lane % 128, 128 + lane % 16)
    z = (k[:, None] // 72) != (q[None, :] // 72)
    l = ((k[:, None] // 12) % 6 >= 3) != ((q[None, :] // 12) % 6 >= 3)
    return jnp.where(z, -1e30, 0.0).astype(BF), jnp.where(l, -1e30, 0.0).astype(BF)


def run_core(xw, gw, weight_qkv, weight_proj, bias_p):
    n = xw.shape[0]
    wq = weight_qkv.reshape(C, 3, C)
    wq_pad = jnp.pad(wq, ((0, 0), (0, 0), (0, 64))).reshape(C, 768)
    wqt = wq.transpose(1, 2, 0)
    wpt = weight_proj.T
    penz, penl = penalties()
    whole = lambda *s: pl.BlockSpec(s, lambda t: (0,) * len(s))
    return pl.pallas_call(
        core_kernel,
        grid=(n,),
        in_specs=[
            pl.BlockSpec((1, 2 * WTOK, C), lambda t: (t, 0, 0)),
            pl.BlockSpec((1, 2 * WTOK, C), lambda t: (t, 0, 0)),
            whole(C, 768), whole(3, C, C), whole(C, C),
            pl.BlockSpec((1, WTOK, PACK), lambda t: (t, 0, 0)),
            whole(WTOK, PACK), whole(WTOK, PACK),
        ],
        out_specs=[
            pl.BlockSpec((1, 2 * WTOK, C), lambda t: (t, 0, 0)),
            whole(3, C, C), whole(C, C),
            pl.BlockSpec((1, WTOK, PACK), lambda t: (t, 0, 0)),
        ],
        out_shape=[
            jax.ShapeDtypeStruct((n, 2 * WTOK, C), BF),
            jax.ShapeDtypeStruct((3, C, C), F32),
            jax.ShapeDtypeStruct((C, C), F32),
            jax.ShapeDtypeStruct((n, WTOK, PACK), BF),
        ],
        scratch_shapes=[pltpu.VMEM((WTOK, PACK), F32)],
        name="core",
    )(xw, gw, wq_pad, wqt, wpt, bias_p, penz, penl)


def bias_pack(bias_table):
    n = bias_table.shape[0]
    b = bias_table.reshape(n, HEADS, WTOK, WTOK).transpose(0, 3, 1, 2)
    main = b[..., :MAIN].reshape(n, WTOK, HEADS * MAIN)
    tail = b[..., MAIN:].reshape(n, WTOK, HEADS * TAIL)
    return jnp.concatenate([main, tail, jnp.zeros((n, WTOK, 32), b.dtype)], axis=2)


def bias_unpack(g):
    n = g.shape[0]
    main = g[..., :768].reshape(n, WTOK, HEADS, MAIN)
    tail = g[..., 768:864].reshape(n, WTOK, HEADS, TAIL)
    b = jnp.concatenate([main, tail], axis=3)
    return b.transpose(0, 2, 3, 1).reshape(n, HEADS, WTOK * WTOK)


def passed_along(block, axis, distance):
    devices = range(lax.axis_size(axis))
    route = [(i - distance, i) for i in devices if i - distance in devices]
    return lax.ppermute(block, axis, route)


def from_behind(block, axis, distance):
    devices = range(lax.axis_size(axis))
    route = [((i - distance) % len(devices), i) for i in devices]
    return lax.ppermute(block, axis, route)


def split_types(f):
    z, h, w, c = f.shape
    f = f.reshape(z // 2, 2, h // 6, 6, w // 12, 12, c).transpose(2, 0, 4, 1, 3, 5, 6)
    return f.reshape((h // 6) * (z // 2), (w // 12) * WTOK, c)


def merge_types(g, z, h, w):
    c = g.shape[-1]
    g = g.reshape(h // 6, z // 2, w // 12, 2, 6, 12, c).transpose(1, 3, 0, 4, 2, 5, 6)
    return g.reshape(z, h, w, c)


def frame(a):
    a = jnp.roll(a, -1, axis=0)
    up = passed_along(a[:, :3], "lat", -1)
    tall = jnp.concatenate([a[:, 3:], up], axis=1)
    across = from_behind(tall[:, :, :6], "lon", -1)
    return jnp.concatenate([tall[:, :, 6:], across], axis=2)


def of_everyone(x, axis):
    n = lax.axis_size(axis)
    e = lax.all_to_all(jnp.broadcast_to(x[None], (n, *x.shape)), axis, 0, 0, tiled=True)
    return jnp.sum(e.astype(F32), axis=0)


def local(normed, cotangent, weight_qkv, weight_proj, bias_table):
    levels, height, breadth, channels = normed.shape
    xw = split_types(frame(normed))
    gw = split_types(frame(cotangent))
    bias_p = bias_pack(bias_table)
    gin, gq, gp, gb = run_core(xw, gw, weight_qkv, weight_proj, bias_p)
    fg = merge_types(gin, levels, height, breadth)
    side = from_behind(fg[:, :, breadth - 6:], "lon", 1)
    tall = jnp.concatenate([side, fg[:, :, :breadth - 6]], axis=2)
    ret = passed_along(tall[:, height - 3:], "lat", 1)
    input_grad = jnp.roll(jnp.concatenate([ret, tall[:, :height - 3]], axis=1), 1, axis=0)
    gb = lax.psum_scatter(gb, "lon", scatter_dimension=0, tiled=True)
    gb = lax.all_gather(bias_unpack(gb), "lon", axis=0, tiled=True)
    bias_grad = gb.astype(F32)
    w = jnp.concatenate([gq.transpose(1, 0, 2).reshape(C, 3 * C), gp], axis=1).astype(BF)
    w = of_everyone(w, "lat")
    w = lax.psum(w.astype(BF), "lon").astype(F32)
    return input_grad, w[:, :3 * C], w[:, 3 * C:], bias_grad


def solution(mesh):
    in_specs = (P(None, "lat", "lon", None), P(None, "lat", "lon", None), P(), P(), P("lat", None, None))
    out_specs = (P(None, "lat", "lon", None), P(), P(), P("lat", None, None))
    return jax.shard_map(local, mesh=mesh, in_specs=in_specs, out_specs=out_specs, check_vma=False)
```

time: 665 us -> 444 us (0.67)
  matrix products: 145 us -> 0 us
  local copies, waits for them, and re-layouts: 214 us -> 89.6 us
  Pallas kernels: 0 us -> 57.9 us
  other arithmetic: 76.8 us -> 21.8 us
  waiting for transfers between devices: 172 us -> 208 us
  blocking collectives: 0 us -> 35.4 us
  starting transfers between devices: 25.7 us -> 15.4 us
  loops' own time: 10.1 us -> 0 us
    dot_general x26 -> x0, matrix products: 145 us -> none  [the longest x2 26.2 us: window_backward(): jnp.einsum('bqhd,bkhd->bhqk', queries, key_rows, preferred_element_type=f32)]
    dot_general x4 -> x0, local copies, waits for them, and re-layouts: 64.9 us -> none  [window_backward(): jnp.dot(block_types.astype(jnp.bfloat16), bias_rows, preferred_element_ty...]
    all_gather x0 -> x1, waiting for transfers between devices: none -> 59.2 us  [local(): gb = lax.all_gather(bias_unpack(gb), 'lon', axis=0, tiled=True)]
    pallas_call x0 -> x1, Pallas kernels: none -> 57.9 us  [run_core(): pl.pallas_call(core_kernel, grid=(n,), in_specs=[pl.BlockSpec((1, 2 * WTO...]
    reduce_scatter x0 -> x1, waiting for transfers between devices: none -> 44.2 us  [local(): gb = lax.psum_scatter(gb, 'lon', scatter_dimension=0, tiled=True)]
    all_to_all x0 -> x1, blocking collectives: none -> 35.4 us  [of_everyone(): lax.all_to_all(jnp.broadcast_to(x[None], (n, *x.shape)), axis, 0, 0, tile...]
    psum x1, waiting for transfers between devices: 129 us -> 94.1 us  [local(): w = lax.psum(w.astype(BF), 'lon').astype(F32)]
    sub x2 -> x0, other arithmetic: 31.9 us -> none  [window_backward(): exp_terms = jnp.where(allowed, jnp.exp(scores - peak_score), 0.0)]
  transfers between devices with their start and end apart: 9 -> 9, of which waited for: 7 -> 5; matrix products, arithmetic and copies ran while one was open for 8% -> 20% of each run, Pallas kernels for 0% -> 0%
where the time goes in v1:
time: 444 us; the launch traced here: 443 us
  waiting for transfers between devices  208 us (47%)
  local copies, waits for them, and re-layouts  89.6 us (20%)
  Pallas kernels  57.9 us (13%)
  blocking collectives  35.4 us (8%)
  other arithmetic  21.8 us (5%)
  starting transfers between devices  15.4 us (3%)
  between operations  14.2 us (3%)
    psum x1, waiting for transfers between devices, local(): w = lax.psum(w.astype(BF), 'lon').astype(F32)  94.1 us
    all_gather x1, waiting for transfers between devices, local(): gb = lax.all_gather(bias_unpack(gb), 'lon', axis=0, tiled=True)  59.2 us
    pallas_call x1, Pallas kernels, run_core(): pl.pallas_call(core_kernel, grid=(n,), in_specs=[pl.BlockSpec((1, 2 * WTO...  57.9 us
    reduce_scatter x1, waiting for transfers between devices, local(): gb = lax.psum_scatter(gb, 'lon', scatter_dimension=0, tiled=True)  44.2 us
    all_to_all x1, blocking collectives, of_everyone(): lax.all_to_all(jnp.broadcast_to(x[None], (n, *x.shape)), axis, 0, 0, tile...  35.4 us
    reshape x2, local copies, waits for them, and re-layouts, bias_pack(): b = bias_table.reshape(n, HEADS, WTOK, WTOK).transpose(0, 3, 1, 2)  18 us
    unnamed x30, local copies, waits for them, and re-layouts  11.4 us
    reshape x4, local copies, waits for them, and re-layouts, split_types(): return f.reshape(h // 6 * (z // 2), w // 12 * WTOK, c)  9.96 us
  transfers between devices with their start and end apart: 9, of which 5 were waited for; matrix products, arithmetic and copies ran while one was open for 20% of the time, Pallas kernels for 0%

profile of v1, /device:TPU:1, one launch (start us, length us, event | category | flops | bytes accessed | tf_op | source)
XLA Modules:
  0.0 442.8 jit_solution(5097437100520863163)
XLA Ops:
  8.2 1.9 slice.76
  15.8 14.3 %reshape.194 = bf16[16,6,144,144]{3,2,0,1:T(8,128)(2,1)} reshape(bf16[16,6,20736]{2,0,1:T(8,128)(2,1)} %param.9) | data formatting | bytes 7962624 | tf_op jit(solution)/shard_map/reshape | solution.py:202
  30.1 3.7 copy.123
  33.9 3.7 slice.108
  38.8 6.0 %copy.119 = bf16[16,144,768]{2,1,0:T(8,128)(2,1)S(1)} copy(bf16[16,144,768]{1,2,0:T(8,128)(2,1)} %bitcast.37) | data formatting | bytes 7077888 | tf_op jit(solution)/shard_map/reshape | solution.py:203
  44.8 4.0 maximum_maximum_fusion.bias_ref
  52.1 1.8 fusion.1
  58.5 4.9 %collective-permute-start.3 = (bf16[8,24,6,192]{3,1,2,0:T(8,128)(2,1)}, bf16[8,24,6,192]{3,1,2,0:T(8,128)(2,1)}, u32[]{:S(2)}, u32[]{:S(2)}) collective-permute-start(bf16[8,24,6,192]{3,1,2,0:T(8,128)(2,1)} %copy.95), channel_id=1, source_target_pairs={{8,0},{16,8},{24,16},{32,24},{40,32},{48,40},{56,48},{64,56},{72,6... | collective-permute-start | bytes 1327112 | tf_op jit(solution)/shard_map/ppermute | solution.py:225
  65.1 3.1 slice_maximum_fusion
  70.6 2.5 reshape.188
  73.2 2.4 copy.117
  75.6 2.6 reshape.202.x_ref
  79.4 2.5 pad_maximum_fusion.5
  83.2 2.6 reshape.190
  85.8 2.4 copy.118
  88.2 2.6 reshape.203.g_ref
  90.8 57.9 %core.1 = (bf16[16,288,192]{2,1,0:T(8,128)(2,1)}, f32[3,192,192]{2,1,0:T(8,128)}, f32[192,192]{1,0:T(8,128)}, bf16[16,144,896]{2,1,0:T(8,128)(2,1)}) custom-call(bf16[16,288,192]{2,1,0:T(8,128)(2,1)} %reshape.202.x_ref, bf16[16,288,192]{2,1,0:T(8,128)(2,1)} %reshape.203.g_ref, bf16[192,768]{1,0:T(8,128)(2,1)} %copy.106.wq_ref, ...), custom_call_target="tpu_custom_call" | custom-call | tf_op jit(solution)/shard_map/core/pallas_call | solution.py:174
  150.4 35.4 %all_to_all.5 = bf16[8,192,768]{2,1,0:T(8,128)(2,1)S(1)} all-to-all(bf16[8,192,768]{2,1,0:T(8,128)(2,1)S(1)} %broadcast_in_dim.26), channel_id=1, replica_groups=mesh['lon'=16,'lat'=8] {'lat'}, dimensions={0} | all-to-all | bytes 4718592 | tf_op jit(solution)/shard_map/all_to_all | solution.py:250
  187.1 44.2 %reduce-scatter.2.cloned.1.call-done = bf16[1,144,896]{2,1,0:T(8,128)(2,1)} async-done(((bf16[16,144,896]{2,1,0:T(8,128)(2,1)}), bf16[1,144,896]{2,1,0:T(8,128)(2,1)}) %reduce-scatter.2.cloned.1.call-update) | async-done | bytes 258064 | tf_op jit(solution)/shard_map/reduce_scatter | solution.py:265
  235.5 3.0 copy.107
  238.5 2.2 reshape.197
  240.7 6.7 %copy.108 = bf16[4,2,4,6,2,12,192]{6,1,0,5,4,3,2:T(2,128)(2,1)} copy(bf16[4,2,4,6,2,12,192]{6,0,2,5,3,1,4:T(4,128)(2,1)} %bitcast.38) | data formatting | bytes 3538944 | tf_op jit(solution)/shard_map/transpose | solution.py:236
  247.4 5.0 %reshape.198 = bf16[8,24,24,192]{3,0,2,1:T(8,128)(2,1)S(1)} reshape(bf16[4,2,4,6,2,12,192]{6,1,0,5,4,3,2:T(2,128)(2,1)} %copy.108) | data formatting | bytes 3538944 | tf_op jit(solution)/shard_map/reshape | solution.py:237
  252.5 3.0 collective-permute-start.4
  255.6 7.2 %collective-permute-done.4 = bf16[8,24,6,192]{3,0,2,1:T(8,128)(2,1)S(1)} collective-permute-done((bf16[8,24,6,192]{3,0,2,1:T(8,128)(2,1)S(1)}, bf16[8,24,6,192]{3,0,2,1:T(8,128)(2,1)S(1)}, u32[]{:S(2)}, u32[]{:S(2)}) %collective-permute-start.4) | collective-permute-done | bytes 442400 | tf_op jit(solution)/shard_map/ppermute | solution.py:225
  262.8 3.2 collective-permute-start.5
  266.0 3.6 collective-permute-done.5
  271.0 1.9 copy.115
  272.9 94.1 %all-reduce.3.cloned.1.call-done = bf16[192,768]{1,0:T(8,128)(2,1)} async-done(((bf16[192,768]{1,0:T(8,128)(2,1)}), bf16[192,768]{1,0:T(8,128)(2,1)}) %all-reduce.3.cloned.1.call-update) | async-done | bytes 294928 | tf_op jit(solution)/shard_map/psum | solution.py:270
  367.0 1.8 slice.112
  370.5 59.2 %all-gather.2.cloned.1.call-done = bf16[16,6,20736]{2,1,0:T(8,128)(2,1)} async-done(((bf16[1,6,20736]{2,1,0:T(8,128)(2,1)}), bf16[16,6,20736]{2,1,0:T(8,128)(2,1)}) %all-gather.2.cloned.1.call-update) | async-done | bytes 3981328 | tf_op jit(solution)/shard_map/all_gather | solution.py:266
  429.7 6.5 %copy.116 = f32[16,6,20736]{2,0,1:T(8,128)} copy(bf16[16,6,20736]{2,1,0:T(8,128)(2,1)} %all-gather.2.cloned.1.call-done) | data formatting | bytes 11943936
  (89 shorter events, 32.7 us)
Async XLA Ops:
  7.2 224.1 %reduce-scatter.2.cloned.1.call-start = ((), (), s32[]{:S(2)}) async-start(), calls=%async_computation.3 | async-start | bytes 4386816 | tf_op jit(solution)/shard_map/reduce_scatter | solution.py:265
  8.2 2.7 copy-start.6
  8.2 4.0 copy-start.8
  10.1 2.1 copy-start.1
  10.9 43.0 %collective-permute-start = (bf16[8,3,24,192]{3,2,1,0:T(8,128)(2,1)}, bf16[8,3,24,192]{3,2,1,0:T(8,128)(2,1)}, u32[]{:S(2)}, u32[]{:S(2)}) collective-permute-start(bf16[8,3,24,192]{3,2,1,0:T(8,128)(2,1)} %pad_maximum_fusion.11), channel_id=1, source_target_pairs={{1,0},{2,1},{3,2},{4,3},{5,4},{6,5},{7,6},{9,8},{10,9},{11,10},{12... | collective-permute-start | bytes 663560 | tf_op jit(solution)/shard_map/ppermute | solution.py:219
  12.3 2.3 copy-start.4
  12.4 1.3 copy-start
  14.5 42.1 %collective-permute-start.2 = (bf16[8,3,24,192]{3,2,1,0:T(8,128)(2,1)}, bf16[8,3,24,192]{3,2,1,0:T(8,128)(2,1)}, u32[]{:S(2)}, u32[]{:S(2)}) collective-permute-start(bf16[8,3,24,192]{3,2,1,0:T(8,128)(2,1)} %pad_maximum_fusion.10), channel_id=1, source_target_pairs={{1,0},{2,1},{3,2},{4,3},{5,4},{6,5},{7,6},{9,8},{10,9},{11,10},{12... | collective-permute-start | bytes 663560 | tf_op jit(solution)/shard_map/ppermute | solution.py:219
  44.8 5.0 %copy-start.2 = (bf16[7,24,24,192]{3,2,1,0:T(8,128)(2,1)S(1)}, bf16[7,24,24,192]{3,2,1,0:T(8,128)(2,1)}, u32[]{:S(2)}) copy-start(bf16[7,24,24,192]{3,2,1,0:T(8,128)(2,1)} %copy-done.1) | copy-start | bytes 4644868
  44.8 5.0 %copy-start.7 = (bf16[1,24,24,192]{3,2,1,0:T(8,128)(2,1)S(1)}, bf16[1,24,24,192]{3,2,1,0:T(8,128)(2,1)}, u32[]{:S(2)}) copy-start(bf16[1,24,24,192]{3,2,1,0:T(8,128)(2,1)} %copy-done.6) | copy-start | bytes 663556
  48.9 1.4 copy-start.10
  49.9 1.5 copy-start.12
  49.9 2.2 copy-start.5
  50.4 3.5 copy-start.3
  55.1 13.1 %collective-permute-start.1 = (bf16[8,24,6,192]{3,1,2,0:T(8,128)(2,1)S(1)}, bf16[8,24,6,192]{3,1,2,0:T(8,128)(2,1)S(1)}, u32[]{:S(2)}, u32[]{:S(2)}) collective-permute-start(bf16[8,24,6,192]{3,1,2,0:T(8,128)(2,1)S(1)} %copy.91), channel_id=1, source_target_pairs={{8,0},{16,8},{24,16},{32,24},{40,32},{48,40},{56,48},{64,56},{72,6... | collective-permute-start | bytes 1327112 | tf_op jit(solution)/shard_map/ppermute | solution.py:225
  58.5 19.6 %collective-permute-start.3 = (bf16[8,24,6,192]{3,1,2,0:T(8,128)(2,1)}, bf16[8,24,6,192]{3,1,2,0:T(8,128)(2,1)}, u32[]{:S(2)}, u32[]{:S(2)}) collective-permute-start(bf16[8,24,6,192]{3,1,2,0:T(8,128)(2,1)} %copy.95), channel_id=1, source_target_pairs={{8,0},{16,8},{24,16},{32,24},{40,32},{48,40},{56,48},{64,56},{72,6... | collective-permute-start | bytes 1327112 | tf_op jit(solution)/shard_map/ppermute | solution.py:225
  148.7 0.9 copy-start.11
  148.7 1.2 copy-start.9
  148.7 218.3 %all-reduce.3.cloned.1.call-start = ((), (), s32[]{:S(2)}) async-start(), calls=%async_computation.2 | async-start | bytes 589824 | tf_op jit(solution)/shard_map/psum | solution.py:270
  187.0 242.7 %all-gather.2.cloned.1.call-start = ((), (), s32[]{:S(2)}) async-start(), calls=%async_computation.4 | async-start | bytes 5640192 | tf_op jit(solution)/shard_map/all_gather | solution.py:266
  252.5 10.3 %collective-permute-start.4 = (bf16[8,24,6,192]{3,0,2,1:T(8,128)(2,1)S(1)}, bf16[8,24,6,192]{3,0,2,1:T(8,128)(2,1)S(1)}, u32[]{:S(2)}, u32[]{:S(2)}) collective-permute-start(bf16[8,24,6,192]{3,0,2,1:T(8,128)(2,1)S(1)} %slice.110), channel_id=1, source_target_pairs={{120,0},{0,8},{8,16},{16,24},{24,32},{32,40},{40,48},{48,56},{56,6... | collective-permute-start | bytes 1327112 | tf_op jit(solution)/shard_map/ppermute | solution.py:225
  262.8 6.8 %collective-permute-start.5 = (bf16[8,3,24,192]{3,0,2,1:T(8,128)(2,1)S(1)}, bf16[8,3,24,192]{3,0,2,1:T(8,128)(2,1)S(1)}, u32[]{:S(2)}, u32[]{:S(2)}) collective-permute-start(bf16[8,3,24,192]{3,0,2,1:T(8,128)(2,1)S(1)} %pad_maximum_fusion.9), channel_id=1, source_target_pairs={{0,1},{1,2},{2,3},{3,4},{4,5},{5,6},{6,7},{8,9},{9,10},{10,11},{11... | collective-permute-start | bytes 663560 | tf_op jit(solution)/shard_map/ppermute | solution.py:219
Sparse Core Ops, SparseCore 0:
  148.8 82.3 reduce-scatter.1
  234.3 132.6 all-reduce.2
  369.4 60.2 all-gather.1

commit v2 on v1

v2 whole, which is shorter than its diff:
```python
import functools
import jax
import jax.numpy as jnp
from jax import lax
from jax.experimental import pallas as pl
from jax.experimental.pallas import tpu as pltpu
from jax.sharding import PartitionSpec as P

HEADS = 6
WTOK = 144
HD = 32
C = 192
MAIN = 128
TAIL = WTOK - MAIN
PACK = 896
NT = 16
SCALE = HD ** -0.5
LOG2E = 1.4426950408889634
BF = jnp.bfloat16
F32 = jnp.float32
MESH = pl.DeviceIdType.MESH
LEAD = 6
FIRST_PAIRS = 6
STEPS = 23


def dot(a, b):
    return jnp.dot(a, b, preferred_element_type=F32)


def lane_head(shape):
    return lax.broadcasted_iota(jnp.int32, shape, 1) // HD


def pack_kernel(b_ref, main_ref, tail_ref, sc):
    lane = lax.broadcasted_iota(jnp.int32, (NT, 128), 1)

    def group(g, _):
        base = pl.multiple_of(g * 1152, 128)
        tiles = [b_ref[0, :, pl.ds(base + 128 * j, 128)].astype(F32) for j in range(9)]
        for j in range(8):
            if j == 0:
                main, sec = tiles[0], tiles[1]
            else:
                r = pltpu.roll(tiles[j], 128 - 16 * j, 1)
                sec = pltpu.roll(tiles[j + 1], 128 - 16 * j, 1)
                main = jnp.where(lane < 128 - 16 * j, r, sec)
            row = pl.multiple_of(g * 128 + 16 * j, 16)
            sc[0, pl.ds(row, NT), :] = main
            sc[1, pl.ds(row, NT), :] = sec
        return 0

    lax.fori_loop(0, 18, group, 0, unroll=9)
    for t in range(NT):
        a = sc[0, pl.ds(t, WTOK, stride=NT), :].astype(BF)
        b = sc[1, pl.ds(t, WTOK, stride=NT), :].astype(BF)
        main_ref[t, 0:128, :] = a[:MAIN].T
        main_ref[t, 128:144, :] = b[:MAIN].T[:16]
        tail_ref[t, :, 0:128] = a[MAIN:]
        tail_ref[t, :, 128:144] = b[MAIN:, 0:16]


def pack(bias_view):
    return pl.pallas_call(
        pack_kernel, grid=(6,),
        in_specs=[pl.BlockSpec((1, NT, WTOK * WTOK), lambda h: (h, 0, 0))],
        out_specs=[pl.BlockSpec((NT, WTOK, MAIN), lambda h: (0, 0, h)),
                   pl.BlockSpec((NT, 16, WTOK), lambda h: (0, h, 0))],
        out_shape=[jax.ShapeDtypeStruct((NT, WTOK, 6 * MAIN), BF), jax.ShapeDtypeStruct((NT, 96, WTOK), BF)],
        scratch_shapes=[pltpu.VMEM((2, WTOK * NT, 128), F32)], name="pack",
        cost_estimate=pl.CostEstimate(flops=10**9, bytes_accessed=8 * 2**20, transcendentals=0),
    )(bias_view)


def unpack_kernel(m_ref, t_ref, out_ref, sc, tn):
    h = pl.program_id(0)

    @pl.when(h == 0)
    def _():
        for t in range(NT):
            tn[t] = t_ref[t].reshape(WTOK, 128).T

    for t in range(NT):
        m = m_ref[t].reshape(WTOK, 128)
        sc[0, pl.ds(t, MAIN, stride=NT), :] = m[:MAIN].T.astype(F32)
        sc[1, pl.ds(t, MAIN, stride=NT), 0:16] = m[MAIN:].T.astype(F32)
        tl = tn[t, pl.ds(pl.multiple_of(h * 16, 16), 16), :].astype(F32)
        sc[0, pl.ds(MAIN * NT + t, 16, stride=NT), :] = tl[:, :128]
        sc[1, pl.ds(MAIN * NT + t, 16, stride=NT), 0:16] = tl[:, 128:]
    lane = lax.broadcasted_iota(jnp.int32, (NT, 128), 1)

    def group(g, _):
        base = pl.multiple_of(g * 1152, 128)
        r, s = [], []
        for j in range(8):
            row = pl.multiple_of(g * 128 + 16 * j, 16)
            m = sc[0, pl.ds(row, NT), :]
            t = sc[1, pl.ds(row, NT), :]
            r.append(pltpu.roll(m, 16 * j, 1) if j else m)
            s.append(pltpu.roll(t, 16 * j, 1) if j else t)
        for j in range(9):
            if j == 0:
                v = r[0]
            else:
                low = jnp.where(lane < 16 * (j - 1), r[j - 1], s[j - 1]) if j > 1 else s[0]
                v = jnp.where(lane < 16 * j, low, r[j]) if j < 8 else low
            out_ref[0, :, pl.ds(base + 128 * j, 128)] = v
        return 0

    lax.fori_loop(0, 18, group, 0, unroll=9)


def unpack(f):
    return pl.pallas_call(
        unpack_kernel, grid=(6,),
        in_specs=[pl.BlockSpec((NT, 9, 16, 128), lambda h: (0, h, 0, 0)),
                  pl.BlockSpec((NT, 9, 16, 128), lambda h: (0, 6, 0, 0))],
        out_specs=pl.BlockSpec((1, NT, WTOK * WTOK), lambda h: (h, 0, 0)),
        out_shape=jax.ShapeDtypeStruct((6, NT, WTOK * WTOK), F32),
        scratch_shapes=[pltpu.VMEM((2, WTOK * NT, 128), F32), pltpu.VMEM((NT, 128, WTOK), BF)], name="unpack",
        cost_estimate=pl.CostEstimate(flops=10**9, bytes_accessed=12 * 2**20, transcendentals=0),
    )(f, f)


def add(*parts):
    total = parts[0].astype(F32)
    for part in parts[1:]:
        total = total + part.astype(F32)
    return total.astype(BF)


def window_pair(s, x2, g2, t_of, wq_ref, wqt_ref, wpt_ref, bm_ref, bt_ref, penz_ref, penl_ref, lat_last,
                gq, gp, gsum, gbuf):
    x = x2[...]
    cot = g2[...]
    proj = dot(x, wq_ref[...]).astype(BF)
    dmix = dot(cot, wpt_ref[...]).astype(BF)
    xt = x.T
    dq_l, dk_l, dv_l, mixm, mixt, cott = [], [], [], [], [], []
    for c in range(2):
        t = t_of[c]
        z_on = (t % 4 == 3).astype(F32)
        l_on = jnp.logical_and(lat_last, t // 4 == 3).astype(F32)
        rows = slice(c * WTOK, (c + 1) * WTOK)
        q = proj[rows, 0:192]
        k = proj[rows, 256:448]
        v = proj[rows, 512:704]
        dm = dmix[rows]
        ct = cot[rows]
        qt, kt, vt, dmt = q.T, k.T, v.T, dm.T
        hm = lane_head((MAIN, C))
        ht = lane_head((TAIL, C))
        zq = jnp.zeros((HD, MAIN), BF)

        def blk(at, p):
            top = jnp.concatenate([at[64 * p:64 * p + 32, :MAIN], zq], axis=1)
            bot = jnp.concatenate([zq, at[64 * p + 32:64 * p + 64, :MAIN]], axis=1)
            two = jnp.concatenate([top, bot], axis=0)
            if p == 2:
                return two
            z64 = jnp.zeros((64, 256), BF)
            return jnp.concatenate([two, z64] if p == 0 else [z64, two], axis=0)

        def nat(a, p):
            lanes = slice(0, 128) if p < 2 else slice(128, 192)
            am = a[:MAIN, lanes]
            hh = hm[:, lanes]
            z = jnp.zeros_like(am)
            return jnp.concatenate([jnp.where(hh == 2 * p, am, z), jnp.where(hh == 2 * p + 1, am, z)], axis=0)

        def nat_tail(a):
            am = a[MAIN:]
            z = jnp.zeros_like(am)
            return jnp.concatenate([jnp.where(ht == h, am, z) for h in range(HEADS)], axis=0)

        q_tail, dm_tail = nat_tail(q), nat_tail(dm)
        dn = (((1,), (1,)), ((), ()))
        dk_a = dk_b = dv_a = dv_b = None
        mix_parts, dq_parts = [], []
        for p in range(4):
            if p < 3:
                ln = slice(256 * p, 256 * p + 256)
                sub = slice(0, 128) if p < 2 else slice(128, 192)
                s_ = dot(k[:, sub], blk(qt, p))
                dp = dot(v[:, sub], blk(dmt, p))
                bias = bm_ref[t, :, ln].astype(F32)
            else:
                ln = slice(768, 864)
                s_ = lax.dot_general(k, q_tail, dn, preferred_element_type=F32)
                dp = lax.dot_general(v, dm_tail, dn, preferred_element_type=F32)
                bias = bt_ref[t].T.astype(F32)
            bias = bias * LOG2E + z_on * penz_ref[:, ln].astype(F32) + l_on * penl_ref[:, ln].astype(F32)
            s_ = s_ * (SCALE * LOG2E) + bias
            m = jnp.max(s_, axis=0, keepdims=True)
            e = jnp.exp2(s_ - m)
            r = 1.0 / jnp.sum(e, axis=0, keepdims=True)
            pr = e * r
            pb = pr.astype(BF)
            d = jnp.sum(pr * dp, axis=0, keepdims=True)
            gs = pr * (dp - d)
            gb = gs.astype(BF)
            tot = gsum[t, :, ln] + gs
            gsum[t, :, ln] = tot
            tot = tot.astype(BF)
            if p < 3:
                gbuf[t, 18 * p:18 * p + 9] = tot[:, :128].reshape(9, 16, 128)
                gbuf[t, 18 * p + 9:18 * p + 18] = tot[:, 128:].reshape(9, 16, 128)
            else:
                gbuf[t, 54:63, :, 0:96] = tot.reshape(9, 16, 96)
            if p < 3:
                mo = dot(vt[64 * p:64 * p + 64], pb).astype(BF)
                do = dot(kt[64 * p:64 * p + 64], gb)
                mix_parts += [mo[:32, :MAIN], mo[32:, MAIN:]]
                dq_parts += [do[:32, :MAIN], do[32:, MAIN:]]
                dkp = dot(gb, nat(q, p))
                dvp = dot(pb, nat(dm, p))
                if p < 2:
                    dk_a = dkp if dk_a is None else dk_a + dkp
                    dv_a = dvp if dv_a is None else dv_a + dvp
                else:
                    dk_b, dv_b = dkp, dvp
            else:
                mo = dot(vt, pb).astype(BF)
                do = (dot(kt, gb) * SCALE).astype(BF)
                rh = lax.broadcasted_iota(jnp.int32, (C, 96), 0) // HD
                lh = lax.broadcasted_iota(jnp.int32, (C, 96), 1) // TAIL
                mixt.append(jnp.where(rh == lh, mo, jnp.zeros_like(mo)))
                dot_t = do.T
                dq_tail = jnp.zeros((TAIL, C), BF)
                for h in range(HEADS):
                    dq_tail = jnp.where(ht == h, dot_t[TAIL * h:TAIL * h + TAIL], dq_tail)
                dk_a = dk_a + dot(gb, q_tail[:, :128])
                dk_b = dk_b + dot(gb, q_tail[:, 128:])
                dv_a = dv_a + dot(pb, dm_tail[:, :128])
                dv_b = dv_b + dot(pb, dm_tail[:, 128:])
        mixm.append(jnp.concatenate(mix_parts, axis=0))
        dqt = (jnp.concatenate(dq_parts, axis=0) * SCALE).astype(BF)
        dq_l.append(jnp.concatenate([dqt.T, dq_tail], axis=0))
        dk_l.append((jnp.concatenate([dk_a, dk_b], axis=1) * SCALE).astype(BF))
        dv_l.append(jnp.concatenate([dv_a, dv_b], axis=1).astype(BF))
        cott.append(jnp.concatenate([ct[MAIN:]] * HEADS, axis=0))
    mm = jnp.concatenate(mixm, axis=1)
    cm = jnp.concatenate([cot[0:MAIN], cot[WTOK:WTOK + MAIN]], axis=0)
    gp[...] += dot(mm, cm) + dot(mixt[0], cott[0]) + dot(mixt[1], cott[1])
    dq = jnp.concatenate(dq_l, axis=0)
    dk = jnp.concatenate(dk_l, axis=0)
    dv = jnp.concatenate(dv_l, axis=0)
    gq[0] += dot(xt, dq)
    gq[1] += dot(xt, dk)
    gq[2] += dot(xt, dv)
    return dot(dq, wqt_ref[0]) + dot(dk, wqt_ref[1]) + dot(dv, wqt_ref[2])


def fused_kernel(x_hbm, g_hbm, wq_ref, wqt_ref, wpt_ref, bm_ref, bt_ref, penz_ref, penl_ref, so_ref, se_ref,
                 to_ref, te_ref, out_ref, w_ref, f_hbm,
                 xo, go, xe, ge, x2, g2, fo, fe, fw, fs, gq, gp, gsum, gbuf, rd, hb, xa, xs, xb, ys, yr, fin,
                 wb, wr, wh, wx, wy, wz, wf,
                 load_sem, halo_s, halo_r, ss, rs, ws, wrs, out_sem):
    lon = lax.axis_index("lon")
    lat = lax.axis_index("lat")
    n_lon = 16
    core = lon % 2
    yh = (lon // 2) % 2
    xx = lon // 4
    zz = lat % 4
    yl = lat // 4
    yy = yh * 2 + yl
    partner = lon + 1 - 2 * core
    right = (lon + 4) % n_lon
    left = (lon + 12) % n_lon
    ymate = lon + 2 - 4 * yh
    east = (lon + 1) % n_lon
    west = (lon + 15) % n_lon
    has_south = lat < 7
    has_north = lat > 0
    lat_last = lat == 7

    def peer(lon_, lat_):
        return {"lon": lon_, "lat": lat_}

    def xpeer(d):
        return peer((xx + d) % 4 * 4 + yh * 2 + core, lat)

    def ypeer(d):
        o = (yy + d) % 4
        return peer(xx * 4 + o // 2 * 2 + core, o % 2 * 4 + zz)

    def zpeer(d):
        return peer(lon, yl * 4 + (zz + d) % 4)

    def remote(src, dst, ssem, rsem, dev):
        return pltpu.make_async_remote_copy(src_ref=src, dst_ref=dst, send_sem=ssem, recv_sem=rsem,
                                            device_id=dev, device_id_type=MESH)

    own_loads = [pltpu.make_async_copy(x_hbm, xo.at[:, 0:24], load_sem.at[0]),
                 pltpu.make_async_copy(g_hbm, go.at[:, 0:24], load_sem.at[1])]
    for cp in own_loads:
        cp.start()
    for buf in (xe, ge):
        buf[...] = jnp.zeros_like(buf)
    for buf in (xo, go):
        buf[:, 24:27] = jnp.zeros((8, 3, 24, C), BF)
    for buf in (fw, fs):
        buf[...] = jnp.zeros_like(buf)

    barrier = pltpu.get_barrier_semaphore()
    greet = [peer(partner, lat), xpeer(1), xpeer(2), xpeer(3)] + [ypeer(d) for d in (1, 2, 3)] + [zpeer(d) for d in (1, 2, 3)]
    for dev in greet:
        pl.semaphore_signal(barrier, inc=1, device_id=dev, device_id_type=MESH)
    for dev in (peer(east, lat), peer(west, lat)):
        pl.semaphore_signal(barrier, inc=1, device_id=dev, device_id_type=MESH)

    @pl.when(has_north)
    def _():
        pl.semaphore_signal(barrier, inc=1, device_id=peer(lon, lat - 1), device_id_type=MESH)
        pl.semaphore_signal(barrier, inc=1, device_id=peer(west, lat - 1), device_id_type=MESH)

    @pl.when(has_south)
    def _():
        pl.semaphore_signal(barrier, inc=1, device_id=peer(lon, lat + 1), device_id_type=MESH)
        pl.semaphore_signal(barrier, inc=1, device_id=peer(east, lat + 1), device_id_type=MESH)

    pl.semaphore_wait(barrier, 12 + 2 * has_north.astype(jnp.int32) + 2 * has_south.astype(jnp.int32))

    def halo(which):
        out = []
        for n, (src, ext, own) in enumerate(((x_hbm, xe, xo), (g_hbm, ge, go))):
            if which == "e":
                out.append(remote(src.at[:, :, 0:8], ext.at[:, 0:24], halo_s.at[n], halo_r.at[n], peer(west, lat)))
            if which == "s":
                out.append(remote(src.at[:, 0:3], own.at[:, 24:27], halo_s.at[2 + n], halo_r.at[2 + n],
                                  peer(lon, lat - 1)))
                out.append(remote(src.at[:, 0:3, 0:8], ext.at[:, 24:27], halo_s.at[4 + n], halo_r.at[4 + n],
                                  peer(west, lat - 1)))
        return out

    for cp in halo("e"):
        cp.start()

    @pl.when(has_north)
    def _():
        for cp in halo("s"):
            cp.start()

    gq[...] = jnp.zeros_like(gq)
    gp[...] = jnp.zeros_like(gp)
    fe[...] = jnp.zeros_like(fe)

    def clear(t, _):
        gsum[t] = jnp.zeros((WTOK, PACK), F32)
        gbuf[t, 54:64] = jnp.zeros((10, 16, 128), BF)
        return 0

    lax.fori_loop(0, NT, clear, 0)

    def clear_out(z, _):
        fo[z] = jnp.zeros((27, 24, C), BF)
        return 0

    lax.fori_loop(0, 8, clear_out, 0)
    for cp in own_loads:
        cp.wait()

    mine = core * 32
    other = 32 - mine
    o8 = (xx + 2) % 4 * 8
    r8 = (xx + 1) % 4 * 8
    l8 = (xx + 3) % 4 * 8
    m8 = xx * 8

    def stage_copies(k, t):
        def rc(kind, src, dst, lon_):
            return remote(src, dst, ss.at[kind, t], rs.at[kind, t], peer(lon_, lat))
        if k == 1:
            return [rc(0, gbuf.at[t, pl.ds(other, 32)], rd.at[t], partner)]
        if k == 2:
            return [rc(1, hb.at[t, pl.ds(o8, 4)], xa.at[t, 0:4], right),
                    rc(2, hb.at[t, pl.ds(o8 + 4, 4)], xa.at[t, 4:8], left)]
        if k == 3:
            return [rc(3, xs.at[t, 0:8], xb.at[t, 0:8], right), rc(4, xs.at[t, 8:16], xb.at[t, 8:16], left)]
        if k == 4:
            return [rc(5, ys.at[t], yr.at[t], ymate)]
        if k == 5:
            here = fin.at[t, pl.ds(mine + m8, 8)]
            return [rc(6, here, here, right), rc(7, here, here, left)]
        if k == 6:
            a = fin.at[t, pl.ds(mine + l8, 4)]
            b = fin.at[t, pl.ds(mine + r8 + 4, 4)]
            return [rc(8, a, a, right), rc(9, b, b, left)]
        half = fin.at[t, pl.ds(mine, 32)]
        return [rc(10, half, half, partner)]

    def stage(k, t):
        if k > 1:
            for cp in stage_copies(k - 1, t):
                cp.wait_recv()
        if k == 2:
            hb[t] = add(gbuf[t, pl.ds(mine, 32)], rd[t])
        if k == 3:
            xs[t, 0:4] = add(hb[t, pl.ds(r8, 4)], xa[t, 0:4])
            xs[t, 4:8] = hb[t, pl.ds(r8 + 4, 4)]
            xs[t, 8:12] = hb[t, pl.ds(l8, 4)]
            xs[t, 12:16] = add(hb[t, pl.ds(l8 + 4, 4)], xa[t, 4:8])
        if k == 4:
            ys[t] = add(hb[t, pl.ds(m8, 8)], xb[t, 0:8], xb[t, 8:16])
        if k == 5:
            fin[t, pl.ds(mine + m8, 8)] = add(ys[t], yr[t])
        if k < 8:
            for cp in stage_copies(k, t):
                cp.start()
        else:
            pltpu.make_async_copy(fin.at[t], f_hbm.at[t], out_sem.at[t]).start()

    def run_stage(k, s):
        d = s - (k - 1)

        @pl.when(jnp.logical_and(d >= FIRST_PAIRS, d < 2 * FIRST_PAIRS))
        def _():
            stage(k, 2 * (d - FIRST_PAIRS))
            stage(k, 2 * (d - FIRST_PAIRS) + 1)

        @pl.when(jnp.logical_and(d >= 2 * FIRST_PAIRS, d < NT))
        def _():
            stage(k, d)

    wm = core * 36
    wo = 36 - wm

    def w_copies(k):
        def rc(src, dst, i, j, dev):
            return remote(src, dst, ws.at[i], wrs.at[j], dev)
        if k == 1:
            return [rc(wb.at[pl.ds(wo, 36)], wr, 0, 0, peer(partner, lat))]
        if k == 2:
            return [rc(wh.at[pl.ds((xx + d) % 4 * 9, 9)], wx.at[d - 1], d, d, xpeer(d)) for d in (1, 2, 3)]
        if k == 3:
            return [rc(wy.at[yy], wy.at[yy], 3 + d, 3 + d, ypeer(d)) for d in (1, 2, 3)]
        if k == 4:
            return [rc(wz.at[zz], wz.at[zz], 6 + d, 6 + d, zpeer(d)) for d in (1, 2, 3)]
        if k == 5:
            here = wf.at[pl.ds(wm + xx * 9, 9)]
            return [rc(here, here, 9 + d, 9 + d, xpeer(d)) for d in (1, 2, 3)]
        half = wf.at[pl.ds(wm, 36)]
        return [rc(half, half, 13, 13, peer(partner, lat))]

    def w_stage(k):
        if k > 1:
            for cp in w_copies(k - 1):
                cp.wait_recv()
        if k == 1:
            for i in range(3):
                wb[24 * i:24 * i + 12] = gq[i, :, 0:128].astype(BF).reshape(12, 16, 128)
                wb[24 * i + 12:24 * i + 24, :, 0:64] = gq[i, :, 128:192].astype(BF).reshape(12, 16, 64)
                wb[24 * i + 12:24 * i + 24, :, 64:128] = gp[:, 64 * i:64 * i + 64].astype(BF).reshape(12, 16, 64)
        if k == 2:
            wh[...] = add(wb[pl.ds(wm, 36)], wr[...])
        if k == 3:
            wy[yy] = add(wh[pl.ds(xx * 9, 9)], wx[0], wx[1], wx[2])
        if k == 4:
            wz[zz] = add(wy[0], wy[1], wy[2], wy[3])
        if k == 5:
            wf[pl.ds(wm + xx * 9, 9)] = add(wz[0], wz[1], wz[2], wz[3])
        if k < 7:
            for cp in w_copies(k):
                cp.start()
        else:
            w_ref[...] = wf[...]

    def strips(part):
        if part == 0:
            return [remote(fe.at[:, 3:21], fw.at[:, 3:21], halo_s.at[6], halo_r.at[6], peer(east, lat))]
        if part == 1:
            return [remote(fe.at[:, 21:24], fw.at[:, 21:24], halo_s.at[7], halo_r.at[7], peer(east, lat))]
        return [remote(fe.at[:, 24:27], fw.at[:, 0:3], halo_s.at[8], halo_r.at[8], peer(east, lat + 1)),
                remote(fo.at[:, 24:27], fs, halo_s.at[9], halo_r.at[9], peer(lon, lat + 1))]

    def place(s):
        early = s < FIRST_PAIRS
        late = s >= 2 * FIRST_PAIRS
        base = jnp.where(early, 2 * s, jnp.where(late, s, 2 * (s - FIRST_PAIRS)))
        t_of = (base, jnp.where(late, s, base + 1))
        c_of = (jnp.where(early, 0, jnp.where(late, 0, 1)), jnp.where(early, 0, 1))
        return t_of, c_of

    def gather(s, with_east):
        t_of, c_of = place(s)
        for w in range(2):
            r0 = t_of[w] // 4 * 6 + 3
            for arr, ext, dst in ((xo, xe, x2), (go, ge, g2)):
                halves = []
                for dz in range(2):
                    z = (t_of[w] % 4 * 2 + dz + 1) % 8
                    own = arr[z, pl.ds(r0, 6)].astype(F32).reshape(144, C).astype(BF)
                    part = dot(so_ref[c_of[w]], own)
                    if with_east:
                        ex = ext[z, pl.ds(r0, 6)].astype(F32).reshape(48, C).astype(BF)
                        part = part + dot(se_ref[c_of[w]], ex)
                    halves.append(part)
                dst[w * WTOK:(w + 1) * WTOK] = jnp.concatenate(halves, axis=0).astype(BF)

    def scatter(s, gin):
        t_of, c_of = place(s)
        for w in range(2):
            r0 = t_of[w] // 4 * 6 + 3
            for dz in range(2):
                z = (t_of[w] % 4 * 2 + dz + 1) % 8
                lo = w * WTOK + dz * 72
                part = gin[lo:lo + 72].astype(BF)
                own = dot(to_ref[c_of[w]], part).reshape(6, 24, C)
                fo[z, pl.ds(r0, 6)] = (fo[z, pl.ds(r0, 6)].astype(F32) + own).astype(BF)
                ex = dot(te_ref[c_of[w]], part).reshape(6, 8, C)
                fe[z, pl.ds(r0, 6)] = (fe[z, pl.ds(r0, 6)].astype(F32) + ex).astype(BF)

    def step(s, _):
        @pl.when(s == FIRST_PAIRS)
        def _():
            for cp in halo("e"):
                cp.wait_recv()

        @pl.when(jnp.logical_and(s == 2 * FIRST_PAIRS, has_south))
        def _():
            for cp in halo("s"):
                cp.wait_recv()

        for k in (8, 7, 6, 5, 4, 3, 2):
            run_stage(k, s)
        for k in (7, 6, 5, 4, 3, 2):
            @pl.when(s == NT - 2 + k)
            def _(k=k):
                w_stage(k)

        @pl.when(s == 2 * FIRST_PAIRS)
        def _():
            for cp in strips(0):
                cp.start()

        @pl.when(s == NT)
        def _():
            for cp in strips(1):
                cp.start()

            @pl.when(has_south)
            def _():
                for cp in strips(2):
                    cp.start()

        @pl.when(s < FIRST_PAIRS)
        def _():
            gather(s, False)

        @pl.when(jnp.logical_and(s >= FIRST_PAIRS, s < NT))
        def _():
            gather(s, True)

        @pl.when(s < NT)
        def _():
            t_of, _c = place(s)
            gin = window_pair(s, x2, g2, t_of, wq_ref, wqt_ref, wpt_ref, bm_ref, bt_ref, penz_ref, penl_ref,
                              lat_last, gq, gp, gsum, gbuf)
            scatter(s, gin)

        run_stage(1, s)

        @pl.when(s == NT - 1)
        def _():
            w_stage(1)
        return 0

    lax.fori_loop(0, STEPS, step, 0)

    for cp in strips(0) + strips(1):
        cp.wait_recv()
        cp.wait_send()

    @pl.when(has_north)
    def _():
        for cp in strips(2):
            cp.wait_recv()

    @pl.when(has_south)
    def _():
        for cp in strips(2):
            cp.wait_send()

    def finish(z, _):
        out_ref[z] = fo[z, 0:24]
        out_ref[z, 0:3] = fs[z]
        out_ref[z, :, 0:8] = add(out_ref[z, :, 0:8], fw[z, 0:24])
        return 0

    lax.fori_loop(0, 8, finish, 0)

    for cp in halo("e"):
        cp.wait_send()

    @pl.when(has_north)
    def _():
        for cp in halo("s"):
            cp.wait_send()

    for k in range(1, 7):
        for cp in w_copies(k):
            cp.wait_send()

    def drain(t, _):
        for k in range(1, 8):
            for cp in stage_copies(k, t):
                cp.wait_send()
        pltpu.make_async_copy(fin.at[t], f_hbm.at[t], out_sem.at[t]).wait()
        return 0

    lax.fori_loop(0, NT, drain, 0)


def selectors():
    tok = jnp.arange(72, dtype=jnp.int32)
    i, j = tok // 12, tok % 12
    own = jnp.arange(144, dtype=jnp.int32)
    ext = jnp.arange(48, dtype=jnp.int32)
    so, se = [], []
    for c in range(2):
        col = 6 + 12 * c + j
        so.append((own[None, :] == (i * 24 + col)[:, None]) & (col < 24)[:, None])
        se.append((ext[None, :] == (i * 8 + col - 24)[:, None]) & (col >= 24)[:, None])
    so = jnp.stack(so).astype(BF)
    se = jnp.stack(se).astype(BF)
    return so, se, so.transpose(0, 2, 1), se.transpose(0, 2, 1)


def penalties():
    k = jnp.arange(WTOK, dtype=jnp.int32)
    lane = jnp.arange(PACK, dtype=jnp.int32)
    q = jnp.where(lane < 768, lane % 128, 128 + lane % 16)
    z = (k[:, None] // 72) != (q[None, :] // 72)
    l = ((k[:, None] // 12) % 6 >= 3) != ((q[None, :] // 12) % 6 >= 3)
    return jnp.where(z, -1e30, 0.0).astype(BF), jnp.where(l, -1e30, 0.0).astype(BF)


def fused(normed, cotangent, weight_qkv, weight_proj, bias_main, bias_tail):
    wq = weight_qkv.reshape(C, 3, C)
    wq_pad = jnp.pad(wq, ((0, 0), (0, 0), (0, 64))).reshape(C, 768)
    wqt = wq.transpose(1, 2, 0)
    wpt = weight_proj.T
    penz, penl = penalties()
    so, se, to, te = selectors()
    vm = pl.BlockSpec(memory_space=pltpu.VMEM)
    hbm = pl.BlockSpec(memory_space=pl.ANY)
    V = pltpu.VMEM
    return pl.pallas_call(
        fused_kernel,
        in_specs=[hbm, hbm] + [vm] * 11,
        out_specs=[vm, vm, hbm],
        out_shape=[
            jax.ShapeDtypeStruct(normed.shape, BF),
            jax.ShapeDtypeStruct((72, 16, 128), BF),
            jax.ShapeDtypeStruct((NT, 64, 16, 128), BF),
        ],
        scratch_shapes=[
            V((8, 27, 24, C), BF), V((8, 27, 24, C), BF), V((8, 27, 8, C), BF), V((8, 27, 8, C), BF),
            V((2 * WTOK, C), BF), V((2 * WTOK, C), BF),
            V((8, 27, 24, C), BF), V((8, 27, 8, C), BF), V((8, 27, 8, C), BF), V((8, 3, 24, C), BF),
            V((3, C, C), F32), V((C, C), F32), V((NT, WTOK, PACK), F32),
            V((NT, 64, 16, 128), BF), V((NT, 32, 16, 128), BF), V((NT, 32, 16, 128), BF),
            V((NT, 8, 16, 128), BF), V((NT, 16, 16, 128), BF), V((NT, 16, 16, 128), BF),
            V((NT, 8, 16, 128), BF), V((NT, 8, 16, 128), BF), V((NT, 64, 16, 128), BF),
            V((72, 16, 128), BF), V((36, 16, 128), BF), V((36, 16, 128), BF), V((3, 9, 16, 128), BF),
            V((4, 9, 16, 128), BF), V((4, 9, 16, 128), BF), V((72, 16, 128), BF),
            pltpu.SemaphoreType.DMA((2,)), pltpu.SemaphoreType.DMA((10,)), pltpu.SemaphoreType.DMA((10,)),
            pltpu.SemaphoreType.DMA((11, NT)), pltpu.SemaphoreType.DMA((11, NT)),
            pltpu.SemaphoreType.DMA((14,)), pltpu.SemaphoreType.DMA((14,)), pltpu.SemaphoreType.DMA((NT,)),
        ],
        compiler_params=pltpu.CompilerParams(collective_id=0, has_side_effects=True, vmem_limit_bytes=66_000_000),
        name="fused",
    )(normed, cotangent, wq_pad, wqt, wpt, bias_main, bias_tail, penz, penl, so, se, to, te)


def local(normed, cotangent, weight_qkv, weight_proj, bias_table):
    bias_main, bias_tail = pack(bias_table.transpose(1, 0, 2))
    input_grad, w, f = fused(normed, cotangent, weight_qkv, weight_proj, bias_main, bias_tail)
    bias_grad = unpack(f).transpose(1, 0, 2)
    w = w.reshape(3, 2, 12, 16, 128).transpose(2, 3, 0, 1, 4).reshape(C, 3, 256).astype(F32)
    return input_grad, w[:, :, :C].reshape(C, 3 * C), w[:, :, C:].reshape(C, C), bias_grad


def solution(mesh):
    in_specs = (P(None, "lat", "lon", None), P(None, "lat", "lon", None), P(), P(), P("lat", None, None))
    out_specs = (P(None, "lat", "lon", None), P(), P(), P("lat", None, None))
    return jax.shard_map(local, mesh=mesh, in_specs=in_specs, out_specs=out_specs, check_vma=False)
```

time: 444 us -> 164 us (0.37)
  waiting for transfers between devices: 208 us -> 0 us
  Pallas kernels: 57.9 us -> 150 us
  local copies, waits for them, and re-layouts: 89.6 us -> 10.6 us
  blocking collectives: 35.4 us -> 0 us
  other arithmetic: 21.8 us -> 2.43 us
  starting transfers between devices: 15.4 us -> 0 us
  between operations: 14.2 us -> 0.75 us
    psum x1 -> x0, waiting for transfers between devices: 94.1 us -> none  [local(): w = lax.psum(w.astype(BF), 'lon').astype(F32)]
    pallas_call x1 -> x3, Pallas kernels: 57.9 us -> 150 us  [the longest x1 126 us: fused(): pl.pallas_call(fused_kernel, in_specs=[hbm, hbm] + [vm] * 11, out_specs=[...]
    all_gather x1 -> x0, waiting for transfers between devices: 59.2 us -> none  [local(): gb = lax.all_gather(bias_unpack(gb), 'lon', axis=0, tiled=True)]
    reshape x16 -> x1, local copies, waits for them, and re-layouts: 50.2 us -> 0.87 us  [fused(): wq_pad = jnp.pad(wq, ((0, 0), (0, 0), (0, 64))).reshape(C, 768)]
    reduce_scatter x1 -> x0, waiting for transfers between devices: 44.2 us -> none  [local(): gb = lax.psum_scatter(gb, 'lon', scatter_dimension=0, tiled=True)]
    all_to_all x1 -> x0, blocking collectives: 35.4 us -> none  [of_everyone(): lax.all_to_all(jnp.broadcast_to(x[None], (n, *x.shape)), axis, 0, 0, tile...]
    concatenate x13 -> x0, other arithmetic: 19.5 us -> none  [the longest x4 6.79 us: frame(): tall = jnp.concatenate([a[:, 3:], up], axis=1)]
    ppermute x6 -> x0, starting transfers between devices: 15.1 us -> none  [the longest x3 9.36 us: from_behind(): return lax.ppermute(block, axis, route)]
  transfers between devices with their start and end apart: 9 -> 0, of which waited for: 5 -> 0; matrix products, arithmetic and copies ran while one was open for 20% -> 0% of each run, Pallas kernels for 0% -> 0%
where the time goes in v2:
time: 164 us
  Pallas kernels  150 us (91%)
  local copies, waits for them, and re-layouts  10.6 us (6%)
  other arithmetic  2.43 us (1%)
    pallas_call x1, Pallas kernels, fused(): pl.pallas_call(fused_kernel, in_specs=[hbm, hbm] + [vm] * 11, out_specs=[...  126 us
    pallas_call x1, Pallas kernels, unpack(): pl.pallas_call(unpack_kernel, grid=(6,), in_specs=[pl.BlockSpec((NT, 9, 1...  14.3 us
    pallas_call x1, Pallas kernels, pack(): pl.pallas_call(pack_kernel, grid=(6,), in_specs=[pl.BlockSpec((1, NT, WTO...  10.1 us
    unnamed x9, local copies, waits for them, and re-layouts  5.94 us

profile of v2, /device:TPU:1, one launch (start us, length us, event | category | flops | bytes accessed | tf_op | source)
XLA Modules:
  0.0 163.8 jit_solution(2463113038417852365)
XLA Ops:
  0.9 0.6 fusion.23
  1.5 0.7 copy.18.se_ref
  2.2 1.6 copy.15
  3.9 0.6 fusion.24
  4.5 0.7 copy.17.so_ref
  5.2 1.1 copy.14
  6.3 0.0 copy-start
  6.4 0.9 copy.16.wq_ref
  7.3 1.0 select_convert_fusion
  8.2 10.1 %pack.1 = (bf16[16,144,768]{2,1,0:T(8,128)(2,1)}, bf16[16,96,144]{2,1,0:T(8,128)(2,1)}) custom-call(bf16[6,16,20736]{2,1,0:T(8,128)(2,1)} %bitcast.22), custom_call_target="tpu_custom_call" | custom-call | flops 1000000000 | bytes 8388608 | tf_op jit(solution)/shard_map/pack/pallas_call | solution.py:64
  18.3 0.0 copy-done
  18.3 125.6 %fused.1 = (bf16[8,24,24,192]{3,2,1,0:T(8,128)(2,1)}, bf16[72,16,128]{2,1,0:T(8,128)(2,1)}, bf16[16,64,16,128]{3,2,1,0:T(8,128)(2,1)}) custom-call(bf16[8,24,24,192]{3,2,1,0:T(8,128)(2,1)} %x_hbm.1, bf16[8,24,24,192]{3,2,1,0:T(8,128)(2,1)} %g_hbm.1, bf16[192,768]{1,0:T(8,128)(2,1)} %copy.16.wq_ref, bf16[3,192,192]{2,1,0:T(8,128)(2,1)} %bitcast.25, ...), custom_call_target="tpu_custom_call" | custom-call | tf_op jit(solution)/shard_map/fused/pallas_call | solution.py:649
  143.9 1.3 copy.25
  145.2 0.5 reshape.399
  145.7 0.1 slice.9
  145.8 0.2 copy.21
  146.0 0.8 copy.23
  146.8 0.2 copy.20
  147.0 1.0 copy.22
  148.0 0.0 copy-start.1
  148.0 14.3 %unpack.1 = f32[6,16,20736]{2,1,0:T(8,128)} custom-call(bf16[16,64,16,128]{3,2,1,0:T(8,128)(2,1)} %get-tuple-element.13.m_ref.t_ref, bf16[16,64,16,128]{3,2,1,0:T(8,128)(2,1)} %get-tuple-element.13.m_ref.t_ref), custom_call_target="tpu_custom_call" | custom-call | flops 1000000000 | bytes 12582912 | tf_op jit(solution)/shard_map/unpack/pallas_call | solution.py:114
  162.4 0.0 copy-done.1
  162.4 1.4 copy.27
  (15 shorter events, 0.3 us)
Async XLA Ops:
  6.3 12.0 %copy-start = (bf16[192,576]{0,1:T(8,128)(2,1)}, bf16[192,576]{0,1:T(8,128)(2,1)S(1)}, u32[]{:S(2)}) copy-start(bf16[192,576]{0,1:T(8,128)(2,1)S(1)} %copy.14) | copy-start | bytes 663556
  148.0 14.3 %copy-start.1 = (bf16[8,24,24,192]{3,2,1,0:T(8,128)(2,1)S(1)}, bf16[8,24,24,192]{3,2,1,0:T(8,128)(2,1)}, u32[]{:S(2)}) copy-start(bf16[8,24,24,192]{3,2,1,0:T(8,128)(2,1)} %get-tuple-element.32) | copy-start | bytes 5308420

commit v3 on v2

--- a/solution.py
+++ b/solution.py
@@ -19,9 +19,12 @@
 BF = jnp.bfloat16
 F32 = jnp.float32
 MESH = pl.DeviceIdType.MESH
-LEAD = 6
-FIRST_PAIRS = 6
+FIRST = 5
+EDGE = 9
+PAIRED = 14
 STEPS = 23
+ST = 17
+MASKED = -1e30
 
 
 def dot(a, b):
@@ -45,19 +48,45 @@
                 r = pltpu.roll(tiles[j], 128 - 16 * j, 1)
                 sec = pltpu.roll(tiles[j + 1], 128 - 16 * j, 1)
                 main = jnp.where(lane < 128 - 16 * j, r, sec)
-            row = pl.multiple_of(g * 128 + 16 * j, 16)
+            row = g * (8 * ST) + ST * j
             sc[0, pl.ds(row, NT), :] = main
             sc[1, pl.ds(row, NT), :] = sec
         return 0
 
     lax.fori_loop(0, 18, group, 0, unroll=9)
+    last = (lax.axis_index("lat") == 7).astype(F32)
+
+    def half(n):
+        return jnp.logical_or(jnp.logical_and(n >= 36, n < 72), n >= 108)
+
+    def masks(shape, k_axis, q_first):
+        k = lax.broadcasted_iota(jnp.int32, shape, k_axis)
+        q = lax.broadcasted_iota(jnp.int32, shape, 1 - k_axis)
+        q = q if q_first == 0 else q * 0 + q_first
+        z_no = jnp.logical_xor(k >= 72, q >= 72)
+        l_no = jnp.logical_xor(half(k), half(q))
+        return jnp.where(z_no, MASKED, 0.0), jnp.where(l_no, MASKED, 0.0) * last
+
+    z_main, l_main = masks((WTOK, MAIN), 0, 0)
+    z_tail, l_tail = masks((16, WTOK), 1, 128)
+
+    def masked(x, t, z, l):
+        if t % 4 != 3 and t // 4 != 3:
+            return x
+        y = x.astype(F32)
+        if t % 4 == 3:
+            y = y + z
+        if t // 4 == 3:
+            y = y + l
+        return y.astype(BF)
+
     for t in range(NT):
-        a = sc[0, pl.ds(t, WTOK, stride=NT), :].astype(BF)
-        b = sc[1, pl.ds(t, WTOK, stride=NT), :].astype(BF)
-        main_ref[t, 0:128, :] = a[:MAIN].T
-        main_ref[t, 128:144, :] = b[:MAIN].T[:16]
-        tail_ref[t, :, 0:128] = a[MAIN:]
-        tail_ref[t, :, 128:144] = b[MAIN:, 0:16]
+        a = sc[0, pl.ds(t, WTOK, stride=ST), :].astype(BF)
+        b = sc[1, pl.ds(t, WTOK, stride=ST), :].astype(BF)
+        main_ref[t, 0:128, :] = masked(a[:MAIN].T, t, z_main[:128], l_main[:128])
+        main_ref[t, 128:144, :] = masked(b[:MAIN].T[:16], t, z_main[128:], l_main[128:])
+        tail_ref[t, :, 0:128] = masked(a[MAIN:], t, z_tail[:, :128], l_tail[:, :128])
+        tail_ref[t, :, 128:144] = masked(b[MAIN:, 0:16], t, z_tail[:, 128:], l_tail[:, 128:])
 
 
 def pack(bias_view):
@@ -67,33 +96,38 @@
         out_specs=[pl.BlockSpec((NT, WTOK, MAIN), lambda h: (0, 0, h)),
                    pl.BlockSpec((NT, 16, WTOK), lambda h: (0, h, 0))],
         out_shape=[jax.ShapeDtypeStruct((NT, WTOK, 6 * MAIN), BF), jax.ShapeDtypeStruct((NT, 96, WTOK), BF)],
-        scratch_shapes=[pltpu.VMEM((2, WTOK * NT, 128), F32)], name="pack",
+        scratch_shapes=[pltpu.VMEM((2, WTOK * ST, 128), F32)], name="pack",
         cost_estimate=pl.CostEstimate(flops=10**9, bytes_accessed=8 * 2**20, transcendentals=0),
     )(bias_view)
 
 
-def unpack_kernel(m_ref, t_ref, out_ref, sc, tn):
+def unpack_kernel(m_ref, t_ref, w_ref, out_ref, gq_ref, gp_ref, sc, tn):
     h = pl.program_id(0)
 
     @pl.when(h == 0)
     def _():
         for t in range(NT):
             tn[t] = t_ref[t].reshape(WTOK, 128).T
+        for i in range(3):
+            gq_ref[:, C * i:C * i + 128] = w_ref[24 * i:24 * i + 12].reshape(C, 128).astype(F32)
+            rest = w_ref[24 * i + 12:24 * i + 24].reshape(C, 128).astype(F32)
+            gq_ref[:, C * i + 128:C * i + C] = rest[:, :64]
+            gp_ref[:, 64 * i:64 * i + 64] = rest[:, 64:]
 
     for t in range(NT):
         m = m_ref[t].reshape(WTOK, 128)
-        sc[0, pl.ds(t, MAIN, stride=NT), :] = m[:MAIN].T.astype(F32)
-        sc[1, pl.ds(t, MAIN, stride=NT), 0:16] = m[MAIN:].T.astype(F32)
+        sc[0, pl.ds(t, MAIN, stride=ST), :] = m[:MAIN].T.astype(F32)
+        sc[1, pl.ds(t, MAIN, stride=ST), 0:16] = m[MAIN:].T.astype(F32)
         tl = tn[t, pl.ds(pl.multiple_of(h * 16, 16), 16), :].astype(F32)
-        sc[0, pl.ds(MAIN * NT + t, 16, stride=NT), :] = tl[:, :128]
-        sc[1, pl.ds(MAIN * NT + t, 16, stride=NT), 0:16] = tl[:, 128:]
+        sc[0, pl.ds(MAIN * ST + t, 16, stride=ST), :] = tl[:, :128]
+        sc[1, pl.ds(MAIN * ST + t, 16, stride=ST), 0:16] = tl[:, 128:]
     lane = lax.broadcasted_iota(jnp.int32, (NT, 128), 1)
 
     def group(g, _):
         base = pl.multiple_of(g * 1152, 128)
         r, s = [], []
         for j in range(8):
-            row = pl.multiple_of(g * 128 + 16 * j, 16)
+            row = g * (8 * ST) + ST * j
             m = sc[0, pl.ds(row, NT), :]
             t = sc[1, pl.ds(row, NT), :]
             r.append(pltpu.roll(m, 16 * j, 1) if j else m)
@@ -110,16 +144,19 @@
     lax.fori_loop(0, 18, group, 0, unroll=9)
 
 
-def unpack(f):
+def unpack(f, w):
     return pl.pallas_call(
         unpack_kernel, grid=(6,),
         in_specs=[pl.BlockSpec((NT, 9, 16, 128), lambda h: (0, h, 0, 0)),
-                  pl.BlockSpec((NT, 9, 16, 128), lambda h: (0, 6, 0, 0))],
-        out_specs=pl.BlockSpec((1, NT, WTOK * WTOK), lambda h: (h, 0, 0)),
-        out_shape=jax.ShapeDtypeStruct((6, NT, WTOK * WTOK), F32),
-        scratch_shapes=[pltpu.VMEM((2, WTOK * NT, 128), F32), pltpu.VMEM((NT, 128, WTOK), BF)], name="unpack",
+                  pl.BlockSpec((NT, 9, 16, 128), lambda h: (0, 6, 0, 0)),
+                  pl.BlockSpec((72, 16, 128), lambda h: (0, 0, 0))],
+        out_specs=[pl.BlockSpec((1, NT, WTOK * WTOK), lambda h: (h, 0, 0)),
+                   pl.BlockSpec((C, 3 * C), lambda h: (0, 0)), pl.BlockSpec((C, C), lambda h: (0, 0))],
+        out_shape=[jax.ShapeDtypeStruct((6, NT, WTOK * WTOK), F32), jax.ShapeDtypeStruct((C, 3 * C), F32),
+                   jax.ShapeDtypeStruct((C, C), F32)],
+        scratch_shapes=[pltpu.VMEM((2, WTOK * ST, 128), F32), pltpu.VMEM((NT, 128, WTOK), BF)], name="unpack",
         cost_estimate=pl.CostEstimate(flops=10**9, bytes_accessed=12 * 2**20, transcendentals=0),
-    )(f, f)
+    )(f, f, w)
 
 
 def add(*parts):
@@ -129,7 +166,7 @@
     return total.astype(BF)
 
 
-def window_pair(s, x2, g2, t_of, wq_ref, wqt_ref, wpt_ref, bm_ref, bt_ref, penz_ref, penl_ref, lat_last,
+def window_pair(s, x2, g2, t_of, wq_ref, wqt_ref, wpt_ref, bm_ref, bt_ref,
                 gq, gp, gsum, gbuf):
     x = x2[...]
     cot = g2[...]
@@ -139,8 +176,6 @@
     dq_l, dk_l, dv_l, mixm, mixt, cott = [], [], [], [], [], []
     for c in range(2):
         t = t_of[c]
-        z_on = (t % 4 == 3).astype(F32)
-        l_on = jnp.logical_and(lat_last, t // 4 == 3).astype(F32)
         rows = slice(c * WTOK, (c + 1) * WTOK)
         q = proj[rows, 0:192]
         k = proj[rows, 256:448]
@@ -189,8 +224,7 @@
                 s_ = lax.dot_general(k, q_tail, dn, preferred_element_type=F32)
                 dp = lax.dot_general(v, dm_tail, dn, preferred_element_type=F32)
                 bias = bt_ref[t].T.astype(F32)
-            bias = bias * LOG2E + z_on * penz_ref[:, ln].astype(F32) + l_on * penl_ref[:, ln].astype(F32)
-            s_ = s_ * (SCALE * LOG2E) + bias
+            s_ = s_ * (SCALE * LOG2E) + bias * LOG2E
             m = jnp.max(s_, axis=0, keepdims=True)
             e = jnp.exp2(s_ - m)
             r = 1.0 / jnp.sum(e, axis=0, keepdims=True)
@@ -251,10 +285,9 @@
     return dot(dq, wqt_ref[0]) + dot(dk, wqt_ref[1]) + dot(dv, wqt_ref[2])
 
 
-def fused_kernel(x_hbm, g_hbm, wq_ref, wqt_ref, wpt_ref, bm_ref, bt_ref, penz_ref, penl_ref, so_ref, se_ref,
-                 to_ref, te_ref, out_ref, w_ref, f_hbm,
+def fused_kernel(x_hbm, g_hbm, wqkv_ref, wproj_ref, bm_ref, bt_ref, out_ref, w_ref, f_hbm,
                  xo, go, xe, ge, x2, g2, fo, fe, fw, fs, gq, gp, gsum, gbuf, rd, hb, xa, xs, xb, ys, yr, fin,
-                 wb, wr, wh, wx, wy, wz, wf,
+                 wb, wr, wh, wx, wy, wz, wf, wq_ref, wqt_ref, wpt_ref, so_ref, se_ref, to_ref, te_ref,
                  load_sem, halo_s, halo_r, ss, rs, ws, wrs, out_sem):
     lon = lax.axis_index("lon")
     lat = lax.axis_index("lat")
@@ -273,7 +306,6 @@
     west = (lon + 15) % n_lon
     has_south = lat < 7
     has_north = lat > 0
-    lat_last = lat == 7
 
     def peer(lon_, lat_):
         return {"lon": lon_, "lat": lat_}
@@ -302,6 +334,26 @@
         buf[:, 24:27] = jnp.zeros((8, 3, 24, C), BF)
     for buf in (fw, fs):
         buf[...] = jnp.zeros_like(buf)
+
+    for i in range(3):
+        part = wqkv_ref[:, C * i:C * i + C]
+        wq_ref[:, 256 * i:256 * i + C] = part
+        wq_ref[:, 256 * i + C:256 * i + 256] = jnp.zeros((C, 64), BF)
+        wqt_ref[i] = part.T
+    wpt_ref[...] = wproj_ref[...].T
+    for c in range(2):
+        for ref, width, over, axis in ((so_ref, 24, False, 0), (se_ref, 8, True, 0), (to_ref, 24, False, 1),
+                                       (te_ref, 8, True, 1)):
+            shape = ref.shape[1:]
+            tok = lax.broadcasted_iota(jnp.int32, shape, axis)
+            at = lax.broadcasted_iota(jnp.int32, shape, 1 - axis)
+            row = jnp.zeros(shape, jnp.int32)
+            for m in range(1, 6):
+                row = row + (tok >= 12 * m).astype(jnp.int32)
+            col = tok - 12 * row + 6 + 12 * c
+            hit = at == row * width + col - (24 if over else 0)
+            hit = jnp.logical_and(hit, col >= 24 if over else col < 24)
+            ref[c] = jnp.where(hit, 1.0, 0.0).astype(BF)
 
     barrier = pltpu.get_barrier_semaphore()
     greet = [peer(partner, lat), xpeer(1), xpeer(2), xpeer(3)] + [ypeer(d) for d in (1, 2, 3)] + [zpeer(d) for d in (1, 2, 3)]
@@ -414,14 +466,14 @@
     def run_stage(k, s):
         d = s - (k - 1)
 
-        @pl.when(jnp.logical_and(d >= FIRST_PAIRS, d < 2 * FIRST_PAIRS))
-        def _():
-            stage(k, 2 * (d - FIRST_PAIRS))
-            stage(k, 2 * (d - FIRST_PAIRS) + 1)
-
-        @pl.when(jnp.logical_and(d >= 2 * FIRST_PAIRS, d < NT))
-        def _():
-            stage(k, d)
+        @pl.when(jnp.logical_and(d >= EDGE, d < PAIRED))
+        def _():
+            stage(k, 2 * (d - EDGE))
+            stage(k, 2 * (d - EDGE) + 1)
+
+        @pl.when(jnp.logical_or(jnp.logical_and(d >= FIRST, d < EDGE), jnp.logical_and(d >= PAIRED, d < NT)))
+        def _():
+            stage(k, jnp.where(d < EDGE, d + 12 - FIRST, d - 4))
 
     wm = core * 36
     wo = 36 - wm
@@ -467,20 +519,20 @@
             w_ref[...] = wf[...]
 
     def strips(part):
-        if part == 0:
-            return [remote(fe.at[:, 3:21], fw.at[:, 3:21], halo_s.at[6], halo_r.at[6], peer(east, lat))]
-        if part == 1:
-            return [remote(fe.at[:, 21:24], fw.at[:, 21:24], halo_s.at[7], halo_r.at[7], peer(east, lat))]
-        return [remote(fe.at[:, 24:27], fw.at[:, 0:3], halo_s.at[8], halo_r.at[8], peer(east, lat + 1)),
-                remote(fo.at[:, 24:27], fs, halo_s.at[9], halo_r.at[9], peer(lon, lat + 1))]
+        if part < 4:
+            r = (21, 3, 9, 15)[part]
+            n = 3 if part == 0 else 6
+            return [remote(fe.at[:, r:r + n], fw.at[:, r:r + n], halo_s.at[6 + part], halo_r.at[6 + part], peer(east, lat))]
+        return [remote(fe.at[:, 24:27], fw.at[:, 0:3], halo_s.at[10], halo_r.at[10], peer(east, lat + 1)),
+                remote(fo.at[:, 24:27], fs, halo_s.at[11], halo_r.at[11], peer(lon, lat + 1))]
 
     def place(s):
-        early = s < FIRST_PAIRS
-        late = s >= 2 * FIRST_PAIRS
-        base = jnp.where(early, 2 * s, jnp.where(late, s, 2 * (s - FIRST_PAIRS)))
-        t_of = (base, jnp.where(late, s, base + 1))
-        c_of = (jnp.where(early, 0, jnp.where(late, 0, 1)), jnp.where(early, 0, 1))
-        return t_of, c_of
+        early = s < FIRST
+        paired = jnp.logical_and(s >= EDGE, s < PAIRED)
+        both = jnp.logical_or(early, paired)
+        base = jnp.where(early, 2 * s, jnp.where(paired, 2 * (s - EDGE), jnp.where(s < EDGE, s + 12 - FIRST, s - 4)))
+        late = jnp.where(paired, 1, 0)
+        return (base, base + jnp.where(both, 1, 0)), (late, jnp.where(early, 0, 1))
 
     def gather(s, with_east):
         t_of, c_of = place(s)
@@ -512,12 +564,12 @@
                 fe[z, pl.ds(r0, 6)] = (fe[z, pl.ds(r0, 6)].astype(F32) + ex).astype(BF)
 
     def step(s, _):
-        @pl.when(s == FIRST_PAIRS)
+        @pl.when(s == FIRST)
         def _():
             for cp in halo("e"):
                 cp.wait_recv()
 
-        @pl.when(jnp.logical_and(s == 2 * FIRST_PAIRS, has_south))
+        @pl.when(jnp.logical_and(s == FIRST, has_south))
         def _():
             for cp in halo("s"):
                 cp.wait_recv()
@@ -529,34 +581,30 @@
             def _(k=k):
                 w_stage(k)
 
-        @pl.when(s == 2 * FIRST_PAIRS)
-        def _():
-            for cp in strips(0):
+        for part, when in ((0, EDGE), (1, EDGE + 2), (2, EDGE + 4), (3, NT)):
+            @pl.when(s == when)
+            def _(part=part):
+                for cp in strips(part):
+                    cp.start()
+
+        @pl.when(jnp.logical_and(s == EDGE, has_south))
+        def _():
+            for cp in strips(4):
                 cp.start()
 
-        @pl.when(s == NT)
-        def _():
-            for cp in strips(1):
-                cp.start()
-
-            @pl.when(has_south)
-            def _():
-                for cp in strips(2):
-                    cp.start()
-
-        @pl.when(s < FIRST_PAIRS)
+        @pl.when(s < FIRST)
         def _():
             gather(s, False)
 
-        @pl.when(jnp.logical_and(s >= FIRST_PAIRS, s < NT))
+        @pl.when(jnp.logical_and(s >= FIRST, s < NT))
         def _():
             gather(s, True)
 
         @pl.when(s < NT)
         def _():
             t_of, _c = place(s)
-            gin = window_pair(s, x2, g2, t_of, wq_ref, wqt_ref, wpt_ref, bm_ref, bt_ref, penz_ref, penl_ref,
-                              lat_last, gq, gp, gsum, gbuf)
+            gin = window_pair(s, x2, g2, t_of, wq_ref, wqt_ref, wpt_ref, bm_ref, bt_ref,
+                              gq, gp, gsum, gbuf)
             scatter(s, gin)
 
         run_stage(1, s)
@@ -568,18 +616,19 @@
 
     lax.fori_loop(0, STEPS, step, 0)
 
-    for cp in strips(0) + strips(1):
-        cp.wait_recv()
-        cp.wait_send()
+    for part in range(4):
+        for cp in strips(part):
+            cp.wait_recv()
+            cp.wait_send()
 
     @pl.when(has_north)
     def _():
-        for cp in strips(2):
+        for cp in strips(4):
             cp.wait_recv()
 
     @pl.when(has_south)
     def _():
-        for cp in strips(2):
+        for cp in strips(4):
             cp.wait_send()
 
     def finish(z, _):
@@ -612,43 +661,13 @@
     lax.fori_loop(0, NT, drain, 0)
 
 
-def selectors():
-    tok = jnp.arange(72, dtype=jnp.int32)
-    i, j = tok // 12, tok % 12
-    own = jnp.arange(144, dtype=jnp.int32)
-    ext = jnp.arange(48, dtype=jnp.int32)
-    so, se = [], []
-    for c in range(2):
-        col = 6 + 12 * c + j
-        so.append((own[None, :] == (i * 24 + col)[:, None]) & (col < 24)[:, None])
-        se.append((ext[None, :] == (i * 8 + col - 24)[:, None]) & (col >= 24)[:, None])
-    so = jnp.stack(so).astype(BF)
-    se = jnp.stack(se).astype(BF)
-    return so, se, so.transpose(0, 2, 1), se.transpose(0, 2, 1)
-
-
-def penalties():
-    k = jnp.arange(WTOK, dtype=jnp.int32)
-    lane = jnp.arange(PACK, dtype=jnp.int32)
-    q = jnp.where(lane < 768, lane % 128, 128 + lane % 16)
-    z = (k[:, None] // 72) != (q[None, :] // 72)
-    l = ((k[:, None] // 12) % 6 >= 3) != ((q[None, :] // 12) % 6 >= 3)
-    return jnp.where(z, -1e30, 0.0).astype(BF), jnp.where(l, -1e30, 0.0).astype(BF)
-
-
 def fused(normed, cotangent, weight_qkv, weight_proj, bias_main, bias_tail):
-    wq = weight_qkv.reshape(C, 3, C)
-    wq_pad = jnp.pad(wq, ((0, 0), (0, 0), (0, 64))).reshape(C, 768)
-    wqt = wq.transpose(1, 2, 0)
-    wpt = weight_proj.T
-    penz, penl = penalties()
-    so, se, to, te = selectors()
     vm = pl.BlockSpec(memory_space=pltpu.VMEM)
     hbm = pl.BlockSpec(memory_space=pl.ANY)
     V = pltpu.VMEM
     return pl.pallas_call(
         fused_kernel,
-        in_specs=[hbm, hbm] + [vm] * 11,
+        in_specs=[hbm, hbm] + [vm] * 4,
         out_specs=[vm, vm, hbm],
         out_shape=[
             jax.ShapeDtypeStruct(normed.shape, BF),
@@ -665,21 +684,22 @@
             V((NT, 8, 16, 128), BF), V((NT, 8, 16, 128), BF), V((NT, 64, 16, 128), BF),
             V((72, 16, 128), BF), V((36, 16, 128), BF), V((36, 16, 128), BF), V((3, 9, 16, 128), BF),
             V((4, 9, 16, 128), BF), V((4, 9, 16, 128), BF), V((72, 16, 128), BF),
-            pltpu.SemaphoreType.DMA((2,)), pltpu.SemaphoreType.DMA((10,)), pltpu.SemaphoreType.DMA((10,)),
+            V((C, 768), BF), V((3, C, C), BF), V((C, C), BF),
+            V((2, 72, 144), BF), V((2, 72, 48), BF), V((2, 144, 72), BF), V((2, 48, 72), BF),
+            pltpu.SemaphoreType.DMA((2,)), pltpu.SemaphoreType.DMA((12,)), pltpu.SemaphoreType.DMA((12,)),
             pltpu.SemaphoreType.DMA((11, NT)), pltpu.SemaphoreType.DMA((11, NT)),
             pltpu.SemaphoreType.DMA((14,)), pltpu.SemaphoreType.DMA((14,)), pltpu.SemaphoreType.DMA((NT,)),
         ],
         compiler_params=pltpu.CompilerParams(collective_id=0, has_side_effects=True, vmem_limit_bytes=66_000_000),
         name="fused",
-    )(normed, cotangent, wq_pad, wqt, wpt, bias_main, bias_tail, penz, penl, so, se, to, te)
+    )(normed, cotangent, weight_qkv, weight_proj, bias_main, bias_tail)
 
 
 def local(normed, cotangent, weight_qkv, weight_proj, bias_table):
     bias_main, bias_tail = pack(bias_table.transpose(1, 0, 2))
     input_grad, w, f = fused(normed, cotangent, weight_qkv, weight_proj, bias_main, bias_tail)
-    bias_grad = unpack(f).transpose(1, 0, 2)
-    w = w.reshape(3, 2, 12, 16, 128).transpose(2, 3, 0, 1, 4).reshape(C, 3, 256).astype(F32)
-    return input_grad, w[:, :, :C].reshape(C, 3 * C), w[:, :, C:].reshape(C, C), bias_grad
+    bias_grad, qkv_grad, proj_grad = unpack(f, w)
+    return input_grad, qkv_grad, proj_grad, bias_grad.transpose(1, 0, 2)
 
 
 def solution(mesh):

time: 164 us -> 154 us (0.939)
  local copies, waits for them, and re-layouts: 10.6 us -> 1.41 us
  other arithmetic: 2.43 us -> 0 us
  Pallas kernels: 150 us -> 152 us
    pallas_call x1, Pallas kernels: 126 us -> 134 us  [fused(): pl.pallas_call(fused_kernel, in_specs=[hbm, hbm] + [vm] * 4, out_specs=[v...]
    unnamed x9 -> x3, local copies, waits for them, and re-layouts: 5.94 us -> 1.41 us
    pallas_call x1, Pallas kernels: 14.3 us -> 10.4 us  [unpack(): pl.pallas_call(unpack_kernel, grid=(6,), in_specs=[pl.BlockSpec((NT, 9, 1...]
    convert_element_type x4 -> x0, local copies, waits for them, and re-layouts: 3.17 us -> none  [the longest x2 1.74 us: local(): w.reshape(3, 2, 12, 16, 128).transpose(2, 3, 0, 1, 4).reshape(C, 3, 256)]
    pallas_call x1, Pallas kernels: 10.1 us -> 7.74 us  [pack(): pl.pallas_call(pack_kernel, grid=(6,), in_specs=[pl.BlockSpec((1, NT, WTO...]
where the time goes in v3:
time: 154 us
  Pallas kernels  152 us (99%)
    pallas_call x1, Pallas kernels, fused(): pl.pallas_call(fused_kernel, in_specs=[hbm, hbm] + [vm] * 4, out_specs=[v...  134 us
    pallas_call x1, Pallas kernels, unpack(): pl.pallas_call(unpack_kernel, grid=(6,), in_specs=[pl.BlockSpec((NT, 9, 1...  10.4 us
    pallas_call x1, Pallas kernels, pack(): pl.pallas_call(pack_kernel, grid=(6,), in_specs=[pl.BlockSpec((1, NT, WTO...  7.74 us

profile of v3, /device:TPU:1, one launch (start us, length us, event | category | flops | bytes accessed | tf_op | source)
XLA Modules:
  0.0 154.0 jit_solution(9069387707371812214)
XLA Ops:
  0.6 7.7 %pack.1 = (bf16[16,144,768]{2,1,0:T(8,128)(2,1)}, bf16[16,96,144]{2,1,0:T(8,128)(2,1)}) custom-call(bf16[6,16,20736]{2,1,0:T(8,128)(2,1)} %bitcast.2), custom_call_target="tpu_custom_call" | custom-call | flops 1000000000 | bytes 8388608 | tf_op jit(solution)/shard_map/pack/pallas_call | solution.py:93
  8.4 133.8 %fused.1 = (bf16[8,24,24,192]{3,2,1,0:T(8,128)(2,1)}, bf16[72,16,128]{2,1,0:T(8,128)(2,1)}, bf16[16,64,16,128]{3,2,1,0:T(8,128)(2,1)}) custom-call(bf16[8,24,24,192]{3,2,1,0:T(8,128)(2,1)} %x_hbm.1, bf16[8,24,24,192]{3,2,1,0:T(8,128)(2,1)} %g_hbm.1, bf16[192,576]{1,0:T(8,128)(2,1)} %wqkv_ref.1, bf16[192,192]{1,0:T(8,128)(2,1)} %wproj_ref.1, ...), custom_call_target="tpu_custom_call" | custom-call | tf_op jit(solution)/shard_map/fused/pallas_call | solution.py:668
  142.2 0.0 copy-start
  142.2 10.4 %unpack.1 = (f32[6,16,20736]{2,1,0:T(8,128)}, f32[192,576]{1,0:T(8,128)}, f32[192,192]{1,0:T(8,128)}) custom-call(bf16[16,64,16,128]{3,2,1,0:T(8,128)(2,1)} %get-tuple-element.15.m_ref.t_ref, bf16[16,64,16,128]{3,2,1,0:T(8,128)(2,1)} %get-tuple-element.15.m_ref.t_ref, bf16[72,16,128]{2,1,0:T(8,128)(2,1)} %get-tuple-element.16.w_ref), custom_call_target="tpu_custom_call" | custom-call | flops 1000000000 | bytes 12582912 | tf_op jit(solution)/shard_map/unpack/pallas_call | solution.py:148
  152.6 0.0 copy-done
  152.6 1.4 copy.10
Async XLA Ops:
  142.2 10.4 %copy-start = (bf16[8,24,24,192]{3,2,1,0:T(8,128)(2,1)S(1)}, bf16[8,24,24,192]{3,2,1,0:T(8,128)(2,1)}, u32[]{:S(2)}) copy-start(bf16[8,24,24,192]{3,2,1,0:T(8,128)(2,1)} %get-tuple-element.24) | copy-start | bytes 5308420

commit v4 on v3

--- a/solution.py
+++ b/solution.py
@@ -19,9 +19,8 @@
 BF = jnp.bfloat16
 F32 = jnp.float32
 MESH = pl.DeviceIdType.MESH
-FIRST = 5
-EDGE = 9
-PAIRED = 14
+FIRST = 6
+EDGE = 10
 STEPS = 23
 ST = 17
 MASKED = -1e30
@@ -35,12 +34,12 @@
     return lax.broadcasted_iota(jnp.int32, shape, 1) // HD
 
 
-def pack_kernel(b_ref, main_ref, tail_ref, sc):
+def pack_head(b_ref, main_ref, tail_ref, sc, lanes, rows):
     lane = lax.broadcasted_iota(jnp.int32, (NT, 128), 1)
 
     def group(g, _):
         base = pl.multiple_of(g * 1152, 128)
-        tiles = [b_ref[0, :, pl.ds(base + 128 * j, 128)].astype(F32) for j in range(9)]
+        tiles = [b_ref[:, pl.ds(base + 128 * j, 128)].astype(F32) for j in range(9)]
         for j in range(8):
             if j == 0:
                 main, sec = tiles[0], tiles[1]
@@ -83,22 +82,10 @@
     for t in range(NT):
         a = sc[0, pl.ds(t, WTOK, stride=ST), :].astype(BF)
         b = sc[1, pl.ds(t, WTOK, stride=ST), :].astype(BF)
-        main_ref[t, 0:128, :] = masked(a[:MAIN].T, t, z_main[:128], l_main[:128])
-        main_ref[t, 128:144, :] = masked(b[:MAIN].T[:16], t, z_main[128:], l_main[128:])
-        tail_ref[t, :, 0:128] = masked(a[MAIN:], t, z_tail[:, :128], l_tail[:, :128])
-        tail_ref[t, :, 128:144] = masked(b[MAIN:, 0:16], t, z_tail[:, 128:], l_tail[:, 128:])
-
-
-def pack(bias_view):
-    return pl.pallas_call(
-        pack_kernel, grid=(6,),
-        in_specs=[pl.BlockSpec((1, NT, WTOK * WTOK), lambda h: (h, 0, 0))],
-        out_specs=[pl.BlockSpec((NT, WTOK, MAIN), lambda h: (0, 0, h)),
-                   pl.BlockSpec((NT, 16, WTOK), lambda h: (0, h, 0))],
-        out_shape=[jax.ShapeDtypeStruct((NT, WTOK, 6 * MAIN), BF), jax.ShapeDtypeStruct((NT, 96, WTOK), BF)],
-        scratch_shapes=[pltpu.VMEM((2, WTOK * ST, 128), F32)], name="pack",
-        cost_estimate=pl.CostEstimate(flops=10**9, bytes_accessed=8 * 2**20, transcendentals=0),
-    )(bias_view)
+        main_ref[t, 0:128, lanes] = masked(a[:MAIN].T, t, z_main[:128], l_main[:128])
+        main_ref[t, 128:144, lanes] = masked(b[:MAIN].T[:16], t, z_main[128:], l_main[128:])
+        tail_ref[t, rows, 0:128] = masked(a[MAIN:], t, z_tail[:, :128], l_tail[:, :128])
+        tail_ref[t, rows, 128:144] = masked(b[MAIN:, 0:16], t, z_tail[:, 128:], l_tail[:, 128:])
 
 
 def unpack_kernel(m_ref, t_ref, w_ref, out_ref, gq_ref, gp_ref, sc, tn):
@@ -285,10 +272,11 @@
     return dot(dq, wqt_ref[0]) + dot(dk, wqt_ref[1]) + dot(dv, wqt_ref[2])
 
 
-def fused_kernel(x_hbm, g_hbm, wqkv_ref, wproj_ref, bm_ref, bt_ref, out_ref, w_ref, f_hbm,
+def fused_kernel(x_hbm, g_hbm, wqkv_ref, wproj_ref, bias_hbm, out_ref, w_ref, f_hbm,
                  xo, go, xe, ge, x2, g2, fo, fe, fw, fs, gq, gp, gsum, gbuf, rd, hb, xa, xs, xb, ys, yr, fin,
                  wb, wr, wh, wx, wy, wz, wf, wq_ref, wqt_ref, wpt_ref, so_ref, se_ref, to_ref, te_ref,
-                 load_sem, halo_s, halo_r, ss, rs, ws, wrs, out_sem):
+                 bm_ref, bt_ref, bias_in, psc,
+                 bias_sem, load_sem, halo_s, halo_r, ss, rs, ws, wrs, out_sem):
     lon = lax.axis_index("lon")
     lat = lax.axis_index("lat")
     n_lon = 16
@@ -378,7 +366,7 @@
         out = []
         for n, (src, ext, own) in enumerate(((x_hbm, xe, xo), (g_hbm, ge, go))):
             if which == "e":
-                out.append(remote(src.at[:, :, 0:8], ext.at[:, 0:24], halo_s.at[n], halo_r.at[n], peer(west, lat)))
+                out.append(remote(src.at[:, 3:24, 0:8], ext.at[:, 3:24], halo_s.at[n], halo_r.at[n], peer(west, lat)))
             if which == "s":
                 out.append(remote(src.at[:, 0:3], own.at[:, 24:27], halo_s.at[2 + n], halo_r.at[2 + n],
                                   peer(lon, lat - 1)))
@@ -394,6 +382,10 @@
         for cp in halo("s"):
             cp.start()
 
+    def bias_load(h):
+        return pltpu.make_async_copy(bias_hbm.at[h], bias_in.at[h % 2], bias_sem.at[h % 2])
+
+    bias_load(0).start()
     gq[...] = jnp.zeros_like(gq)
     gp[...] = jnp.zeros_like(gp)
     fe[...] = jnp.zeros_like(fe)
@@ -410,6 +402,16 @@
         return 0
 
     lax.fori_loop(0, 8, clear_out, 0)
+    def pack_one(h, _):
+        @pl.when(h < HEADS - 1)
+        def _():
+            bias_load(h + 1).start()
+        bias_load(h).wait()
+        pack_head(bias_in.at[h % 2], bm_ref, bt_ref, psc, pl.ds(pl.multiple_of(h * MAIN, MAIN), MAIN),
+                  pl.ds(pl.multiple_of(h * TAIL, TAIL), TAIL))
+        return 0
+
+    lax.fori_loop(0, HEADS, pack_one, 0)
     for cp in own_loads:
         cp.wait()
 
@@ -421,31 +423,36 @@
     m8 = xx * 8
 
     def stage_copies(k, t):
-        def rc(kind, src, dst, lon_):
-            return remote(src, dst, ss.at[kind, t], rs.at[kind, t], peer(lon_, lat))
+        def rc(src, dst, lon_):
+            return remote(src, dst, ss.at[k - 1], rs.at[k - 1, t], peer(lon_, lat))
         if k == 1:
-            return [rc(0, gbuf.at[t, pl.ds(other, 32)], rd.at[t], partner)]
+            return [rc(gbuf.at[t, pl.ds(other, 32)], rd.at[t], partner)]
         if k == 2:
-            return [rc(1, hb.at[t, pl.ds(o8, 4)], xa.at[t, 0:4], right),
-                    rc(2, hb.at[t, pl.ds(o8 + 4, 4)], xa.at[t, 4:8], left)]
+            return [rc(hb.at[t, pl.ds(o8, 4)], xa.at[t, 0:4], right),
+                    rc(hb.at[t, pl.ds(o8 + 4, 4)], xa.at[t, 4:8], left)]
         if k == 3:
-            return [rc(3, xs.at[t, 0:8], xb.at[t, 0:8], right), rc(4, xs.at[t, 8:16], xb.at[t, 8:16], left)]
+            return [rc(xs.at[t, 0:8], xb.at[t, 0:8], right), rc(xs.at[t, 8:16], xb.at[t, 8:16], left)]
         if k == 4:
-            return [rc(5, ys.at[t], yr.at[t], ymate)]
+            return [rc(ys.at[t], yr.at[t], ymate)]
         if k == 5:
             here = fin.at[t, pl.ds(mine + m8, 8)]
-            return [rc(6, here, here, right), rc(7, here, here, left)]
+            return [rc(here, here, right), rc(here, here, left)]
         if k == 6:
             a = fin.at[t, pl.ds(mine + l8, 4)]
             b = fin.at[t, pl.ds(mine + r8 + 4, 4)]
-            return [rc(8, a, a, right), rc(9, b, b, left)]
+            return [rc(a, a, right), rc(b, b, left)]
         half = fin.at[t, pl.ds(mine, 32)]
-        return [rc(10, half, half, partner)]
+        return [rc(half, half, partner)]
+
+    volume = (rd, xa, xb, yr, xb, xa, rd)
+
+    def stage_arrived(k, t):
+        ref = volume[k - 1].at[t]
+        remote(ref, ref, ss.at[k - 1], rs.at[k - 1, t], peer(partner, lat)).wait_recv()
 
     def stage(k, t):
         if k > 1:
-            for cp in stage_copies(k - 1, t):
-                cp.wait_recv()
+            stage_arrived(k - 1, t)
         if k == 2:
             hb[t] = add(gbuf[t, pl.ds(mine, 32)], rd[t])
         if k == 3:
@@ -461,44 +468,46 @@
             for cp in stage_copies(k, t):
                 cp.start()
         else:
-            pltpu.make_async_copy(fin.at[t], f_hbm.at[t], out_sem.at[t]).start()
+            pltpu.make_async_copy(fin.at[t], f_hbm.at[t], out_sem).start()
 
     def run_stage(k, s):
         d = s - (k - 1)
 
-        @pl.when(jnp.logical_and(d >= EDGE, d < PAIRED))
+        @pl.when(jnp.logical_and(d >= EDGE, d < NT))
         def _():
             stage(k, 2 * (d - EDGE))
             stage(k, 2 * (d - EDGE) + 1)
 
-        @pl.when(jnp.logical_or(jnp.logical_and(d >= FIRST, d < EDGE), jnp.logical_and(d >= PAIRED, d < NT)))
-        def _():
-            stage(k, jnp.where(d < EDGE, d + 12 - FIRST, d - 4))
+        @pl.when(jnp.logical_and(d >= FIRST, d < EDGE))
+        def _():
+            stage(k, d + 12 - FIRST)
 
     wm = core * 36
     wo = 36 - wm
 
     def w_copies(k):
-        def rc(src, dst, i, j, dev):
-            return remote(src, dst, ws.at[i], wrs.at[j], dev)
+        def rc(src, dst, dev):
+            return remote(src, dst, ws.at[0 if k in (1, 6) else 1], wrs.at[k - 1], dev)
         if k == 1:
-            return [rc(wb.at[pl.ds(wo, 36)], wr, 0, 0, peer(partner, lat))]
+            return [rc(wb.at[pl.ds(wo, 36)], wr, peer(partner, lat))]
         if k == 2:
-            return [rc(wh.at[pl.ds((xx + d) % 4 * 9, 9)], wx.at[d - 1], d, d, xpeer(d)) for d in (1, 2, 3)]
+            return [rc(wh.at[pl.ds((xx + d) % 4 * 9, 9)], wx.at[d - 1], xpeer(d)) for d in (1, 2, 3)]
         if k == 3:
-            return [rc(wy.at[yy], wy.at[yy], 3 + d, 3 + d, ypeer(d)) for d in (1, 2, 3)]
+            return [rc(wy.at[yy], wy.at[yy], ypeer(d)) for d in (1, 2, 3)]
         if k == 4:
-            return [rc(wz.at[zz], wz.at[zz], 6 + d, 6 + d, zpeer(d)) for d in (1, 2, 3)]
+            return [rc(wz.at[zz], wz.at[zz], zpeer(d)) for d in (1, 2, 3)]
         if k == 5:
             here = wf.at[pl.ds(wm + xx * 9, 9)]
-            return [rc(here, here, 9 + d, 9 + d, xpeer(d)) for d in (1, 2, 3)]
+            return [rc(here, here, xpeer(d)) for d in (1, 2, 3)]
         half = wf.at[pl.ds(wm, 36)]
-        return [rc(half, half, 13, 13, peer(partner, lat))]
+        return [rc(half, half, peer(partner, lat))]
+
+    def w_done(k, ref):
+        return remote(ref, ref, ws.at[0 if k in (1, 6) else 1], wrs.at[k - 1], peer(partner, lat))
 
     def w_stage(k):
         if k > 1:
-            for cp in w_copies(k - 1):
-                cp.wait_recv()
+            w_done(k - 1, wr if k in (2, 7) else wx).wait_recv()
         if k == 1:
             for i in range(3):
                 wb[24 * i:24 * i + 12] = gq[i, :, 0:128].astype(BF).reshape(12, 16, 128)
@@ -528,9 +537,9 @@
 
     def place(s):
         early = s < FIRST
-        paired = jnp.logical_and(s >= EDGE, s < PAIRED)
+        paired = s >= EDGE
         both = jnp.logical_or(early, paired)
-        base = jnp.where(early, 2 * s, jnp.where(paired, 2 * (s - EDGE), jnp.where(s < EDGE, s + 12 - FIRST, s - 4)))
+        base = jnp.where(early, 2 * s, jnp.where(paired, 2 * (s - EDGE), s + 12 - FIRST))
         late = jnp.where(paired, 1, 0)
         return (base, base + jnp.where(both, 1, 0)), (late, jnp.where(early, 0, 1))
 
@@ -647,27 +656,22 @@
         for cp in halo("s"):
             cp.wait_send()
 
-    for k in range(1, 7):
-        for cp in w_copies(k):
-            cp.wait_send()
-
-    def drain(t, _):
-        for k in range(1, 8):
-            for cp in stage_copies(k, t):
-                cp.wait_send()
-        pltpu.make_async_copy(fin.at[t], f_hbm.at[t], out_sem.at[t]).wait()
-        return 0
-
-    lax.fori_loop(0, NT, drain, 0)
-
-
-def fused(normed, cotangent, weight_qkv, weight_proj, bias_main, bias_tail):
+    w_done(1, wf).wait_send()
+    for _ in range(4):
+        w_done(2, wx).wait_send()
+    for k in range(1, 8):
+        ref = volume[k - 1]
+        remote(ref, ref, ss.at[k - 1], rs.at[k - 1, 0], peer(partner, lat)).wait_send()
+    pltpu.make_async_copy(fin, f_hbm, out_sem).wait()
+
+
+def fused(normed, cotangent, weight_qkv, weight_proj, bias_view):
     vm = pl.BlockSpec(memory_space=pltpu.VMEM)
     hbm = pl.BlockSpec(memory_space=pl.ANY)
     V = pltpu.VMEM
     return pl.pallas_call(
         fused_kernel,
-        in_specs=[hbm, hbm] + [vm] * 4,
+        in_specs=[hbm, hbm, vm, vm, hbm],
         out_specs=[vm, vm, hbm],
         out_shape=[
             jax.ShapeDtypeStruct(normed.shape, BF),
@@ -686,18 +690,19 @@
             V((4, 9, 16, 128), BF), V((4, 9, 16, 128), BF), V((72, 16, 128), BF),
             V((C, 768), BF), V((3, C, C), BF), V((C, C), BF),
             V((2, 72, 144), BF), V((2, 72, 48), BF), V((2, 144, 72), BF), V((2, 48, 72), BF),
+            V((NT, WTOK, 6 * MAIN), BF), V((NT, 96, WTOK), BF), V((2, NT, WTOK * WTOK), BF),
+            V((2, WTOK * ST, 128), F32), pltpu.SemaphoreType.DMA((2,)),
             pltpu.SemaphoreType.DMA((2,)), pltpu.SemaphoreType.DMA((12,)), pltpu.SemaphoreType.DMA((12,)),
-            pltpu.SemaphoreType.DMA((11, NT)), pltpu.SemaphoreType.DMA((11, NT)),
-            pltpu.SemaphoreType.DMA((14,)), pltpu.SemaphoreType.DMA((14,)), pltpu.SemaphoreType.DMA((NT,)),
+            pltpu.SemaphoreType.DMA((7,)), pltpu.SemaphoreType.DMA((7, NT)),
+            pltpu.SemaphoreType.DMA((2,)), pltpu.SemaphoreType.DMA((6,)), pltpu.SemaphoreType.DMA,
         ],
         compiler_params=pltpu.CompilerParams(collective_id=0, has_side_effects=True, vmem_limit_bytes=66_000_000),
         name="fused",
-    )(normed, cotangent, weight_qkv, weight_proj, bias_main, bias_tail)
+    )(normed, cotangent, weight_qkv, weight_proj, bias_view)
 
 
 def local(normed, cotangent, weight_qkv, weight_proj, bias_table):
-    bias_main, bias_tail = pack(bias_table.transpose(1, 0, 2))
-    input_grad, w, f = fused(normed, cotangent, weight_qkv, weight_proj, bias_main, bias_tail)
+    input_grad, w, f = fused(normed, cotangent, weight_qkv, weight_proj, bias_table.transpose(1, 0, 2))
     bias_grad, qkv_grad, proj_grad = unpack(f, w)
     return input_grad, qkv_grad, proj_grad, bias_grad.transpose(1, 0, 2)
 

time: 154 us -> 136 us (0.88)
  Pallas kernels: 152 us -> 134 us
    pallas_call x2 -> x1, Pallas kernels: 142 us -> 124 us  [fused(): pl.pallas_call(fused_kernel, in_specs=[hbm, hbm, vm, vm, hbm], out_specs=...]
where the time goes in v4:
time: 136 us
  Pallas kernels  134 us (99%)
  local copies, waits for them, and re-layouts  1.41 us (1%)
    pallas_call x1, Pallas kernels, fused(): pl.pallas_call(fused_kernel, in_specs=[hbm, hbm, vm, vm, hbm], out_specs=...  124 us
    pallas_call x1, Pallas kernels, unpack(): pl.pallas_call(unpack_kernel, grid=(6,), in_specs=[pl.BlockSpec((NT, 9, 1...  10.4 us

profile of v4, /device:TPU:1, one launch (start us, length us, event | category | flops | bytes accessed | tf_op | source)
XLA Modules:
  0.0 136.1 jit_solution(16336856320393810778)
XLA Ops:
  0.6 123.6 %fused.1 = (bf16[8,24,24,192]{3,2,1,0:T(8,128)(2,1)}, bf16[72,16,128]{2,1,0:T(8,128)(2,1)}, bf16[16,64,16,128]{3,2,1,0:T(8,128)(2,1)}) custom-call(bf16[8,24,24,192]{3,2,1,0:T(8,128)(2,1)} %x_hbm.1, bf16[8,24,24,192]{3,2,1,0:T(8,128)(2,1)} %g_hbm.1, bf16[192,576]{1,0:T(8,128)(2,1)} %wqkv_ref.1, bf16[192,192]{1,0:T(8,128)(2,1)} %wproj_ref.1, ...), custom_call_target="tpu_custom_call" | custom-call | tf_op jit(solution)/shard_map/fused/pallas_call | solution.py:672
  124.2 0.0 copy-start
  124.2 10.4 %unpack.1 = (f32[6,16,20736]{2,1,0:T(8,128)}, f32[192,576]{1,0:T(8,128)}, f32[192,192]{1,0:T(8,128)}) custom-call(bf16[16,64,16,128]{3,2,1,0:T(8,128)(2,1)} %get-tuple-element.11.m_ref.t_ref, bf16[16,64,16,128]{3,2,1,0:T(8,128)(2,1)} %get-tuple-element.11.m_ref.t_ref, bf16[72,16,128]{2,1,0:T(8,128)(2,1)} %get-tuple-element.12.w_ref), custom_call_target="tpu_custom_call" | custom-call | flops 1000000000 | bytes 12582912 | tf_op jit(solution)/shard_map/unpack/pallas_call | solution.py:135
  134.6 0.0 copy-done
  134.6 1.4 %copy.10 = bf16[8,24,24,192]{3,2,1,0:T(8,128)(2,1)} copy(bf16[8,24,24,192]{3,2,1,0:T(8,128)(2,1)S(1)} %copy-done) | data formatting | bytes 3538944
Async XLA Ops:
  124.2 10.4 %copy-start = (bf16[8,24,24,192]{3,2,1,0:T(8,128)(2,1)S(1)}, bf16[8,24,24,192]{3,2,1,0:T(8,128)(2,1)}, u32[]{:S(2)}) copy-start(bf16[8,24,24,192]{3,2,1,0:T(8,128)(2,1)} %get-tuple-element.20) | copy-start | bytes 5308420

commit v5 on v4

--- a/solution.py
+++ b/solution.py
@@ -153,113 +153,117 @@
     return total.astype(BF)
 
 
-def window_pair(s, x2, g2, t_of, wq_ref, wqt_ref, wpt_ref, bm_ref, bt_ref,
-                gq, gp, gsum, gbuf):
+def blk(at, p):
+    zq = jnp.zeros((HD, MAIN), BF)
+    top = jnp.concatenate([at[64 * p:64 * p + 32, :MAIN], zq], axis=1)
+    bot = jnp.concatenate([zq, at[64 * p + 32:64 * p + 64, :MAIN]], axis=1)
+    two = jnp.concatenate([top, bot], axis=0)
+    if p == 2:
+        return two
+    z64 = jnp.zeros((64, 256), BF)
+    return jnp.concatenate([two, z64] if p == 0 else [z64, two], axis=0)
+
+
+def nat(a, p):
+    lanes = slice(0, 128) if p < 2 else slice(128, 192)
+    am = a[:MAIN, lanes]
+    hh = lane_head((MAIN, C))[:, lanes]
+    z = jnp.zeros_like(am)
+    return jnp.concatenate([jnp.where(hh == 2 * p, am, z), jnp.where(hh == 2 * p + 1, am, z)], axis=0)
+
+
+def nat_tail(a):
+    am = a[MAIN:]
+    ht = lane_head((TAIL, C))
+    z = jnp.zeros_like(am)
+    return jnp.concatenate([jnp.where(ht == h, am, z) for h in range(HEADS)], axis=0)
+
+
+def score_part(x2, g2, pr, dmx, sc, dpc, wq_ref, wpt_ref):
+    proj = dot(x2[...], wq_ref[...]).astype(BF)
+    dmix = dot(g2[...], wpt_ref[...]).astype(BF)
+    pr[...] = proj
+    dmx[...] = dmix
+    dn = (((1,), (1,)), ((), ()))
+    for w in range(2):
+        rows = slice(w * WTOK, (w + 1) * WTOK)
+        q, k, v, dm = proj[rows, 0:192], proj[rows, 256:448], proj[rows, 512:704], dmix[rows]
+        qt, dmt = q.T, dm.T
+        for p in range(3):
+            sub = slice(0, 128) if p < 2 else slice(128, 192)
+            ln = slice(256 * p, 256 * p + 256)
+            sc[w, :, ln] = dot(k[:, sub], blk(qt, p))
+            dpc[w, :, ln] = dot(v[:, sub], blk(dmt, p))
+        sc[w, :, 768:864] = lax.dot_general(k, nat_tail(q), dn, preferred_element_type=F32)
+        dpc[w, :, 768:864] = lax.dot_general(v, nat_tail(dm), dn, preferred_element_type=F32)
+
+
+def softmax_part(t_of, sc, dpc, pbs, gbs, bm_ref, bt_ref, gsum, gbuf):
+    for w in range(2):
+        t = t_of[w]
+        for j in range(7):
+            width = 128 if j < 6 else 96
+            ln = slice(128 * j, 128 * j + width)
+            bias = (bm_ref[t, :, ln] if j < 6 else bt_ref[t].T).astype(F32)
+            z = sc[w, :, ln] * (SCALE * LOG2E) + bias * LOG2E
+            m = jnp.max(z, axis=0, keepdims=True)
+            e = jnp.exp2(z - m)
+            r = 1.0 / jnp.sum(e, axis=0, keepdims=True)
+            prob = e * r
+            pbs[w, :, ln] = prob.astype(BF)
+            dp = dpc[w, :, ln]
+            d = jnp.sum(prob * dp, axis=0, keepdims=True)
+            gs = prob * (dp - d)
+            gbs[w, :, ln] = gs.astype(BF)
+            tot = gsum[t, :, ln] + gs
+            gsum[t, :, ln] = tot
+            gbuf[t, 9 * j:9 * j + 9, :, 0:width] = tot.astype(BF).reshape(9, 16, width)
+
+
+def closing_part(x2, g2, pr, dmx, pbs, gbs, wqt_ref, gq, gp):
     x = x2[...]
     cot = g2[...]
-    proj = dot(x, wq_ref[...]).astype(BF)
-    dmix = dot(cot, wpt_ref[...]).astype(BF)
+    proj = pr[...]
     xt = x.T
+    ht = lane_head((TAIL, C))
     dq_l, dk_l, dv_l, mixm, mixt, cott = [], [], [], [], [], []
-    for c in range(2):
-        t = t_of[c]
-        rows = slice(c * WTOK, (c + 1) * WTOK)
-        q = proj[rows, 0:192]
-        k = proj[rows, 256:448]
-        v = proj[rows, 512:704]
-        dm = dmix[rows]
-        ct = cot[rows]
-        qt, kt, vt, dmt = q.T, k.T, v.T, dm.T
-        hm = lane_head((MAIN, C))
-        ht = lane_head((TAIL, C))
-        zq = jnp.zeros((HD, MAIN), BF)
-
-        def blk(at, p):
-            top = jnp.concatenate([at[64 * p:64 * p + 32, :MAIN], zq], axis=1)
-            bot = jnp.concatenate([zq, at[64 * p + 32:64 * p + 64, :MAIN]], axis=1)
-            two = jnp.concatenate([top, bot], axis=0)
-            if p == 2:
-                return two
-            z64 = jnp.zeros((64, 256), BF)
-            return jnp.concatenate([two, z64] if p == 0 else [z64, two], axis=0)
-
-        def nat(a, p):
-            lanes = slice(0, 128) if p < 2 else slice(128, 192)
-            am = a[:MAIN, lanes]
-            hh = hm[:, lanes]
-            z = jnp.zeros_like(am)
-            return jnp.concatenate([jnp.where(hh == 2 * p, am, z), jnp.where(hh == 2 * p + 1, am, z)], axis=0)
-
-        def nat_tail(a):
-            am = a[MAIN:]
-            z = jnp.zeros_like(am)
-            return jnp.concatenate([jnp.where(ht == h, am, z) for h in range(HEADS)], axis=0)
-
+    for w in range(2):
+        rows = slice(w * WTOK, (w + 1) * WTOK)
+        q, k, v = proj[rows, 0:192], proj[rows, 256:448], proj[rows, 512:704]
+        dm = dmx[rows]
+        kt, vt = k.T, v.T
         q_tail, dm_tail = nat_tail(q), nat_tail(dm)
-        dn = (((1,), (1,)), ((), ()))
-        dk_a = dk_b = dv_a = dv_b = None
-        mix_parts, dq_parts = [], []
-        for p in range(4):
-            if p < 3:
-                ln = slice(256 * p, 256 * p + 256)
-                sub = slice(0, 128) if p < 2 else slice(128, 192)
-                s_ = dot(k[:, sub], blk(qt, p))
-                dp = dot(v[:, sub], blk(dmt, p))
-                bias = bm_ref[t, :, ln].astype(F32)
-            else:
-                ln = slice(768, 864)
-                s_ = lax.dot_general(k, q_tail, dn, preferred_element_type=F32)
-                dp = lax.dot_general(v, dm_tail, dn, preferred_element_type=F32)
-                bias = bt_ref[t].T.astype(F32)
-            s_ = s_ * (SCALE * LOG2E) + bias * LOG2E
-            m = jnp.max(s_, axis=0, keepdims=True)
-            e = jnp.exp2(s_ - m)
-            r = 1.0 / jnp.sum(e, axis=0, keepdims=True)
-            pr = e * r
-            pb = pr.astype(BF)
-            d = jnp.sum(pr * dp, axis=0, keepdims=True)
-            gs = pr * (dp - d)
-            gb = gs.astype(BF)
-            tot = gsum[t, :, ln] + gs
-            gsum[t, :, ln] = tot
-            tot = tot.astype(BF)
-            if p < 3:
-                gbuf[t, 18 * p:18 * p + 9] = tot[:, :128].reshape(9, 16, 128)
-                gbuf[t, 18 * p + 9:18 * p + 18] = tot[:, 128:].reshape(9, 16, 128)
-            else:
-                gbuf[t, 54:63, :, 0:96] = tot.reshape(9, 16, 96)
-            if p < 3:
-                mo = dot(vt[64 * p:64 * p + 64], pb).astype(BF)
-                do = dot(kt[64 * p:64 * p + 64], gb)
-                mix_parts += [mo[:32, :MAIN], mo[32:, MAIN:]]
-                dq_parts += [do[:32, :MAIN], do[32:, MAIN:]]
-                dkp = dot(gb, nat(q, p))
-                dvp = dot(pb, nat(dm, p))
-                if p < 2:
-                    dk_a = dkp if dk_a is None else dk_a + dkp
-                    dv_a = dvp if dv_a is None else dv_a + dvp
-                else:
-                    dk_b, dv_b = dkp, dvp
-            else:
-                mo = dot(vt, pb).astype(BF)
-                do = (dot(kt, gb) * SCALE).astype(BF)
-                rh = lax.broadcasted_iota(jnp.int32, (C, 96), 0) // HD
-                lh = lax.broadcasted_iota(jnp.int32, (C, 96), 1) // TAIL
-                mixt.append(jnp.where(rh == lh, mo, jnp.zeros_like(mo)))
-                dot_t = do.T
-                dq_tail = jnp.zeros((TAIL, C), BF)
-                for h in range(HEADS):
-                    dq_tail = jnp.where(ht == h, dot_t[TAIL * h:TAIL * h + TAIL], dq_tail)
-                dk_a = dk_a + dot(gb, q_tail[:, :128])
-                dk_b = dk_b + dot(gb, q_tail[:, 128:])
-                dv_a = dv_a + dot(pb, dm_tail[:, :128])
-                dv_b = dv_b + dot(pb, dm_tail[:, 128:])
+        mix_parts, dq_parts, dkp, dvp = [], [], [], []
+        for p in range(3):
+            pb = pbs[w, :, 256 * p:256 * p + 256]
+            gb = gbs[w, :, 256 * p:256 * p + 256]
+            mo = dot(vt[64 * p:64 * p + 64], pb).astype(BF)
+            do = dot(kt[64 * p:64 * p + 64], gb)
+            mix_parts += [mo[:32, :MAIN], mo[32:, MAIN:]]
+            dq_parts += [do[:32, :MAIN], do[32:, MAIN:]]
+            dkp.append(dot(gb, nat(q, p)))
+            dvp.append(dot(pb, nat(dm, p)))
+        pb = pbs[w, :, 768:864]
+        gb = gbs[w, :, 768:864]
+        mo = dot(vt, pb).astype(BF)
+        do = (dot(kt, gb) * SCALE).astype(BF)
+        rh = lax.broadcasted_iota(jnp.int32, (C, 96), 0) // HD
+        lh = lax.broadcasted_iota(jnp.int32, (C, 96), 1) // TAIL
+        mixt.append(jnp.where(rh == lh, mo, jnp.zeros_like(mo)))
+        dot_t = do.T
+        dq_tail = jnp.zeros((TAIL, C), BF)
+        for h in range(HEADS):
+            dq_tail = jnp.where(ht == h, dot_t[TAIL * h:TAIL * h + TAIL], dq_tail)
+        dk_a = dkp[0] + dkp[1] + dot(gb, q_tail[:, :128])
+        dk_b = dkp[2] + dot(gb, q_tail[:, 128:])
+        dv_a = dvp[0] + dvp[1] + dot(pb, dm_tail[:, :128])
+        dv_b = dvp[2] + dot(pb, dm_tail[:, 128:])
         mixm.append(jnp.concatenate(mix_parts, axis=0))
         dqt = (jnp.concatenate(dq_parts, axis=0) * SCALE).astype(BF)
         dq_l.append(jnp.concatenate([dqt.T, dq_tail], axis=0))
         dk_l.append((jnp.concatenate([dk_a, dk_b], axis=1) * SCALE).astype(BF))
         dv_l.append(jnp.concatenate([dv_a, dv_b], axis=1).astype(BF))
-        cott.append(jnp.concatenate([ct[MAIN:]] * HEADS, axis=0))
+        cott.append(jnp.concatenate([cot[rows][MAIN:]] * HEADS, axis=0))
     mm = jnp.concatenate(mixm, axis=1)
     cm = jnp.concatenate([cot[0:MAIN], cot[WTOK:WTOK + MAIN]], axis=0)
     gp[...] += dot(mm, cm) + dot(mixt[0], cott[0]) + dot(mixt[1], cott[1])
@@ -273,7 +277,7 @@
 
 
 def fused_kernel(x_hbm, g_hbm, wqkv_ref, wproj_ref, bias_hbm, out_ref, w_ref, f_hbm,
-                 xo, go, xe, ge, x2, g2, fo, fe, fw, fs, gq, gp, gsum, gbuf, rd, hb, xa, xs, xb, ys, yr, fin,
+                 xo, go, xe, ge, x2, g2, pr, dmx, sc, dpc, x2b, g2b, prb, dmxb, scb, dpcb, pbs, gbs, fo, fe, fw, fs, gq, gp, gsum, gbuf, rd, hb, xa, xs, xb, ys, yr, fin,
                  wb, wr, wh, wx, wy, wz, wf, wq_ref, wqt_ref, wpt_ref, so_ref, se_ref, to_ref, te_ref,
                  bm_ref, bt_ref, bias_in, psc,
                  bias_sem, load_sem, halo_s, halo_r, ss, rs, ws, wrs, out_sem):
@@ -366,11 +370,11 @@
         out = []
         for n, (src, ext, own) in enumerate(((x_hbm, xe, xo), (g_hbm, ge, go))):
             if which == "e":
-                out.append(remote(src.at[:, 3:24, 0:8], ext.at[:, 3:24], halo_s.at[n], halo_r.at[n], peer(west, lat)))
+                out.append(remote(src.at[:, 3:24, 0:8], ext.at[0:8, 3:24], halo_s.at[n], halo_r.at[n], peer(west, lat)))
             if which == "s":
                 out.append(remote(src.at[:, 0:3], own.at[:, 24:27], halo_s.at[2 + n], halo_r.at[2 + n],
                                   peer(lon, lat - 1)))
-                out.append(remote(src.at[:, 0:3, 0:8], ext.at[:, 24:27], halo_s.at[4 + n], halo_r.at[4 + n],
+                out.append(remote(src.at[:, 0:3, 0:8], ext.at[0:8, 24:27], halo_s.at[4 + n], halo_r.at[4 + n],
                                   peer(west, lat - 1)))
         return out
 
@@ -543,7 +547,7 @@
         late = jnp.where(paired, 1, 0)
         return (base, base + jnp.where(both, 1, 0)), (late, jnp.where(early, 0, 1))
 
-    def gather(s, with_east):
+    def gather(s, x2, g2):
         t_of, c_of = place(s)
         for w in range(2):
             r0 = t_of[w] // 4 * 6 + 3
@@ -551,12 +555,10 @@
                 halves = []
                 for dz in range(2):
                     z = (t_of[w] % 4 * 2 + dz + 1) % 8
+                    ze = jnp.where(s < FIRST, 8, z)
                     own = arr[z, pl.ds(r0, 6)].astype(F32).reshape(144, C).astype(BF)
-                    part = dot(so_ref[c_of[w]], own)
-                    if with_east:
-                        ex = ext[z, pl.ds(r0, 6)].astype(F32).reshape(48, C).astype(BF)
-                        part = part + dot(se_ref[c_of[w]], ex)
-                    halves.append(part)
+                    ex = ext[ze, pl.ds(r0, 6)].astype(F32).reshape(48, C).astype(BF)
+                    halves.append(dot(so_ref[c_of[w]], own) + dot(se_ref[c_of[w]], ex))
                 dst[w * WTOK:(w + 1) * WTOK] = jnp.concatenate(halves, axis=0).astype(BF)
 
     def scatter(s, gin):
@@ -572,23 +574,21 @@
                 ex = dot(te_ref[c_of[w]], part).reshape(6, 8, C)
                 fe[z, pl.ds(r0, 6)] = (fe[z, pl.ds(r0, 6)].astype(F32) + ex).astype(BF)
 
-    def step(s, _):
-        @pl.when(s == FIRST)
+    sets = ((x2, g2, pr, dmx, sc, dpc), (x2b, g2b, prb, dmxb, scb, dpcb))
+
+    def comm(s):
+        @pl.when(s == FIRST - 1)
         def _():
             for cp in halo("e"):
                 cp.wait_recv()
 
-        @pl.when(jnp.logical_and(s == FIRST, has_south))
+        @pl.when(jnp.logical_and(s == FIRST - 1, has_south))
         def _():
             for cp in halo("s"):
                 cp.wait_recv()
 
         for k in (8, 7, 6, 5, 4, 3, 2):
             run_stage(k, s)
-        for k in (7, 6, 5, 4, 3, 2):
-            @pl.when(s == NT - 2 + k)
-            def _(k=k):
-                w_stage(k)
 
         for part, when in ((0, EDGE), (1, EDGE + 2), (2, EDGE + 4), (3, NT)):
             @pl.when(s == when)
@@ -601,29 +601,43 @@
             for cp in strips(4):
                 cp.start()
 
-        @pl.when(s < FIRST)
-        def _():
-            gather(s, False)
-
-        @pl.when(jnp.logical_and(s >= FIRST, s < NT))
-        def _():
-            gather(s, True)
-
-        @pl.when(s < NT)
-        def _():
-            t_of, _c = place(s)
-            gin = window_pair(s, x2, g2, t_of, wq_ref, wqt_ref, wpt_ref, bm_ref, bt_ref,
-                              gq, gp, gsum, gbuf)
-            scatter(s, gin)
-
-        run_stage(1, s)
-
-        @pl.when(s == NT - 1)
-        def _():
-            w_stage(1)
+    def begin(s, buf):
+        gather(s, buf[0], buf[1])
+        score_part(*buf, wq_ref, wpt_ref)
+
+    def work(s, buf, after):
+        t_of, _c = place(s)
+        softmax_part(t_of, buf[4], buf[5], pbs, gbs, bm_ref, bt_ref, gsum, gbuf)
+        if after is not None:
+            begin(s + 1, after)
+        scatter(s, closing_part(*buf[:4], pbs, gbs, wqt_ref, gq, gp))
+
+    def two_steps(i, last):
+        comm(2 * i)
+        work(2 * i, sets[0], sets[1])
+        run_stage(1, 2 * i)
+        comm(2 * i + 1)
+        work(2 * i + 1, sets[1], None if last else sets[0])
+        run_stage(1, 2 * i + 1)
+
+    def looped(i, _):
+        two_steps(i, False)
         return 0
 
-    lax.fori_loop(0, STEPS, step, 0)
+    begin(0, sets[0])
+    lax.fori_loop(0, NT // 2 - 1, looped, 0)
+    two_steps(NT // 2 - 1, True)
+    w_stage(1)
+
+    def tail(s, _):
+        comm(s)
+        for k in (7, 6, 5, 4, 3, 2):
+            @pl.when(s == NT - 2 + k)
+            def _(k=k):
+                w_stage(k)
+        return 0
+
+    lax.fori_loop(NT, STEPS, tail, 0)
 
     for part in range(4):
         for cp in strips(part):
@@ -679,8 +693,12 @@
             jax.ShapeDtypeStruct((NT, 64, 16, 128), BF),
         ],
         scratch_shapes=[
-            V((8, 27, 24, C), BF), V((8, 27, 24, C), BF), V((8, 27, 8, C), BF), V((8, 27, 8, C), BF),
-            V((2 * WTOK, C), BF), V((2 * WTOK, C), BF),
+            V((8, 27, 24, C), BF), V((8, 27, 24, C), BF), V((9, 27, 8, C), BF), V((9, 27, 8, C), BF),
+            V((2 * WTOK, C), BF), V((2 * WTOK, C), BF), V((2 * WTOK, 768), BF), V((2 * WTOK, C), BF),
+            V((2, WTOK, PACK), F32), V((2, WTOK, PACK), F32),
+            V((2 * WTOK, C), BF), V((2 * WTOK, C), BF), V((2 * WTOK, 768), BF), V((2 * WTOK, C), BF),
+            V((2, WTOK, PACK), F32), V((2, WTOK, PACK), F32),
+            V((2, WTOK, PACK), BF), V((2, WTOK, PACK), BF),
             V((8, 27, 24, C), BF), V((8, 27, 8, C), BF), V((8, 27, 8, C), BF), V((8, 3, 24, C), BF),
             V((3, C, C), F32), V((C, C), F32), V((NT, WTOK, PACK), F32),
             V((NT, 64, 16, 128), BF), V((NT, 32, 16, 128), BF), V((NT, 32, 16, 128), BF),

time: 136 us -> 131 us (0.963)
  Pallas kernels: 134 us -> 129 us
    pallas_call x1, Pallas kernels: 124 us -> 118 us  [fused(): pl.pallas_call(fused_kernel, in_specs=[hbm, hbm, vm, vm, hbm], out_specs=...]
where the time goes in v5:
time: 131 us
  Pallas kernels  129 us (98%)
  local copies, waits for them, and re-layouts  1.41 us (1%)
    pallas_call x1, Pallas kernels, fused(): pl.pallas_call(fused_kernel, in_specs=[hbm, hbm, vm, vm, hbm], out_specs=...  118 us
    pallas_call x1, Pallas kernels, unpack(): pl.pallas_call(unpack_kernel, grid=(6,), in_specs=[pl.BlockSpec((NT, 9, 1...  10.4 us

profile of v5, /device:TPU:1, one launch (start us, length us, event | category | flops | bytes accessed | tf_op | source)
XLA Modules:
  0.0 130.9 jit_solution(18326803750672576070)
XLA Ops:
  0.6 118.4 %fused.1 = (bf16[8,24,24,192]{3,2,1,0:T(8,128)(2,1)}, bf16[72,16,128]{2,1,0:T(8,128)(2,1)}, bf16[16,64,16,128]{3,2,1,0:T(8,128)(2,1)}) custom-call(bf16[8,24,24,192]{3,2,1,0:T(8,128)(2,1)} %x_hbm.1, bf16[8,24,24,192]{3,2,1,0:T(8,128)(2,1)} %g_hbm.1, bf16[192,576]{1,0:T(8,128)(2,1)} %wqkv_ref.1, bf16[192,192]{1,0:T(8,128)(2,1)} %wproj_ref.1, ...), custom_call_target="tpu_custom_call" | custom-call | tf_op jit(solution)/shard_map/fused/pallas_call | solution.py:686
  119.0 0.0 copy-start
  119.0 10.4 %unpack.1 = (f32[6,16,20736]{2,1,0:T(8,128)}, f32[192,576]{1,0:T(8,128)}, f32[192,192]{1,0:T(8,128)}) custom-call(bf16[16,64,16,128]{3,2,1,0:T(8,128)(2,1)} %get-tuple-element.11.m_ref.t_ref, bf16[16,64,16,128]{3,2,1,0:T(8,128)(2,1)} %get-tuple-element.11.m_ref.t_ref, bf16[72,16,128]{2,1,0:T(8,128)(2,1)} %get-tuple-element.12.w_ref), custom_call_target="tpu_custom_call" | custom-call | flops 1000000000 | bytes 12582912 | tf_op jit(solution)/shard_map/unpack/pallas_call | solution.py:135
  129.5 0.0 copy-done
  129.5 1.4 %copy.10 = bf16[8,24,24,192]{3,2,1,0:T(8,128)(2,1)} copy(bf16[8,24,24,192]{3,2,1,0:T(8,128)(2,1)S(1)} %copy-done) | data formatting | bytes 3538944
Async XLA Ops:
  119.0 10.4 %copy-start = (bf16[8,24,24,192]{3,2,1,0:T(8,128)(2,1)S(1)}, bf16[8,24,24,192]{3,2,1,0:T(8,128)(2,1)}, u32[]{:S(2)}) copy-start(bf16[8,24,24,192]{3,2,1,0:T(8,128)(2,1)} %get-tuple-element.20) | copy-start | bytes 5308420

commit v6 on v5

--- a/solution.py
+++ b/solution.py
@@ -19,9 +19,12 @@
 BF = jnp.bfloat16
 F32 = jnp.float32
 MESH = pl.DeviceIdType.MESH
-FIRST = 6
-EDGE = 10
-STEPS = 23
+FIRST = 5
+EDGE = 9
+PAIRED = 14
+STEPS = 28
+OFFSET = (0, 0, 1, 3, 5, 7, 9, 11, 12)
+W_AT = (0, 0, 16, 18, 20, 22, 24, 25)
 ST = 17
 MASKED = -1e30
 
@@ -279,7 +282,7 @@
 def fused_kernel(x_hbm, g_hbm, wqkv_ref, wproj_ref, bias_hbm, out_ref, w_ref, f_hbm,
                  xo, go, xe, ge, x2, g2, pr, dmx, sc, dpc, x2b, g2b, prb, dmxb, scb, dpcb, pbs, gbs, fo, fe, fw, fs, gq, gp, gsum, gbuf, rd, hb, xa, xs, xb, ys, yr, fin,
                  wb, wr, wh, wx, wy, wz, wf, wq_ref, wqt_ref, wpt_ref, so_ref, se_ref, to_ref, te_ref,
-                 bm_ref, bt_ref, bias_in, psc,
+                 bm_ref, bt_ref, bias_in, psc, hs, hx, cs_ref, sse_ref,
                  bias_sem, load_sem, halo_s, halo_r, ss, rs, ws, wrs, out_sem):
     lon = lax.axis_index("lon")
     lat = lax.axis_index("lat")
@@ -333,19 +336,37 @@
         wq_ref[:, 256 * i + C:256 * i + 256] = jnp.zeros((C, 64), BF)
         wqt_ref[i] = part.T
     wpt_ref[...] = wproj_ref[...].T
+    def token(shape, axis):
+        tok = lax.broadcasted_iota(jnp.int32, shape, axis)
+        row = jnp.zeros(shape, jnp.int32)
+        for m in range(1, 6):
+            row = row + (tok >= 12 * m).astype(jnp.int32)
+        return row, tok - 12 * row, lax.broadcasted_iota(jnp.int32, shape, 1 - axis)
+
+    def one_hot(hit):
+        return jnp.where(hit, 1.0, 0.0).astype(BF)
+
     for c in range(2):
-        for ref, width, over, axis in ((so_ref, 24, False, 0), (se_ref, 8, True, 0), (to_ref, 24, False, 1),
-                                       (te_ref, 8, True, 1)):
-            shape = ref.shape[1:]
-            tok = lax.broadcasted_iota(jnp.int32, shape, axis)
-            at = lax.broadcasted_iota(jnp.int32, shape, 1 - axis)
-            row = jnp.zeros(shape, jnp.int32)
-            for m in range(1, 6):
-                row = row + (tok >= 12 * m).astype(jnp.int32)
-            col = tok - 12 * row + 6 + 12 * c
+        for ref, width, over, axis in ((so_ref, 24, False, 0), (to_ref, 24, False, 1), (te_ref, 8, True, 1)):
+            row, col, at = token(ref.shape[1:], axis)
+            col = col + 6 + 12 * c
             hit = at == row * width + col - (24 if over else 0)
-            hit = jnp.logical_and(hit, col >= 24 if over else col < 24)
-            ref[c] = jnp.where(hit, 1.0, 0.0).astype(BF)
+            ref[c] = one_hot(jnp.logical_and(hit, col >= 24 if over else col < 24))
+    for b in range(4):
+        row, col, at = token((72, 128), 0)
+        hit = jnp.logical_and(at == 36 * b + 6 * row + col - 6, col >= 6)
+        se_ref[b] = one_hot(jnp.logical_and(hit, row < 3) if b == 3 else hit)
+    se_ref[4] = jnp.zeros((72, 128), BF)
+    row, col, at = token((72, 24), 0)
+    sse_ref[0] = jnp.zeros((72, 24), BF)
+    sse_ref[1] = one_hot(jnp.logical_and(at == 8 * row - 24 + col - 6, jnp.logical_and(row >= 3, col >= 6)))
+    kept_row = lax.broadcasted_iota(jnp.int32, (128, 168), 0)
+    group = jnp.zeros((128, 168), jnp.int32)
+    for m in range(1, 21):
+        group = group + (kept_row >= 6 * m).astype(jnp.int32)
+    at = lax.broadcasted_iota(jnp.int32, (128, 168), 1)
+    cs_ref[...] = one_hot(jnp.logical_and(at == kept_row + 2 * group, kept_row < 126))
+    hx[:, 4] = jnp.zeros((2, 3, 128, 128), BF)
 
     barrier = pltpu.get_barrier_semaphore()
     greet = [peer(partner, lat), xpeer(1), xpeer(2), xpeer(3)] + [ypeer(d) for d in (1, 2, 3)] + [zpeer(d) for d in (1, 2, 3)]
@@ -370,21 +391,32 @@
         out = []
         for n, (src, ext, own) in enumerate(((x_hbm, xe, xo), (g_hbm, ge, go))):
             if which == "e":
-                out.append(remote(src.at[:, 3:24, 0:8], ext.at[0:8, 3:24], halo_s.at[n], halo_r.at[n], peer(west, lat)))
+                out.append(remote(hs.at[n], hx.at[n, 0:4], halo_s.at[n], halo_r.at[n], peer(west, lat)))
             if which == "s":
                 out.append(remote(src.at[:, 0:3], own.at[:, 24:27], halo_s.at[2 + n], halo_r.at[2 + n],
                                   peer(lon, lat - 1)))
-                out.append(remote(src.at[:, 0:3, 0:8], ext.at[0:8, 24:27], halo_s.at[4 + n], halo_r.at[4 + n],
+                out.append(remote(src.at[:, 0:3, 0:8], ext.at[0:8], halo_s.at[4 + n], halo_r.at[4 + n],
                                   peer(west, lat - 1)))
         return out
-
-    for cp in halo("e"):
-        cp.start()
 
     @pl.when(has_north)
     def _():
         for cp in halo("s"):
             cp.start()
+
+    for cp in own_loads:
+        cp.wait()
+    for n, arr in enumerate((xo, go)):
+        for zp in range(4):
+            kept = []
+            for dz in range(2):
+                edge = arr[2 * zp + dz, 3:24, 0:8].astype(F32).reshape(168, C).astype(BF)
+                kept.append(dot(cs_ref[...], edge).astype(BF))
+            hs[n, zp, 0] = kept[0][:, :128]
+            hs[n, zp, 1] = kept[1][:, :128]
+            hs[n, zp, 2] = jnp.concatenate([kept[0][:, 128:], kept[1][:, 128:]], axis=1)
+    for cp in halo("e"):
+        cp.start()
 
     def bias_load(h):
         return pltpu.make_async_copy(bias_hbm.at[h], bias_in.at[h % 2], bias_sem.at[h % 2])
@@ -416,8 +448,6 @@
         return 0
 
     lax.fori_loop(0, HEADS, pack_one, 0)
-    for cp in own_loads:
-        cp.wait()
 
     mine = core * 32
     other = 32 - mine
@@ -475,16 +505,16 @@
             pltpu.make_async_copy(fin.at[t], f_hbm.at[t], out_sem).start()
 
     def run_stage(k, s):
-        d = s - (k - 1)
-
-        @pl.when(jnp.logical_and(d >= EDGE, d < NT))
+        d = s - OFFSET[k]
+
+        @pl.when(jnp.logical_and(d >= EDGE, d < PAIRED))
         def _():
             stage(k, 2 * (d - EDGE))
             stage(k, 2 * (d - EDGE) + 1)
 
-        @pl.when(jnp.logical_and(d >= FIRST, d < EDGE))
+        @pl.when(jnp.logical_or(jnp.logical_and(d >= FIRST, d < EDGE), jnp.logical_and(d >= PAIRED, d < NT)))
         def _():
-            stage(k, d + 12 - FIRST)
+            stage(k, jnp.where(d < EDGE, d + 12 - FIRST, d - 4))
 
     wm = core * 36
     wo = 36 - wm
@@ -541,24 +571,31 @@
 
     def place(s):
         early = s < FIRST
-        paired = s >= EDGE
+        paired = jnp.logical_and(s >= EDGE, s < PAIRED)
         both = jnp.logical_or(early, paired)
-        base = jnp.where(early, 2 * s, jnp.where(paired, 2 * (s - EDGE), s + 12 - FIRST))
+        base = jnp.where(early, 2 * s, jnp.where(paired, 2 * (s - EDGE), jnp.where(s < EDGE, s + 12 - FIRST, s - 4)))
         late = jnp.where(paired, 1, 0)
         return (base, base + jnp.where(both, 1, 0)), (late, jnp.where(early, 0, 1))
 
     def gather(s, x2, g2):
         t_of, c_of = place(s)
         for w in range(2):
-            r0 = t_of[w] // 4 * 6 + 3
-            for arr, ext, dst in ((xo, xe, x2), (go, ge, g2)):
+            b = t_of[w] // 4
+            r0 = b * 6 + 3
+            pick = jnp.where(c_of[w] == 1, b, 4)
+            corner = jnp.where(jnp.logical_and(c_of[w] == 1, b == 3), 1, 0)
+            for n, (arr, ext, dst) in enumerate(((xo, xe, x2), (go, ge, g2))):
                 halves = []
                 for dz in range(2):
                     z = (t_of[w] % 4 * 2 + dz + 1) % 8
                     ze = jnp.where(s < FIRST, 8, z)
+                    zp = jnp.where(s < FIRST, 4, z // 2)
                     own = arr[z, pl.ds(r0, 6)].astype(F32).reshape(144, C).astype(BF)
-                    ex = ext[ze, pl.ds(r0, 6)].astype(F32).reshape(48, C).astype(BF)
-                    halves.append(dot(so_ref[c_of[w]], own) + dot(se_ref[c_of[w]], ex))
+                    rest = hx[n, zp, 2].astype(F32)
+                    rest = jnp.where(z % 2 == 1, rest[:, 64:], rest[:, :64]).astype(BF)
+                    east_cols = jnp.concatenate([hx[n, zp, z % 2], rest], axis=1)
+                    ex = ext[ze].astype(F32).reshape(24, C).astype(BF)
+                    halves.append(dot(so_ref[c_of[w]], own) + dot(se_ref[pick], east_cols) + dot(sse_ref[corner], ex))
                 dst[w * WTOK:(w + 1) * WTOK] = jnp.concatenate(halves, axis=0).astype(BF)
 
     def scatter(s, gin):
@@ -632,7 +669,7 @@
     def tail(s, _):
         comm(s)
         for k in (7, 6, 5, 4, 3, 2):
-            @pl.when(s == NT - 2 + k)
+            @pl.when(s == W_AT[k])
             def _(k=k):
                 w_stage(k)
         return 0
@@ -693,7 +730,7 @@
             jax.ShapeDtypeStruct((NT, 64, 16, 128), BF),
         ],
         scratch_shapes=[
-            V((8, 27, 24, C), BF), V((8, 27, 24, C), BF), V((9, 27, 8, C), BF), V((9, 27, 8, C), BF),
+            V((8, 27, 24, C), BF), V((8, 27, 24, C), BF), V((9, 3, 8, C), BF), V((9, 3, 8, C), BF),
             V((2 * WTOK, C), BF), V((2 * WTOK, C), BF), V((2 * WTOK, 768), BF), V((2 * WTOK, C), BF),
             V((2, WTOK, PACK), F32), V((2, WTOK, PACK), F32),
             V((2 * WTOK, C), BF), V((2 * WTOK, C), BF), V((2 * WTOK, 768), BF), V((2 * WTOK, C), BF),
@@ -707,9 +744,10 @@
             V((72, 16, 128), BF), V((36, 16, 128), BF), V((36, 16, 128), BF), V((3, 9, 16, 128), BF),
             V((4, 9, 16, 128), BF), V((4, 9, 16, 128), BF), V((72, 16, 128), BF),
             V((C, 768), BF), V((3, C, C), BF), V((C, C), BF),
-            V((2, 72, 144), BF), V((2, 72, 48), BF), V((2, 144, 72), BF), V((2, 48, 72), BF),
+            V((2, 72, 144), BF), V((5, 72, 128), BF), V((2, 144, 72), BF), V((2, 48, 72), BF),
             V((NT, WTOK, 6 * MAIN), BF), V((NT, 96, WTOK), BF), V((2, NT, WTOK * WTOK), BF),
-            V((2, WTOK * ST, 128), F32), pltpu.SemaphoreType.DMA((2,)),
+            V((2, WTOK * ST, 128), F32), V((2, 4, 3, 128, 128), BF), V((2, 5, 3, 128, 128), BF),
+            V((128, 168), BF), V((2, 72, 24), BF), pltpu.SemaphoreType.DMA((2,)),
             pltpu.SemaphoreType.DMA((2,)), pltpu.SemaphoreType.DMA((12,)), pltpu.SemaphoreType.DMA((12,)),
             pltpu.SemaphoreType.DMA((7,)), pltpu.SemaphoreType.DMA((7, NT)),
             pltpu.SemaphoreType.DMA((2,)), pltpu.SemaphoreType.DMA((6,)), pltpu.SemaphoreType.DMA,

time: 131 us -> 127 us (0.969); the launches traced: 131 us -> 125 us
  Pallas kernels: 129 us -> 123 us
    pallas_call x1, Pallas kernels: 118 us -> 112 us  [fused(): pl.pallas_call(fused_kernel, in_specs=[hbm, hbm, vm, vm, hbm], out_specs=...]
where the time goes in v6:
time: 127 us; the launch traced here: 125 us
  Pallas kernels  123 us (97%)
  local copies, waits for them, and re-layouts  1.41 us (1%)
    pallas_call x1, Pallas kernels, fused(): pl.pallas_call(fused_kernel, in_specs=[hbm, hbm, vm, vm, hbm], out_specs=...  112 us
    pallas_call x1, Pallas kernels, unpack(): pl.pallas_call(unpack_kernel, grid=(6,), in_specs=[pl.BlockSpec((NT, 9, 1...  10.4 us

profile of v6, /device:TPU:1, one launch (start us, length us, event | category | flops | bytes accessed | tf_op | source)
XLA Modules:
  0.0 124.8 jit_solution(5001731309290893958)
XLA Ops:
  0.6 112.3 %fused.1 = (bf16[8,24,24,192]{3,2,1,0:T(8,128)(2,1)}, bf16[72,16,128]{2,1,0:T(8,128)(2,1)}, bf16[16,64,16,128]{3,2,1,0:T(8,128)(2,1)}) custom-call(bf16[8,24,24,192]{3,2,1,0:T(8,128)(2,1)} %x_hbm.1, bf16[8,24,24,192]{3,2,1,0:T(8,128)(2,1)} %g_hbm.1, bf16[192,576]{1,0:T(8,128)(2,1)} %wqkv_ref.1, bf16[192,192]{1,0:T(8,128)(2,1)} %wproj_ref.1, ...), custom_call_target="tpu_custom_call" | custom-call | tf_op jit(solution)/shard_map/fused/pallas_call | solution.py:723
  113.0 0.0 copy-start
  113.0 10.4 %unpack.1 = (f32[6,16,20736]{2,1,0:T(8,128)}, f32[192,576]{1,0:T(8,128)}, f32[192,192]{1,0:T(8,128)}) custom-call(bf16[16,64,16,128]{3,2,1,0:T(8,128)(2,1)} %get-tuple-element.11.m_ref.t_ref, bf16[16,64,16,128]{3,2,1,0:T(8,128)(2,1)} %get-tuple-element.11.m_ref.t_ref, bf16[72,16,128]{2,1,0:T(8,128)(2,1)} %get-tuple-element.12.w_ref), custom_call_target="tpu_custom_call" | custom-call | flops 1000000000 | bytes 12582912 | tf_op jit(solution)/shard_map/unpack/pallas_call | solution.py:138
  123.4 0.0 copy-done
  123.4 1.4 %copy.10 = bf16[8,24,24,192]{3,2,1,0:T(8,128)(2,1)} copy(bf16[8,24,24,192]{3,2,1,0:T(8,128)(2,1)S(1)} %copy-done) | data formatting | bytes 3538944
Async XLA Ops:
  113.0 10.4 %copy-start = (bf16[8,24,24,192]{3,2,1,0:T(8,128)(2,1)S(1)}, bf16[8,24,24,192]{3,2,1,0:T(8,128)(2,1)}, u32[]{:S(2)}) copy-start(bf16[8,24,24,192]{3,2,1,0:T(8,128)(2,1)} %get-tuple-element.20) | copy-start | bytes 5308420

commit v7 on v6

--- a/solution.py
+++ b/solution.py
@@ -22,9 +22,9 @@
 FIRST = 5
 EDGE = 9
 PAIRED = 14
-STEPS = 28
-OFFSET = (0, 0, 1, 3, 5, 7, 9, 11, 12)
-W_AT = (0, 0, 16, 18, 20, 22, 24, 25)
+STEPS = 35
+OFFSET = (0, 0, 2, 5, 8, 11, 14, 17, 19)
+W_AT = (0, 0, 17, 20, 23, 26, 29, 31)
 ST = 17
 MASKED = -1e30
 

time: 127 us -> 122 us (0.961)
  the two profiles are of different devices: /device:TPU:1 before, /device:TPU:9 now
where the time goes in v7:
time: 122 us; the launch traced here: 121 us
  Pallas kernels  119 us (98%)
  local copies, waits for them, and re-layouts  1.41 us (1%)
    pallas_call x1, Pallas kernels, fused(): pl.pallas_call(fused_kernel, in_specs=[hbm, hbm, vm, vm, hbm], out_specs=...  109 us
    pallas_call x1, Pallas kernels, unpack(): pl.pallas_call(unpack_kernel, grid=(6,), in_specs=[pl.BlockSpec((NT, 9, 1...  10.4 us

profile of v7, /device:TPU:9, one launch (start us, length us, event | category | flops | bytes accessed | tf_op | source)
XLA Modules:
  0.0 121.2 jit_solution(7699213031415361487)
XLA Ops:
  0.6 108.8 %fused.1 = (bf16[8,24,24,192]{3,2,1,0:T(8,128)(2,1)}, bf16[72,16,128]{2,1,0:T(8,128)(2,1)}, bf16[16,64,16,128]{3,2,1,0:T(8,128)(2,1)}) custom-call(bf16[8,24,24,192]{3,2,1,0:T(8,128)(2,1)} %x_hbm.1, bf16[8,24,24,192]{3,2,1,0:T(8,128)(2,1)} %g_hbm.1, bf16[192,576]{1,0:T(8,128)(2,1)} %wqkv_ref.1, bf16[192,192]{1,0:T(8,128)(2,1)} %wproj_ref.1, ...), custom_call_target="tpu_custom_call" | custom-call | tf_op jit(solution)/shard_map/fused/pallas_call | solution.py:723
  109.4 0.0 copy-start
  109.4 10.4 %unpack.1 = (f32[6,16,20736]{2,1,0:T(8,128)}, f32[192,576]{1,0:T(8,128)}, f32[192,192]{1,0:T(8,128)}) custom-call(bf16[16,64,16,128]{3,2,1,0:T(8,128)(2,1)} %get-tuple-element.11.m_ref.t_ref, bf16[16,64,16,128]{3,2,1,0:T(8,128)(2,1)} %get-tuple-element.11.m_ref.t_ref, bf16[72,16,128]{2,1,0:T(8,128)(2,1)} %get-tuple-element.12.w_ref), custom_call_target="tpu_custom_call" | custom-call | flops 1000000000 | bytes 12582912 | tf_op jit(solution)/shard_map/unpack/pallas_call | solution.py:138
  119.8 0.0 copy-done
  119.8 1.4 %copy.10 = bf16[8,24,24,192]{3,2,1,0:T(8,128)(2,1)} copy(bf16[8,24,24,192]{3,2,1,0:T(8,128)(2,1)S(1)} %copy-done) | data formatting | bytes 3538944
Async XLA Ops:
  109.4 10.4 %copy-start = (bf16[8,24,24,192]{3,2,1,0:T(8,128)(2,1)S(1)}, bf16[8,24,24,192]{3,2,1,0:T(8,128)(2,1)}, u32[]{:S(2)}) copy-start(bf16[8,24,24,192]{3,2,1,0:T(8,128)(2,1)} %get-tuple-element.20) | copy-start | bytes 5308420
